TPU v7x, 32 devices: a 4x4x1 block of a 4x4x8 slice. The times are simulated.
32 devices in a mesh: rep: 1 (over z), kv2: 4 (over y), kv: 8 (over x, core).
Axes of the slice: x: 4, y: 4, z: 1, core: 2. Of those that a mesh axis runs over, the one named last changes fastest.
The devices are a block of a 4x4x8 slice.
Arguments:
- x_embed: bfloat16 [2, 1024, 2048], P(None, ('rep', 'kv2', 'kv'))
- w_query: bfloat16 [2, 2048, 2048], replicated
- w_key: bfloat16 [2, 2048, 512], replicated
- w_value: bfloat16 [2, 2048, 512], replicated
- w_out: bfloat16 [2, 2048, 2048], replicated
- w_up: bfloat16 [2, 2048, 8192], replicated
- w_down: bfloat16 [2, 8192, 2048], replicated
- k_pool: bfloat16 [6656, 2, 16, 8, 64], P(('rep', 'kv2', 'kv'))
- v_pool: bfloat16 [6656, 2, 16, 8, 64], P(('rep', 'kv2', 'kv'))
- old_table: int32 [1024, 3], P(('rep', 'kv2', 'kv'))
- seq_len: int32 [1024], P(('rep', 'kv2', 'kv'))
- src_slot: int32 [512], P(('rep', 'kv2', 'kv'))
- dst_slot: int32 [512], P(('rep', 'kv2', 'kv'))
Outputs:
- output 1: bfloat16 [2, 1024, 2048], P(None, ('rep', 'kv2', 'kv'))
- output 2: bfloat16 [6656, 2, 16, 8, 64], P(('rep', 'kv2', 'kv'))
- output 3: bfloat16 [6656, 2, 16, 8, 64], P(('rep', 'kv2', 'kv'))
All inputs are finite; a program needn't handle non-finite values.
Results may differ from a plain program's by a relative error of at most 0.0135625.
Values are sent between devices in bfloat16 or wider.
A program may use at most 768 MiB of HBM per device.

v0:
```python
import jax
import jax.numpy as jnp
from jax import lax
from jax.sharding import PartitionSpec as P


def solution(mesh):
    n_rows = mesh.shape['kv2']
    n_cols = mesh.shape['kv']
    dev_axes = ('rep', 'kv2', 'kv')
    seq_spec = P(None, dev_axes, None)
    pool_spec = P(dev_axes, None, None, None, None)
    table_spec = P(dev_axes, None)
    vec_spec = P(dev_axes)
    full_spec = P()

    def per_device(x_embed, w_query, w_key, w_value, w_out, w_up, w_down, k_pool, v_pool, old_table, seq_len, src_slot, dst_slot):
        n_slots, layers, page, kv_heads, head_dim = k_pool.shape
        heads = w_query.shape[2] // head_dim
        q_group = heads // kv_heads
        seq_dev = x_embed.shape[1]
        n_pages = old_table.shape[1]
        row_seqs = seq_dev * n_cols
        slot_base = (lax.axis_index('kv2') * n_cols + lax.axis_index('kv')) * n_slots
        src_all = lax.all_gather(src_slot, ('kv2', 'kv'), tiled=True)
        dst_all = lax.all_gather(dst_slot, ('kv2', 'kv'), tiled=True)
        src_local = src_slot - slot_base
        out_pages = jnp.stack([k_pool[src_local], v_pool[src_local]], axis=1)
        in_pages = lax.all_gather(out_pages, ('kv2', 'kv'), tiled=True)
        dst_local = dst_all - slot_base
        dst_local = jnp.where((dst_local >= 0) & (dst_local < n_slots), dst_local, n_slots)
        k_pool = k_pool.at[dst_local].set(in_pages[:, 0], mode='drop')
        v_pool = v_pool.at[dst_local].set(in_pages[:, 1], mode='drop')
        row_table = lax.all_gather(old_table, 'kv', tiled=True)
        row_len = lax.all_gather(seq_len, 'kv', tiled=True)
        slot_move = jnp.full((n_rows * n_cols * n_slots,), -1, jnp.int32).at[src_all].set(jnp.arange(src_all.shape[0], dtype=jnp.int32))
        move_idx = slot_move[jnp.maximum(row_table, 0)]
        new_table = jnp.where((row_table >= 0) & (move_idx >= 0), dst_all[jnp.maximum(move_idx, 0)], row_table)
        table_local = new_table - slot_base
        owned = (new_table >= 0) & (table_local >= 0) & (table_local < n_slots)
        cell_ids = jnp.arange(row_seqs * n_pages, dtype=jnp.int32).reshape(row_seqs, n_pages)
        slot_cell = jnp.full((n_slots,), -1, jnp.int32).at[jnp.where(owned, table_local, n_slots)].set(cell_ids, mode='drop')
        slot_used = slot_cell >= 0
        seq_of_slot = jnp.where(slot_used, slot_cell // n_pages, 0)
        seg_ids = jnp.where(slot_used, seq_of_slot, row_seqs)
        slot_first = jnp.where(slot_used, slot_cell % n_pages, 0) * page
        tok_off = jnp.arange(page)
        row_ids = jnp.arange(row_seqs)
        q_scale = head_dim ** -0.5
        step_outs = []
        for step_idx in range(2):
            cur_pos = row_len + step_idx
            w_slot = new_table[row_ids, cur_pos // page] - slot_base
            w_slot = jnp.where((w_slot >= 0) & (w_slot < n_slots), w_slot, n_slots)
            w_off = cur_pos % page
            visible = slot_used[:, None] & (tok_off[None, :] <= (cur_pos[seq_of_slot] - slot_first)[:, None])
            hidden = x_embed[step_idx]
            for layer_idx in range(layers):
                query = jnp.dot(hidden, w_query[layer_idx], preferred_element_type=jnp.float32).astype(jnp.bfloat16)
                k_new = jnp.dot(hidden, w_key[layer_idx], preferred_element_type=jnp.float32).astype(jnp.bfloat16)
                v_new = jnp.dot(hidden, w_value[layer_idx], preferred_element_type=jnp.float32).astype(jnp.bfloat16)
                q_row = lax.all_gather(query, 'kv', tiled=True)
                kv_row = lax.all_gather(jnp.stack([k_new, v_new]), 'kv', axis=1, tiled=True).reshape(2, row_seqs, kv_heads, head_dim)
                k_pool = k_pool.at[w_slot, layer_idx, w_off].set(kv_row[0], mode='drop')
                v_pool = v_pool.at[w_slot, layer_idx, w_off].set(kv_row[1], mode='drop')
                q_slot = q_row[seq_of_slot].reshape(n_slots, kv_heads, q_group, head_dim)
                scores = jnp.einsum('sgrd,spgd->sgrp', q_slot, k_pool[:, layer_idx], preferred_element_type=jnp.float32) * q_scale
                scores = jnp.where(visible[:, None, None, :], scores, -1e30)
                slot_max = scores.max(axis=-1)
                expo = jnp.exp(scores - slot_max[..., None])
                slot_out = jnp.einsum('sgrp,spgd->sgrd', expo.astype(jnp.bfloat16), v_pool[:, layer_idx], preferred_element_type=jnp.float32)
                seq_max = jnp.full((row_seqs, kv_heads, q_group), -1e30, jnp.float32).at[seg_ids].max(slot_max, mode='drop')
                slot_w = jnp.exp(jnp.where(slot_used[:, None, None], slot_max - seq_max[seq_of_slot], -1e30))
                seq_sum = jax.ops.segment_sum(slot_w * expo.sum(axis=-1), seg_ids, num_segments=row_seqs)
                seq_out = jax.ops.segment_sum(slot_w[..., None] * slot_out, seg_ids, num_segments=row_seqs)
                partial_res = jnp.concatenate([seq_max[..., None], seq_sum[..., None], seq_out], axis=-1)
                home = lax.all_to_all(partial_res, 'kv', 0, 0, tiled=True).reshape(n_cols, seq_dev, kv_heads, q_group, head_dim + 2)
                scale_w = jnp.exp(home[..., 0] - home[..., 0].max(axis=0))
                total = (scale_w * home[..., 1]).sum(axis=0)
                attn_out = ((scale_w[..., None] * home[..., 2:]).sum(axis=0) / total[..., None]).astype(jnp.bfloat16).reshape(seq_dev, heads * head_dim)
                hidden = (hidden.astype(jnp.float32) + jnp.dot(attn_out, w_out[layer_idx], preferred_element_type=jnp.float32)).astype(jnp.bfloat16)
                up_act = jax.nn.gelu(jnp.dot(hidden, w_up[layer_idx], preferred_element_type=jnp.float32)).astype(jnp.bfloat16)
                hidden = (hidden.astype(jnp.float32) + jnp.dot(up_act, w_down[layer_idx], preferred_element_type=jnp.float32)).astype(jnp.bfloat16)
            step_outs.append(hidden)
        return jnp.stack(step_outs), k_pool, v_pool

    return jax.shard_map(per_device, mesh=mesh, in_specs=(seq_spec, full_spec, full_spec, full_spec, full_spec, full_spec, full_spec, pool_spec, pool_spec, table_spec, vec_spec, vec_spec, vec_spec), out_specs=(seq_spec, pool_spec, pool_spec), check_vma=False)
```

profile of v0, /device:TPU:97, one launch (start us, length us, event | category | flops | bytes accessed | tf_op | source)
XLA Modules:
  0.0 1676.2 jit_solution(14861639740243592280)
XLA Ops:
  13.1 17.7 %copy.403 = bf16[208,2,16,8,64]{4,2,3,1,0:T(8,128)(2,1)} copy(bf16[208,2,16,8,64]{0,4,3,2,1:T(8,128)(2,1)} %param.20) | data formatting | bytes 13631488 | tf_op args[7]
  30.8 17.7 %copy.404 = bf16[208,2,16,8,64]{4,2,3,1,0:T(8,128)(2,1)} copy(bf16[208,2,16,8,64]{0,4,3,2,1:T(8,128)(2,1)} %param.21) | data formatting | bytes 13631488 | tf_op args[8]
  61.7 17.7 %copy.405 = bf16[208,2,16,8,64]{4,3,2,1,0:T(8,128)(2,1)} copy(bf16[208,2,16,8,64]{0,4,3,2,1:T(8,128)(2,1)} %param.20) | data formatting | bytes 13631488 | tf_op args[7]
  79.3 17.7 %copy.417 = bf16[208,2,16,8,64]{4,3,2,1,0:T(8,128)(2,1)} copy(bf16[208,2,16,8,64]{0,4,3,2,1:T(8,128)(2,1)} %param.21) | data formatting | bytes 13631488 | tf_op args[8]
  97.0 20.5 %all-gather = s32[8,32,3]{1,2,0:T(4,128)S(1)} all-gather(s32[1,32,3]{1,2,0:T(4,128)S(1)} %bitcast.395), channel_id=1, replica_groups=mesh['rep'=1,'kv2'=4,'kv'=8] {'kv'}, dimensions={0}, use_global_device_ids=true | all-gather | bytes 3456 | tf_op jit(solution)/shard_map/all_gather | solution.py:34
  118.4 52.4 %all-reduce.3 = (s32[512]{0:T(512)S(1)}, s32[512]{0:T(512)S(1)}) all-reduce(s32[512]{0:T(512)S(1)} %dynamic-update-slice.1, s32[512]{0:T(512)S(1)} %dynamic-update-slice), channel_id=1, replica_groups=mesh['rep'=1,'kv2'=4,'kv'=8] {'kv2','kv'}, use_global_device_ids=true, to_apply=%add.1 | all-reduce | flops 1024 | bytes 8192
  208.8 22.5 %all_gather.45 = bf16[2,256,512]{2,1,0:T(8,128)(2,1)S(1)} all-gather(bf16[2,32,512]{2,1,0:T(8,128)(2,1)S(1)} %pad_maximum_fusion.6), channel_id=1, replica_groups=mesh['rep'=1,'kv2'=4,'kv'=8] {'kv'}, dimensions={1}, use_global_device_ids=true | all-gather | bytes 589824 | tf_op jit(solution)/shard_map/all_gather | solution.py:63
  240.5 24.9 %all-gather.9.cloned.1.call-done = bf16[512,2,2,16,8,64]{5,3,4,2,0,1:T(8,128)(2,1)} async-done(((bf16[16,2,2,16,8,64]{5,3,4,2,0,1:T(8,128)(2,1)}), bf16[512,2,2,16,8,64]{5,3,4,2,0,1:T(8,128)(2,1)}) %all-gather.9.cloned.1.call-update) | async-done | bytes 33554448 | tf_op jit(solution)/shard_map/all_gather | solution.py:29
  265.4 44.5 %slice_bitcast_fusion.1 = (bf16[512,2,16,8,64]{4,2,3,1,0:T(8,128)(2,1)}, bf16[512,2,16,8,64]{4,2,3,1,0:T(8,128)(2,1)}) fusion(bf16[512,2,2,16,8,64]{5,3,4,2,0,1:T(8,128)(2,1)} %all-gather.9.cloned.1.call-done), kind=kLoop, calls=%fused_computation.41 | loop fusion | bytes 67108864 | tf_op jit(solution)/shard_map/squeeze | solution.py:32
  309.9 23.3 %copy.406 = bf16[512,2,16,8,64]{4,3,2,1,0:T(8,128)(2,1)} copy(bf16[512,2,16,8,64]{4,2,3,1,0:T(8,128)(2,1)} %get-tuple-element.40) | data formatting | bytes 33554432 | tf_op jit(solution)/shard_map/squeeze | solution.py:32
  333.3 78.0 %scatter_fusion = bf16[208,2,16,8,64]{4,3,2,1,0:T(8,128)(2,1)} fusion(bf16[208,2,16,8,64]{4,3,2,1,0:T(8,128)(2,1)} %copy.405, s32[512]{0:T(512)S(1)} %compare_select_fusion.3, bf16[512,2,16,8,64]{4,3,2,1,0:T(8,128)(2,1)} %copy.406), kind=kCustom, calls=%fused_computation.18 | custom fusion | bytes 50333696 | tf_op jit(solution)/shard_map/scatter | solution.py:32
  411.2 26.3 %scatter_fusion.1 = bf16[208,2,16,8,64]{4,3,2,1,0:T(8,128)(2,1)} fusion(bf16[208,2,16,8,64]{4,3,2,1,0:T(8,128)(2,1)} %scatter_fusion, s32[256]{0:T(256)S(1)} %bitcast.361, bf16[256,8,64]{2,1,0:T(8,128)(2,1)S(1)} %copy.408), kind=kCustom, calls=%fused_computation.19 | custom fusion | bytes 789504 | tf_op jit(solution)/shard_map/scatter | solution.py:64
  437.5 8.9 slice.258
  446.4 8.4 fusion.60
  462.4 19.8 %scatter_fusion.2 = f32[256,8,4]{1,2,0:T(4,128)S(1)} fusion(f32[256,8,4]{1,2,0:T(4,128)S(1)} %broadcast.282.clone, s32[208]{0:T(256)S(1)} %get-tuple-element.33, f32[208,8,4]{1,2,0:T(4,128)S(1)} %copy.411), kind=kCustom, calls=%fused_computation.20 | custom fusion | flops 6656 | bytes 80704 | tf_op jit(solution)/shard_map/scatter-max | solution.py:72
  483.7 23.3 %copy.418 = bf16[512,2,16,8,64]{4,3,2,1,0:T(8,128)(2,1)} copy(bf16[512,2,16,8,64]{4,2,3,1,0:T(8,128)(2,1)} %get-tuple-element.41) | data formatting | bytes 33554432 | tf_op jit(solution)/shard_map/squeeze | solution.py:33
  507.1 79.4 %scatter_fusion.4 = bf16[208,2,16,8,64]{4,3,2,1,0:T(8,128)(2,1)} fusion(bf16[208,2,16,8,64]{4,3,2,1,0:T(8,128)(2,1)} %copy.417, s32[512]{0:T(512)S(1)} %compare_select_fusion.3, bf16[512,2,16,8,64]{4,3,2,1,0:T(8,128)(2,1)} %copy.418), kind=kCustom, calls=%fused_computation.22 | custom fusion | bytes 50333696 | tf_op jit(solution)/shard_map/scatter | solution.py:33
  586.5 26.7 %scatter_fusion.5 = bf16[208,2,16,8,64]{4,3,2,1,0:T(8,128)(2,1)} fusion(bf16[208,2,16,8,64]{4,3,2,1,0:T(8,128)(2,1)} %scatter_fusion.4, s32[256]{0:T(256)S(1)} %bitcast.362, bf16[256,8,64]{2,1,0:T(8,128)(2,1)S(1)} %copy.420), kind=kCustom, calls=%fused_computation.23 | custom fusion | bytes 789504 | tf_op jit(solution)/shard_map/scatter | solution.py:65
  624.9 8.1 scatter_fusion.3
  651.1 23.1 %scatter_fusion.6 = f32[256,8,4,64]{3,1,2,0:T(8,128)} fusion(f32[256,8,4,64]{3,1,2,0:T(8,128)} %broadcast.297.clone.1, s32[208]{0:T(256)S(1)} %copy-done.11, f32[208,8,4,64]{3,1,2,0:T(8,128)S(1)} %copy-done.3), kind=kCustom, calls=%fused_computation.24 | custom fusion | flops 425984 | bytes 5112640 | tf_op jit(solution)/shard_map/scatter-add | solution.py:75
  674.2 8.8 pad_maximum_fusion
  683.1 32.0 %all-to-all-start = ((f32[256,8,4,66]{3,1,2,0:T(8,128)}), f32[256,8,4,66]{3,1,2,0:T(8,128)}, u32[]{:S(2)}, u32[]{:S(2)}) async-start(f32[256,8,4,66]{3,1,2,0:T(8,128)} %pad_maximum_fusion), calls=%async_computation | async-start | bytes 8388608 | tf_op jit(solution)/shard_map/all_to_all | solution.py:77
  724.9 55.0 %all_gather.49 = bf16[2,256,512]{2,1,0:T(8,128)(2,1)S(1)} all-gather(bf16[2,32,512]{2,1,0:T(8,128)(2,1)S(1)} %pad_maximum_fusion.8), channel_id=1, replica_groups=mesh['rep'=1,'kv2'=4,'kv'=8] {'kv'}, dimensions={1}, use_global_device_ids=true | all-gather | bytes 589824 | tf_op jit(solution)/shard_map/all_gather | solution.py:63
  788.2 8.2 fusion.376
  813.6 23.5 %fusion.97 = bf16[32,2048]{1,0:T(8,128)(2,1)S(1)} fusion(bf16[2,8192,2048]{2,1,0:T(8,128)(2,1)} %param.19, bf16[32,2048]{1,0:T(8,128)(2,1)S(1)} %fusion.121, bf16[2,2048,8192]{2,1,0:T(8,128)(2,1)} %param.18), kind=kOutput, calls=%fused_computation.141 | convolution fusion | flops 2150039552 | bytes 67502080 | tf_op jit(solution)/shard_map/dot_general | solution.py:83
  847.0 21.8 %all_gather.47 = bf16[2,256,512]{2,1,0:T(8,128)(2,1)S(1)} all-gather(bf16[2,32,512]{2,1,0:T(8,128)(2,1)S(1)} %pad_maximum_fusion.7), channel_id=1, replica_groups=mesh['rep'=1,'kv2'=4,'kv'=8] {'kv'}, dimensions={1}, use_global_device_ids=true | all-gather | bytes 589824 | tf_op jit(solution)/shard_map/all_gather | solution.py:63
  869.3 26.4 %scatter_fusion.7 = bf16[208,2,16,8,64]{4,3,2,1,0:T(8,128)(2,1)} fusion(bf16[208,2,16,8,64]{4,3,2,1,0:T(8,128)(2,1)} %scatter_fusion.1, s32[256]{0:T(256)S(1)} %bitcast.357, bf16[256,8,64]{2,1,0:T(8,128)(2,1)S(1)} %copy.432), kind=kCustom, calls=%fused_computation.25 | custom fusion | bytes 789504 | tf_op jit(solution)/shard_map/scatter | solution.py:64
  895.7 8.8 slice.266
  904.5 26.2 %scatter_fusion.12 = bf16[208,2,16,8,64]{4,3,2,1,0:T(8,128)(2,1)} fusion(bf16[208,2,16,8,64]{4,3,2,1,0:T(8,128)(2,1)} %scatter_fusion.7, s32[256]{0:T(256)S(1)} %bitcast.359, bf16[256,8,64]{2,1,0:T(8,128)(2,1)S(1)} %copy.454), kind=kCustom, calls=%fused_computation.30 | custom fusion | bytes 789504 | tf_op jit(solution)/shard_map/scatter | solution.py:64
  930.7 8.9 slice.273
  939.6 8.4 fusion.62
  956.2 8.3 scatter_fusion.13
  966.7 26.6 %scatter_fusion.10 = bf16[208,2,16,8,64]{4,3,2,1,0:T(8,128)(2,1)} fusion(bf16[208,2,16,8,64]{4,3,2,1,0:T(8,128)(2,1)} %scatter_fusion.5, s32[256]{0:T(256)S(1)} %bitcast.358, bf16[256,8,64]{2,1,0:T(8,128)(2,1)S(1)} %copy.442), kind=kCustom, calls=%fused_computation.28 | custom fusion | bytes 789504 | tf_op jit(solution)/shard_map/scatter | solution.py:65
  993.3 8.7 slice.268
  1002.0 26.6 %scatter_fusion.15 = bf16[208,2,16,8,64]{4,3,2,1,0:T(8,128)(2,1)} fusion(bf16[208,2,16,8,64]{4,3,2,1,0:T(8,128)(2,1)} %scatter_fusion.10, s32[256]{0:T(256)S(1)} %bitcast.360, bf16[256,8,64]{2,1,0:T(8,128)(2,1)S(1)} %copy.464), kind=kCustom, calls=%fused_computation.33 | custom fusion | bytes 789504 | tf_op jit(solution)/shard_map/scatter | solution.py:65
  1028.6 8.8 slice.275
  1051.6 8.9 fusion.61
  1062.3 8.1 scatter_fusion.8
  1087.6 8.1 scatter_fusion.14
  1105.7 24.4 %scatter_fusion.16 = f32[256,8,4,64]{3,1,2,0:T(8,128)} fusion(f32[256,8,4,64]{3,1,2,0:T(8,128)} %broadcast.297.clone.2, s32[208]{0:T(256)S(1)} %copy-done.11, f32[208,8,4,64]{3,1,2,0:T(8,128)} %copy.466), kind=kCustom, calls=%fused_computation.34 | custom fusion | flops 425984 | bytes 5112640 | tf_op jit(solution)/shard_map/scatter-add | solution.py:75
  1130.1 8.9 pad_maximum_fusion.2
  1139.0 27.3 %all-to-all-start.2 = ((f32[256,8,4,66]{3,1,2,0:T(8,128)}), f32[256,8,4,66]{3,1,2,0:T(8,128)}, u32[]{:S(2)}, u32[]{:S(2)}) async-start(f32[256,8,4,66]{3,1,2,0:T(8,128)} %pad_maximum_fusion.2), calls=%async_computation.2 | async-start | bytes 8388608 | tf_op jit(solution)/shard_map/all_to_all | solution.py:77
  1176.4 8.1 scatter_fusion.9
  1202.6 23.1 %scatter_fusion.11 = f32[256,8,4,64]{3,1,2,0:T(8,128)} fusion(f32[256,8,4,64]{3,1,2,0:T(8,128)} %broadcast.297.clone.3, s32[208]{0:T(256)S(1)} %copy-done.11, f32[208,8,4,64]{3,1,2,0:T(8,128)S(1)} %copy-done.4), kind=kCustom, calls=%fused_computation.29 | custom fusion | flops 425984 | bytes 5112640 | tf_op jit(solution)/shard_map/scatter-add | solution.py:75
  1225.7 8.8 pad_maximum_fusion.1
  1241.6 8.2 fusion.375
  1267.1 23.5 %fusion.94 = bf16[32,2048]{1,0:T(8,128)(2,1)S(1)} fusion(bf16[2,8192,2048]{2,1,0:T(8,128)(2,1)} %param.19, bf16[32,2048]{1,0:T(8,128)(2,1)S(1)} %fusion.118, bf16[2,2048,8192]{2,1,0:T(8,128)(2,1)} %param.18), kind=kOutput, calls=%fused_computation.140 | convolution fusion | flops 2150039552 | bytes 67502080 | tf_op jit(solution)/shard_map/dot_general | solution.py:83
  1300.3 8.1 fusion.373
  1308.5 19.1 %all_gather.51 = bf16[2,256,512]{2,1,0:T(8,128)(2,1)S(1)} all-gather(bf16[2,32,512]{2,1,0:T(8,128)(2,1)S(1)} %pad_maximum_fusion.9), channel_id=1, replica_groups=mesh['rep'=1,'kv2'=4,'kv'=8] {'kv'}, dimensions={1}, use_global_device_ids=true | all-gather | bytes 589824 | tf_op jit(solution)/shard_map/all_gather | solution.py:63
  1328.2 26.2 %scatter_fusion.17 = bf16[208,2,16,8,64]{4,3,2,1,0:T(8,128)(2,1)} fusion(bf16[208,2,16,8,64]{4,3,2,1,0:T(8,128)(2,1)} %scatter_fusion.12, s32[256]{0:T(256)S(1)} %bitcast.355, bf16[256,8,64]{2,1,0:T(8,128)(2,1)S(1)} %copy.476), kind=kCustom, calls=%fused_computation.35 | custom fusion | bytes 789504 | tf_op jit(solution)/shard_map/scatter | solution.py:64
  1354.4 8.7 slice.280
  1363.1 17.8 %copy.496 = bf16[208,2,16,8,64]{0,4,3,2,1:T(8,128)(2,1)} copy(bf16[208,2,16,8,64]{4,3,2,1,0:T(8,128)(2,1)} %scatter_fusion.17) | data formatting | bytes 13631488
  1381.4 26.6 %scatter_fusion.20 = bf16[208,2,16,8,64]{4,3,2,1,0:T(8,128)(2,1)} fusion(bf16[208,2,16,8,64]{4,3,2,1,0:T(8,128)(2,1)} %scatter_fusion.15, s32[256]{0:T(256)S(1)} %bitcast.356, bf16[256,8,64]{2,1,0:T(8,128)(2,1)S(1)} %copy.486), kind=kCustom, calls=%fused_computation.38 | custom fusion | bytes 789504 | tf_op jit(solution)/shard_map/scatter | solution.py:65
  1407.9 8.7 slice.282
  1416.7 17.8 %copy.497 = bf16[208,2,16,8,64]{0,4,3,2,1:T(8,128)(2,1)} copy(bf16[208,2,16,8,64]{4,3,2,1,0:T(8,128)(2,1)} %scatter_fusion.20) | data formatting | bytes 13631488
  1457.9 8.3 fusion.63
  1468.0 8.1 scatter_fusion.18
  1493.4 8.1 scatter_fusion.19
  1519.5 23.1 %scatter_fusion.21 = f32[256,8,4,64]{3,1,2,0:T(8,128)} fusion(f32[256,8,4,64]{3,1,2,0:T(8,128)} %broadcast.297.clone, s32[208]{0:T(256)S(1)} %copy-done.11, f32[208,8,4,64]{3,1,2,0:T(8,128)S(1)} %copy-done.2), kind=kCustom, calls=%fused_computation.39 | custom fusion | flops 425984 | bytes 5112640 | tf_op jit(solution)/shard_map/scatter-add | solution.py:75
  1542.7 8.9 pad_maximum_fusion.3
  1551.5 19.6 %all-to-all-start.3 = ((f32[256,8,4,66]{3,1,2,0:T(8,128)}), f32[256,8,4,66]{3,1,2,0:T(8,128)}, u32[]{:S(2)}, u32[]{:S(2)}) async-start(f32[256,8,4,66]{3,1,2,0:T(8,128)} %pad_maximum_fusion.3), calls=%async_computation.3 | async-start | bytes 8388608 | tf_op jit(solution)/shard_map/all_to_all | solution.py:77
  1571.1 23.5 %fusion.124 = bf16[1,32,2048]{2,1,0:T(8,128)(2,1)S(1)} fusion(bf16[2,8192,2048]{2,1,0:T(8,128)(2,1)} %param.19, bf16[32,2048]{1,0:T(8,128)(2,1)S(1)} %copy-done.30, bf16[2,2048,8192]{2,1,0:T(8,128)(2,1)} %param.18), kind=kOutput, calls=%fused_computation.150 | convolution fusion | flops 2150039552 | bytes 67502080 | tf_op jit(solution)/shard_map/dot_general | solution.py:83
  1594.6 25.0 %all-to-all-done.3 = f32[256,8,4,66]{3,1,2,0:T(8,128)} async-done(((f32[256,8,4,66]{3,1,2,0:T(8,128)}), f32[256,8,4,66]{3,1,2,0:T(8,128)}, u32[]{:S(2)}, u32[]{:S(2)}) %all-to-all-start.3) | async-done | bytes 2162720 | tf_op jit(solution)/shard_map/all_to_all | solution.py:77
  1645.0 23.5 %fusion.127 = bf16[1,32,2048]{2,1,0:T(8,128)(2,1)S(1)} fusion(bf16[2,8192,2048]{2,1,0:T(8,128)(2,1)} %param.19, bf16[32,2048]{1,0:T(8,128)(2,1)S(1)} %fusion.112, bf16[2,2048,8192]{2,1,0:T(8,128)(2,1)} %param.18), kind=kOutput, calls=%fused_computation.151 | convolution fusion | flops 2150039552 | bytes 67502080 | tf_op jit(solution)/shard_map/dot_general | solution.py:83
  (293 shorter events, 353.2 us)
Async XLA Ops:
  7.2 227.1 %all-gather.7.cloned.1.call-start = ((), (), s32[]{:S(2)}) async-start(), calls=%async_computation.4 | async-start | bytes 1179648 | tf_op jit(solution)/shard_map/all_gather | solution.py:62
  13.0 252.4 %all-gather.9.cloned.1.call-start = ((), (), s32[]{:S(2)}) async-start(), calls=%async_computation.5 | async-start | bytes 69206016 | tf_op jit(solution)/shard_map/all_gather | solution.py:29
  30.8 17.7 %copy-start.22 = (s32[16]{0:T(128)S(1)}, s32[16]{0:T(128)}, u32[]{:S(2)}) copy-start(s32[16]{0:T(128)} %param.24) | copy-start | bytes 196
  79.3 17.7 %copy-start.18 = (s32[32,3]{0,1:T(4,128)S(1)}, s32[32,3]{0,1:T(4,128)}, u32[]{:S(2)}) copy-start(s32[32,3]{0,1:T(4,128)} %param.22) | copy-start | bytes 1156
  79.3 38.8 %copy-start.23 = (s32[16]{0:T(128)S(1)}, s32[16]{0:T(128)}, u32[]{:S(2)}) copy-start(s32[16]{0:T(128)} %param.25) | copy-start | bytes 196
  177.8 6.0 copy-start.25
  177.8 10.6 copy-start.24
  182.9 21.9 %copy-start.19 = (bf16[2,32,2048]{2,1,0:T(8,128)(2,1)S(1)}, bf16[2,32,2048]{2,1,0:T(8,128)(2,1)}, u32[]{:S(2)}) copy-start(bf16[2,32,2048]{2,1,0:T(8,128)(2,1)} %param.13) | copy-start | bytes 786436
  196.3 266.1 %copy-start.12 = (s32[208]{0:T(256)}, s32[208]{0:T(256)S(1)}, u32[]{:S(2)}) copy-start(s32[208]{0:T(256)S(1)} %get-tuple-element.33) | copy-start | bytes 2500
  232.3 251.0 %copy-start.15 = (pred[208]{0:T(512)(128)(4,1)}, pred[208]{0:T(512)(128)(4,1)S(1)}, u32[]{:S(2)}) copy-start(pred[208]{0:T(512)(128)(4,1)S(1)} %broadcast_compare_fusion.5) | copy-start | bytes 628
  437.5 8.9 copy-start.7
  613.2 4.6 copy-start.5
  622.6 2.4 copy-start.11
  648.0 3.1 copy-start.3
  683.1 32.0 %copy-start.20 = (bf16[2,32,2048]{2,1,0:T(8,128)(2,1)S(1)}, bf16[2,32,2048]{2,1,0:T(8,128)(2,1)}, u32[]{:S(2)}) copy-start(bf16[2,32,2048]{2,1,0:T(8,128)(2,1)} %param.13) | copy-start | bytes 786436
  683.1 105.1 %all-to-all-start = ((f32[256,8,4,66]{3,1,2,0:T(8,128)}), f32[256,8,4,66]{3,1,2,0:T(8,128)}, u32[]{:S(2)}, u32[]{:S(2)}) async-start(f32[256,8,4,66]{3,1,2,0:T(8,128)} %pad_maximum_fusion), calls=%async_computation | async-start | bytes 8388608 | tf_op jit(solution)/shard_map/all_to_all | solution.py:77
  715.0 66.4 %all-gather.13.cloned.1.call-start = ((), (), s32[]{:S(2)}) async-start(), calls=%async_computation.7 | async-start | bytes 1179648 | tf_op jit(solution)/shard_map/all_gather | solution.py:62
  720.7 60.2 %copy-start.14 = (s32[256]{0:T(256)S(1)}, s32[256]{0:T(256)}, u32[]{:S(2)}) copy-start(s32[256]{0:T(256)} %get-tuple-element.66) | copy-start | bytes 3076
  720.7 60.2 %copy-start.17 = (s32[256]{0:T(256)S(1)}, s32[256]{0:T(256)}, u32[]{:S(2)}) copy-start(s32[256]{0:T(256)} %get-tuple-element.81) | copy-start | bytes 3076
  720.7 324.2 %all-gather.11.cloned.1.call-start = ((), (), s32[]{:S(2)}) async-start(), calls=%async_computation.6 | async-start | bytes 1179648 | tf_op jit(solution)/shard_map/all_gather | solution.py:62
  837.1 7.8 copy-start.26
  844.8 24.5 %copy-start.1 = (s32[256,1]{0,1:T(1,128)S(1)}, s32[256,1]{0,1:T(1,128)}, u32[]{:S(2)}) copy-start(s32[256,1]{0,1:T(1,128)} %get-tuple-element.36) | copy-start | bytes 3076
  930.7 8.9 copy-start.6
  930.7 8.9 copy-start.8
  948.0 8.2 copy-start.13
  1070.4 6.9 copy-start.9
  1070.4 6.9 copy-start.10
  1070.4 6.9 copy-start.16
  1139.0 95.5 %all-to-all-start.2 = ((f32[256,8,4,66]{3,1,2,0:T(8,128)}), f32[256,8,4,66]{3,1,2,0:T(8,128)}, u32[]{:S(2)}, u32[]{:S(2)}) async-start(f32[256,8,4,66]{3,1,2,0:T(8,128)} %pad_maximum_fusion.2), calls=%async_computation.2 | async-start | bytes 8388608 | tf_op jit(solution)/shard_map/all_to_all | solution.py:77
  1199.4 3.1 copy-start.4
  1234.5 65.8 %all-to-all-start.1 = ((f32[256,8,4,66]{3,1,2,0:T(8,128)}), f32[256,8,4,66]{3,1,2,0:T(8,128)}, u32[]{:S(2)}, u32[]{:S(2)}) async-start(f32[256,8,4,66]{3,1,2,0:T(8,128)} %pad_maximum_fusion.1), calls=%async_computation.1 | async-start | bytes 8388608 | tf_op jit(solution)/shard_map/all_to_all | solution.py:77
  1241.4 211.2 %all-gather.15.cloned.1.call-start = ((), (), s32[]{:S(2)}) async-start(), calls=%async_computation.8 | async-start | bytes 1179648 | tf_op jit(solution)/shard_map/all_gather | solution.py:62
  1257.0 5.1 copy-start.21
  1290.5 9.8 copy-start.28
  1300.3 27.9 %copy-start = (s32[256,1]{0,1:T(1,128)S(1)}, s32[256,1]{0,1:T(1,128)}, u32[]{:S(2)}) copy-start(s32[256,1]{0,1:T(1,128)} %get-tuple-element.29) | copy-start | bytes 3076
  1441.7 5.2 copy-start.27
  1516.4 3.1 copy-start.2
  1551.5 19.6 %copy-start.30 = (bf16[32,2048]{1,0:T(8,128)(2,1)S(1)}, bf16[32,2048]{1,0:T(8,128)(2,1)}, u32[]{:S(2)}) copy-start(bf16[32,2048]{1,0:T(8,128)(2,1)} %fusion.115) | copy-start | bytes 393220
  1551.5 68.1 %all-to-all-start.3 = ((f32[256,8,4,66]{3,1,2,0:T(8,128)}), f32[256,8,4,66]{3,1,2,0:T(8,128)}, u32[]{:S(2)}, u32[]{:S(2)}) async-start(f32[256,8,4,66]{3,1,2,0:T(8,128)} %pad_maximum_fusion.3), calls=%async_computation.3 | async-start | bytes 8388608 | tf_op jit(solution)/shard_map/all_to_all | solution.py:77
  1635.0 5.1 copy-start.29
Sparse Core Ops, SparseCore 0:
  13.1 24.8 all-gather.6
  61.8 203.5 all-gather.8
  720.8 29.6 all-gather.12
  845.0 29.5 all-gather.10
  1327.8 30.8 all-gather.14
where the time goes:
time: 1700 us; the launch traced here: 1680 us
  local copies, waits for them, and re-layouts  827 us (49%)
  other arithmetic  284 us (17%)
  matrix products  214 us (13%)
  blocking collectives  198 us (12%)
  starting transfers between devices  86.1 us (5%)
  waiting for transfers between devices  50.3 us (3%)
    unnamed x88, local copies, waits for them, and re-layouts  139 us
    all_gather x4, blocking collectives, per_device(): lax.all_gather(jnp.stack([k_new, v_new]), 'kv', axis=1, tiled=True)  118 us
    scatter x4, local copies, waits for them, and re-layouts, per_device(): v_pool = v_pool.at[w_slot, layer_idx, w_off].set(kv_row[1], mode='drop')  106 us
    scatter x4, local copies, waits for them, and re-layouts, per_device(): k_pool = k_pool.at[w_slot, layer_idx, w_off].set(kv_row[0], mode='drop')  105 us
    dot_general x4, matrix products, per_device(): jnp.dot(up_act, w_down[layer_idx], preferred_element_type=jnp.float32)  93.9 us
    scatter-add x4, other arithmetic, per_device(): jax.ops.segment_sum(slot_w[..., None] * slot_out, seg_ids, num_segments=r...  93.8 us
    all_to_all x4, starting transfers between devices, per_device(): lax.all_to_all(partial_res, 'kv', 0, 0, tiled=True)  85.7 us
    scatter x1, local copies, waits for them, and re-layouts, per_device(): v_pool = v_pool.at[dst_local].set(in_pages[:, 1], mode='drop')  79.4 us
  transfers between devices with their start and end apart: 9, of which 2 were waited for; matrix products, arithmetic and copies ran while one was open for 35% of the time, Pallas kernels for 0%

commit v1 on v0

v1 whole, which is shorter than its diff:
```python
import functools

import jax
import jax.numpy as jnp
from jax import lax
from jax.experimental import pallas as pl
from jax.experimental.pallas import tpu as pltpu
from jax.sharding import PartitionSpec as P

F32 = jnp.float32
BF16 = jnp.bfloat16
NEG = -1e30
NN = (((1,), (0,)), ((), ()))
NT = (((1,), (1,)), ((), ()))
TN = (((0,), (0,)), ((), ()))


def _dot(a, b, dims):
    return lax.dot_general(a, b, dims, preferred_element_type=F32)


def _split(x):
    hi = x.astype(BF16)
    rest = x - hi.astype(F32)
    mid = rest.astype(BF16)
    low = (rest - mid.astype(F32)).astype(BF16)
    return hi, mid, low


def _pick_lhs(x, sel, dims):
    hi, mid, low = _split(x)
    return _dot(hi, sel, dims) + _dot(mid, sel, dims) + _dot(low, sel, dims)


def _pick_rhs(sel, x, dims):
    hi, mid, low = _split(x)
    return _dot(sel, hi, dims) + _dot(sel, mid, dims) + _dot(sel, low, dims)


def _prep_kernel(n_pages, page, old_ref, src_ref, dstr_ref, dstc_ref, len_ref, base_ref, qsel_ref, wsel_ref, cell_ref, mig_ref, info_ref):
    n_slots = qsel_ref.shape[1]
    n_seq = len_ref.shape[0]
    base = base_ref[0]
    found = jnp.sum(jnp.where(old_ref[...] == src_ref[...], dstr_ref[...] + 1, 0).astype(F32), axis=1, keepdims=True).astype(jnp.int32)
    new = jnp.where(found > 0, found - 1, old_ref[...])
    local = new - base
    slot_ids = lax.broadcasted_iota(jnp.int32, (1, n_slots), 1)
    lens = len_ref[...]
    last = lens // page
    q_sel = jnp.zeros((n_seq, n_slots), F32)
    w_sel = jnp.zeros((n_seq, n_slots), F32)
    first = jnp.zeros((1, n_slots), F32)
    for j in range(n_pages):
        eq = (local[j * n_seq:(j + 1) * n_seq] == slot_ids).astype(F32)
        cell_ref[j * n_seq:(j + 1) * n_seq, :] = eq.astype(BF16)
        q_sel = q_sel + eq
        w_sel = w_sel + jnp.where(last == j, eq, 0.0)
        first = first + jnp.sum(eq, axis=0, keepdims=True) * float(j * page)
    qsel_ref[...] = q_sel.astype(BF16)
    wsel_ref[...] = w_sel.astype(BF16)
    used = jnp.sum(q_sel, axis=0, keepdims=True)
    slot_len = jnp.sum(q_sel * lens.astype(F32), axis=0, keepdims=True)
    written = jnp.sum(w_sel, axis=0, keepdims=True)
    w_off = jnp.sum(w_sel * (lens - last * page).astype(F32), axis=0, keepdims=True)
    mig = ((dstc_ref[...] - base) == slot_ids).astype(F32)
    mig_ref[...] = mig.astype(BF16)
    moved = jnp.sum(mig, axis=0, keepdims=True)
    info_ref[0:1, :] = used
    info_ref[1:2, :] = jnp.where(used > 0, slot_len - first, -100.0)
    info_ref[2:3, :] = jnp.where(written > 0, w_off, -100.0)
    info_ref[3:4, :] = moved
    info_ref[4:8, :] = jnp.zeros((4, n_slots), F32)


def _pack_kernel(heads, onehot_ref, k_ref, v_ref, ko_ref, vo_ref):
    page, _, dim, n_slots = k_ref.shape[1:]
    width = page * dim
    for h in range(heads):
        for src, out in ((k_ref, ko_ref), (v_ref, vo_ref)):
            rows = src[0, :, h].reshape(width, n_slots)
            out[:, h * width:(h + 1) * width] = _dot(onehot_ref[...], rows, NT).astype(BF16)


def _attn_kernel(steps, group, layer, heads, n_alias, *refs):
    (q_ref, kn_ref, vn_ref, k_ref, v_ref, mk_ref, mv_ref, qsel_ref, wsel_ref, cell_ref, mig_ref, info_ref) = refs[:12]
    ko_ref, vo_ref, o_ref, ml_ref, q_s, kv_s, kf_s, vf_s, s_s, os_s, ml_s = refs[12 + n_alias:]
    page, _, dim, n_slots = k_ref.shape[1:]
    n_seq = qsel_ref.shape[0]
    n_home = o_ref.shape[0]
    home = n_seq // n_home
    pid = pl.program_id(0)
    n_rt = steps * group
    used = info_ref[0:1, :]
    limit = info_ref[1:2, :]
    w_off = info_ref[2:3, :]
    moved = info_ref[3:4, :] > 0
    cells = cell_ref[...]
    owned = _dot(jnp.ones((8, n_slots), BF16), cells, NT)[0:1] > 0
    scale = dim ** -0.5
    q_sel = qsel_ref[...]
    w_sel = wsel_ref[...]
    for t in range(steps):
        rows = q_ref[:, t].reshape(n_seq, heads * group * dim)
        q_s[t] = _dot(rows, q_sel, TN)
        kv_s[0, t] = _dot(kn_ref[:, t].reshape(n_seq, heads * dim), w_sel, TN)
        kv_s[1, t] = _dot(vn_ref[:, t].reshape(n_seq, heads * dim), w_sel, TN)
    for h in range(heads):
        for which, (pool, pages, out, full) in enumerate(((k_ref, mk_ref, ko_ref, kf_s), (v_ref, mv_ref, vo_ref, vf_s))):
            width = page * dim
            full[...] = _dot(pages[:, h * width:(h + 1) * width], mig_ref[...], TN).reshape(page, dim, n_slots)

            def fill(tok, _, which=which, pool=pool, out=out, full=full, h=h):
                val = jnp.where(moved, full[tok], pool[0, tok, h].astype(F32))
                at = w_off - tok.astype(F32)
                for t in range(steps):
                    val = jnp.where(at == -float(t), kv_s[which, t, h * dim:(h + 1) * dim, :], val)
                full[tok] = val
                out[0, tok, h] = val.astype(BF16)
                return 0

            lax.fori_loop(0, page, fill, 0)

        def score(tok, _, h=h):
            keys = kf_s[tok]
            for t in range(steps):
                for r in range(group):
                    q_row = q_s[t, (h * group + r) * dim:(h * group + r + 1) * dim, :]
                    s_s[t * group + r, pl.ds(tok, 1), :] = jnp.sum(keys * q_row, axis=0, keepdims=True)
            return 0

        lax.fori_loop(0, page, score, 0)
        tok_ids = lax.broadcasted_iota(jnp.int32, (page, n_slots), 0).astype(F32)
        for t in range(steps):
            visible = tok_ids <= limit + float(t)
            for r in range(group):
                sc = jnp.where(visible, s_s[t * group + r] * scale, NEG)
                top = jnp.max(sc, axis=0, keepdims=True)
                ex = jnp.exp(sc - top)
                s_s[t * group + r] = ex
                ml_s[t * group + r:t * group + r + 1, :] = jnp.where(used > 0, top, 0.0)
                ml_s[n_rt + t * group + r:n_rt + t * group + r + 1, :] = jnp.sum(ex, axis=0, keepdims=True)
        m_slot = ml_s[0:n_rt]
        l_slot = ml_s[n_rt:2 * n_rt]
        m_cell = jnp.where(owned, _pick_lhs(m_slot, cells, NT), NEG)
        m_seq = m_cell[:, 0:n_seq]
        for j in range(1, cells.shape[0] // n_seq):
            m_seq = jnp.maximum(m_seq, m_cell[:, j * n_seq:(j + 1) * n_seq])
        has = m_seq > NEG
        m_back = _pick_lhs(jnp.where(has, m_seq, 0.0), q_sel, NN)
        w_slot = jnp.where(used > 0, jnp.exp(m_slot - m_back), 0.0)
        l_seq = _pick_lhs(l_slot * w_slot, q_sel, NT)
        row = (pid * heads + h) * n_rt
        ml_ref[pl.ds(row, n_rt), :] = m_seq
        ml_ref[pl.ds(pl.num_programs(0) * heads * n_rt + row, n_rt), :] = l_seq
        for rt in range(n_rt):
            s_s[rt] = s_s[rt] * w_slot[rt:rt + 1]

        for t in range(steps):
            def weigh(c, _, t=t):
                at = pl.multiple_of(c * 8, 8)
                acc = [jnp.zeros((8, n_slots), F32) for _ in range(group)]
                for tok in range(page):
                    vals = vf_s[tok, pl.ds(at, 8), :]
                    for r in range(group):
                        acc[r] = acc[r] + s_s[t * group + r, tok:tok + 1, :] * vals
                for r in range(group):
                    os_s[pl.ds(r * dim + at, 8), :] = acc[r]
                return 0

            lax.fori_loop(0, dim // 8, weigh, 0)
            part = _pick_rhs(q_sel, os_s[...], NT)
            o_ref[:, t, :, h * group * dim:(h + 1) * group * dim] = part.reshape(n_home, home, group * dim)


def _merge_kernel(heads, dim, group, o_ref, ml_ref, out_ref):
    n_home, steps, home, _ = o_ref.shape
    half = ml_ref.shape[2] // 2
    m = ml_ref[:, :, 0:half]
    l = ml_ref[:, :, half:2 * half]
    top = jnp.max(m, axis=0, keepdims=True)
    w = jnp.exp(m - top)
    total = jnp.sum(w * l, axis=0, keepdims=True)
    w = w / total
    for t in range(steps):
        lane = lax.broadcasted_iota(jnp.int32, (half, heads * dim), 1) // dim
        src = lax.broadcasted_iota(jnp.int32, (half, heads * dim), 0)
        want = (lane // group) * (steps * group) + t * group + lane % group
        spread = (src == want).astype(BF16)
        acc = jnp.zeros((home, heads * dim), F32)
        for k in range(n_home):
            acc = acc + _pick_lhs(w[k], spread, NN) * o_ref[k, t]
        out_ref[t] = acc.astype(BF16)


def solution(mesh):
    n_cols = mesh.shape['kv']
    dev_axes = ('rep', 'kv2', 'kv')
    group_axes = ('kv2', 'kv')
    seq_spec = P(None, dev_axes, None)
    pool_spec = P(dev_axes, None, None, None, None)
    table_spec = P(dev_axes, None)
    vec_spec = P(dev_axes)
    full_spec = P()
    pair = 2

    def per_device(x_embed, w_query, w_key, w_value, w_out, w_up, w_down, k_pool, v_pool, old_table, seq_len, src_slot, dst_slot):
        n_slots, layers, page, kv_heads, dim = k_pool.shape
        steps, seq_dev, width = x_embed.shape
        heads = w_query.shape[2] // dim
        group = heads // kv_heads
        n_pages = old_table.shape[1]
        n_seq = seq_dev * n_cols
        n_move = src_slot.shape[0]
        n_rt = steps * group
        n_grid = kv_heads // pair
        page_w = page * dim
        me = lax.axis_index('kv2') * n_cols + lax.axis_index('kv')
        slot_base = me * n_slots
        k_t = jnp.transpose(k_pool, (1, 2, 3, 4, 0))
        v_t = jnp.transpose(v_pool, (1, 2, 3, 4, 0))

        src_hot = ((src_slot - slot_base)[:, None] == jnp.arange(n_slots, dtype=jnp.int32)[None, :]).astype(BF16)

        def pack(layer):
            blk = pl.BlockSpec((1, page, pair, dim, n_slots), lambda i: (layer, 0, i, 0, 0))
            out = pl.BlockSpec((n_move, pair * page_w), lambda i: (0, i))
            shape = jax.ShapeDtypeStruct((n_move, kv_heads * page_w), BF16)
            return pl.pallas_call(
                functools.partial(_pack_kernel, pair),
                grid=(n_grid,),
                in_specs=[pl.BlockSpec((n_move, n_slots), lambda i: (0, 0)), blk, blk],
                out_specs=[out, out],
                out_shape=[shape, shape],
                cost_estimate=pl.CostEstimate(flops=4 * 256 * n_slots * kv_heads * page_w, bytes_accessed=8 * 2**20, transcendentals=0),
                name='pack_pages',
            )(src_hot, k_t, v_t)

        packed = [pack(layer) for layer in range(layers)]
        moved = [lax.all_gather(jnp.concatenate(p, axis=1), group_axes, tiled=True) for p in packed]

        meta = jnp.concatenate([old_table.T.reshape(-1), seq_len, src_slot, dst_slot])
        meta_all = lax.all_gather(meta, group_axes)
        n_tab = n_pages * seq_dev
        row = lax.dynamic_slice_in_dim(meta_all, lax.axis_index('kv2') * n_cols, n_cols, axis=0)
        old_col = row[:, :n_tab].reshape(n_cols, n_pages, seq_dev).transpose(1, 0, 2).reshape(-1, 1)
        len_col = row[:, n_tab:n_tab + seq_dev].reshape(-1, 1)
        src_all = meta_all[:, n_tab + seq_dev:n_tab + seq_dev + n_move].reshape(1, -1)
        dst_all = meta_all[:, n_tab + seq_dev + n_move:].reshape(1, -1)
        n_all = src_all.shape[1]
        vmem = pl.BlockSpec(memory_space=pltpu.VMEM)
        q_sel, w_sel, cells, mig, info = pl.pallas_call(
            functools.partial(_prep_kernel, n_pages, page),
            in_specs=[vmem] * 5 + [pl.BlockSpec(memory_space=pltpu.SMEM)],
            out_specs=[vmem] * 5,
            out_shape=[
                jax.ShapeDtypeStruct((n_seq, n_slots), BF16),
                jax.ShapeDtypeStruct((n_seq, n_slots), BF16),
                jax.ShapeDtypeStruct((n_pages * n_seq, n_slots), BF16),
                jax.ShapeDtypeStruct((n_all, n_slots), BF16),
                jax.ShapeDtypeStruct((8, n_slots), F32),
            ],
            name='prep_tables',
        )(old_col, src_all, dst_all, dst_all.reshape(-1, 1), len_col, slot_base.reshape(1))

        def attend(layer, qkv, k_prev, v_prev):
            blk = pl.BlockSpec((1, page, pair, dim, n_slots), lambda i: (layer, 0, i, 0, 0))
            q_w, kv_w, m_w = pair * group * dim, pair * dim, pair * page_w
            k_at, v_at = heads * dim // kv_w, (heads + kv_heads) * dim // kv_w

            def fixed(shape):
                return pl.BlockSpec(shape, lambda i: (0,) * len(shape), pipeline_mode=pl.Buffered(1))

            qkv4 = qkv.reshape(n_cols, steps, seq_dev, qkv.shape[-1])
            in_specs = [
                pl.BlockSpec((n_cols, steps, seq_dev, q_w), lambda i: (0, 0, 0, i)),
                pl.BlockSpec((n_cols, steps, seq_dev, kv_w), lambda i: (0, 0, 0, k_at + i)),
                pl.BlockSpec((n_cols, steps, seq_dev, kv_w), lambda i: (0, 0, 0, v_at + i)),
                blk, blk,
                pl.BlockSpec((n_all, m_w), lambda i: (0, i)),
                pl.BlockSpec((n_all, m_w), lambda i: (0, n_grid + i)),
                fixed(q_sel.shape), fixed(w_sel.shape), fixed(cells.shape), fixed(mig.shape), fixed(info.shape),
            ]
            args = [qkv4, qkv4, qkv4, k_t, v_t, moved[layer], moved[layer], q_sel, w_sel, cells, mig, info]
            aliases = {}
            if k_prev is not None:
                in_specs += [pl.BlockSpec(memory_space=pl.ANY)] * 2
                aliases = {len(args): 0, len(args) + 1: 1}
                args += [k_prev, v_prev]
            ml_rows = 2 * kv_heads * n_rt
            return pl.pallas_call(
                functools.partial(_attn_kernel, steps, group, layer, pair, len(aliases)),
                grid=(n_grid,),
                in_specs=in_specs,
                out_specs=[
                    blk, blk,
                    pl.BlockSpec((n_cols, steps, seq_dev, q_w), lambda i: (0, 0, 0, i)),
                    pl.BlockSpec((ml_rows, n_seq), lambda i: (0, 0)),
                ],
                out_shape=[
                    jax.ShapeDtypeStruct(k_t.shape, BF16),
                    jax.ShapeDtypeStruct(v_t.shape, BF16),
                    jax.ShapeDtypeStruct((n_cols, steps, seq_dev, heads * dim), F32),
                    jax.ShapeDtypeStruct((ml_rows, n_seq), F32),
                ],
                scratch_shapes=[
                    pltpu.VMEM((steps, q_w, n_slots), F32),
                    pltpu.VMEM((2, steps, kv_w, n_slots), F32),
                    pltpu.VMEM((page, dim, n_slots), F32),
                    pltpu.VMEM((page, dim, n_slots), F32),
                    pltpu.VMEM((n_rt, page, n_slots), F32),
                    pltpu.VMEM((group * dim, n_slots), F32),
                    pltpu.VMEM((2 * n_rt, n_slots), F32),
                ],
                input_output_aliases=aliases,
                compiler_params=pltpu.CompilerParams(vmem_limit_bytes=48 * 2**20),
                cost_estimate=pl.CostEstimate(flops=40 * 10**9, bytes_accessed=40 * 2**20, transcendentals=0),
                name='slot_attention',
            )(*args)

        hidden = x_embed.reshape(steps * seq_dev, width)
        k_out = v_out = None
        for layer in range(layers):
            qkv = jnp.concatenate([jnp.dot(hidden, w[layer], preferred_element_type=F32).astype(BF16) for w in (w_query, w_key, w_value)], axis=1)
            qkv_row = lax.all_gather(qkv, 'kv', tiled=True)
            k_out, v_out, part, ml = attend(layer, qkv_row, k_out, v_out)
            ml = ml.T.reshape(n_cols, seq_dev, -1)
            part = lax.all_to_all(part, 'kv', 0, 0, tiled=True)
            ml = lax.all_to_all(ml, 'kv', 0, 0, tiled=True)
            attn = pl.pallas_call(
                functools.partial(_merge_kernel, heads, dim, group),
                in_specs=[vmem] * 2,
                out_specs=vmem,
                out_shape=jax.ShapeDtypeStruct((steps, seq_dev, heads * dim), BF16),
                compiler_params=pltpu.CompilerParams(vmem_limit_bytes=32 * 2**20),
                name='merge_partials',
            )(part, ml).reshape(steps * seq_dev, heads * dim)
            hidden = (hidden.astype(F32) + jnp.dot(attn, w_out[layer], preferred_element_type=F32)).astype(BF16)
            up_act = jax.nn.gelu(jnp.dot(hidden, w_up[layer], preferred_element_type=F32)).astype(BF16)
            hidden = (hidden.astype(F32) + jnp.dot(up_act, w_down[layer], preferred_element_type=F32)).astype(BF16)
        y_out = hidden.reshape(steps, seq_dev, width)
        back = (4, 0, 1, 2, 3)
        return y_out, jnp.transpose(k_out, back), jnp.transpose(v_out, back)

    return jax.shard_map(per_device, mesh=mesh, in_specs=(seq_spec, full_spec, full_spec, full_spec, full_spec, full_spec, full_spec, pool_spec, pool_spec, table_spec, vec_spec, vec_spec, vec_spec), out_specs=(seq_spec, pool_spec, pool_spec), check_vma=False)
```

time: 1700 us -> 455 us (0.27); the launches traced: 1680 us -> 454 us
  local copies, waits for them, and re-layouts: 827 us -> 12.9 us
  other arithmetic: 284 us -> 6.13 us
  matrix products: 214 us -> 76.2 us
  Pallas kernels: 0 us -> 119 us
  starting transfers between devices: 86.1 us -> 0.26 us
  blocking collectives: 198 us -> 176 us
    scatter x12 -> x0, local copies, waits for them, and re-layouts: 375 us -> none  [the longest x4 106 us: per_device(): v_pool = v_pool.at[w_slot, layer_idx, w_off].set(kv_row[1], mode='drop')]
    all_gather x5 -> x0, blocking collectives: 139 us -> none  [the longest x4 118 us: per_device(): lax.all_gather(jnp.stack([k_new, v_new]), 'kv', axis=1, tiled=True)]
    dot_general x28 -> x10, matrix products: 214 us -> 76.2 us  [the longest x2 47.8 us: per_device(): jnp.dot(up_act, w_down[layer], preferred_element_type=F32)]
    unnamed x88 -> x35, local copies, waits for them, and re-layouts: 139 us -> 8.28 us
    scatter-add x8 -> x0, other arithmetic: 126 us -> none  [the longest x4 93.8 us: per_device(): jax.ops.segment_sum(slot_w[..., None] * slot_out, seg_ids, num_segments=r...]
    all_to_all x0 -> x4, blocking collectives: none -> 125 us  [the longest x2 106 us: per_device(): part = lax.all_to_all(part, 'kv', 0, 0, tiled=True)]
    pallas_call x0 -> x7, Pallas kernels: none -> 119 us  [the longest x2 101 us: attend(): pl.pallas_call(functools.partial(_attn_kernel, steps, group, layer, pair,...]
    squeeze x11 -> x0, local copies, waits for them, and re-layouts: 93.7 us -> none  [the longest x2 67.8 us: per_device(): k_pool = k_pool.at[dst_local].set(in_pages[:, 0], mode='drop')]
  transfers between devices with their start and end apart: 9 -> 4, of which waited for: 2 -> 2; matrix products, arithmetic and copies ran while one was open for 35% -> 10% of each run, Pallas kernels for 0% -> 15%
where the time goes in v1:
time: 455 us; the launch traced here: 454 us
  blocking collectives  176 us (39%)
  Pallas kernels  119 us (26%)
  matrix products  76.2 us (17%)
  waiting for transfers between devices  49.2 us (11%)
  between operations  14.1 us (3%)
  local copies, waits for them, and re-layouts  12.9 us (3%)
  other arithmetic  6.13 us (1%)
    all_to_all x2, blocking collectives, per_device(): part = lax.all_to_all(part, 'kv', 0, 0, tiled=True)  106 us
    pallas_call x2, Pallas kernels, attend(): pl.pallas_call(functools.partial(_attn_kernel, steps, group, layer, pair,...  101 us
    unnamed x1, blocking collectives  51 us
    dot_general x2, matrix products, per_device(): jnp.dot(up_act, w_down[layer], preferred_element_type=F32)  47.8 us
    all_gather x2, waiting for transfers between devices, per_device(): lax.all_gather(jnp.concatenate(p, axis=1), group_axes, tiled=True)  25 us
    all_gather x2, waiting for transfers between devices, per_device(): qkv_row = lax.all_gather(qkv, 'kv', tiled=True)  23.9 us
    all_to_all x2, blocking collectives, per_device(): ml = lax.all_to_all(ml, 'kv', 0, 0, tiled=True)  19 us
    dot_general x6, matrix products, per_device(): jnp.dot(hidden, w[layer], preferred_element_type=F32).astype(BF16)  18.4 us
  transfers between devices with their start and end apart: 4, of which 2 were waited for; matrix products, arithmetic and copies ran while one was open for 10% of the time, Pallas kernels for 15%

profile of v1, /device:TPU:97, one launch (start us, length us, event | category | flops | bytes accessed | tf_op | source)
XLA Modules:
  0.0 454.1 jit_solution(10845256675205130448)
XLA Ops:
  7.2 0.0 copy-start.16
  7.2 0.1 all-gather.6.cloned.1.call-start
  7.3 2.2 fusion.93
  9.4 2.2 fusion.90
  11.6 0.0 copy-start.13
  11.6 5.0 %fusion.48 = bf16[64,2048]{1,0:T(8,128)(2,1)S(1)} fusion(bf16[64,2048]{1,0:T(8,128)(2,1)S(1)} %bitcast.127, bf16[2,2048,2048]{2,1,0:T(8,128)(2,1)} %param.14), kind=kOutput, calls=%fused_computation.34 | convolution fusion | flops 537001984 | bytes 8912896 | tf_op jit(solution)/shard_map/dot_general | solution.py:323
  16.6 0.8 pad_maximum_fusion.2
  17.4 0.1 all-gather.6.cloned.1.call-update
  17.4 0.1 all-gather.8.cloned.1.call-start
  17.5 0.0 copy-done.13
  17.5 0.7 fusion.112.onehot_ref
  18.2 5.9 %pack_pages.2 = (bf16[16,8192]{1,0:T(8,128)(2,1)}, bf16[16,8192]{1,0:T(8,128)(2,1)}) custom-call(bf16[16,208]{1,0:T(8,128)(2,1)} %fusion.112.onehot_ref, bf16[2,16,8,64,208]{4,3,2,1,0:T(8,128)(2,1)} %bitcast.113, bf16[2,16,8,64,208]{4,3,2,1,0:T(8,128)(2,1)} %bitcast.117), custom_call_target="tpu_custom_call" | custom-call | flops 1744830464 | bytes 8388608 | tf_op jit(solution)/shard_map/pack_pages/pallas_call | solution.py:228
  24.1 1.9 pad_maximum_fusion
  25.9 0.1 all-gather.8.cloned.1.call-update
  26.0 0.0 copy-start.12
  26.0 0.0 copy-start.14
  26.0 0.0 copy-start.15
  26.0 0.1 all-gather.12.cloned.1.call-start
  26.1 5.9 %pack_pages.3 = (bf16[16,8192]{1,0:T(8,128)(2,1)}, bf16[16,8192]{1,0:T(8,128)(2,1)}) custom-call(bf16[16,208]{1,0:T(8,128)(2,1)} %fusion.112.onehot_ref, bf16[2,16,8,64,208]{4,3,2,1,0:T(8,128)(2,1)} %bitcast.114, bf16[2,16,8,64,208]{4,3,2,1,0:T(8,128)(2,1)} %bitcast.118), custom_call_target="tpu_custom_call" | custom-call | flops 1744830464 | bytes 8388608 | tf_op jit(solution)/shard_map/pack_pages/pallas_call | solution.py:228
  32.0 1.9 pad_maximum_fusion.1
  33.9 0.1 all-gather.12.cloned.1.call-update
  34.0 0.1 all-gather.10.cloned.1.call-start
  34.1 0.1 reshape.54
  34.1 0.2 add_dynamic-update-slice_fusion
  34.3 51.0 %all-reduce = s32[5120]{0:T(1024)S(1)} all-reduce(s32[5120]{0:T(1024)S(1)} %add_dynamic-update-slice_fusion), channel_id=2, replica_groups=mesh['rep'=1,'kv2'=4,'kv'=8] {'kv2','kv'}, use_global_device_ids=true, to_apply=%add | all-reduce | flops 5120 | bytes 40960
  85.4 0.1 reshape.67
  85.4 0.1 fusion.121
  85.5 0.6 reshape.58.dstr_ref
  86.1 0.9 reshape_reshape.4.dstc_ref
  87.0 0.6 reshape.57.src_ref
  87.6 0.1 dynamic-slice.1
  87.7 0.1 reshape.55
  87.8 0.8 reshape.71.len_ref
  88.6 1.2 reshape.70.old_ref
  89.7 2.7 prep_tables.1
  92.4 25.0 %all-gather.8.cloned.1.call-done.refs_5_.refs_6_ = bf16[512,16384]{1,0:T(8,128)(2,1)} async-done(((bf16[16,16384]{1,0:T(8,128)(2,1)}), bf16[512,16384]{1,0:T(8,128)(2,1)}) %all-gather.8.cloned.1.call-update) | async-done | bytes 16777232 | tf_op jit(solution)/shard_map/all_gather | solution.py:239
  117.4 1.9 copy-done
  119.3 1.0 copy-done.2
  120.3 0.9 copy-done.4
  121.3 0.9 copy-done.6
  122.2 0.9 copy-done.8
  123.1 0.7 copy-done.10
  123.8 50.4 %slot_attention.2 = (bf16[2,16,8,64,208]{4,3,2,1,0:T(8,128)(2,1)}, bf16[2,16,8,64,208]{4,3,2,1,0:T(8,128)(2,1)}, f32[8,2,32,2048]{3,2,1,0:T(8,128)}, f32[128,256]{1,0:T(8,128)S(1)}) custom-call(bf16[8,2,32,3072]{3,2,1,0:T(8,128)(2,1)S(1)} %bitcast.107, bf16[8,2,32,3072]{3,2,1,0:T(8,128)(2,1)S(1)} %bitcast.108, bf16[8,2,32,3072]{3,2,1,0:T(8,128)(2,1)S(1)} %bitcast.109, ...), custom_call_target="tpu_custom_call" | custom-call | flops 40000000000 | bytes 41943040 | tf_op jit(solution)/shard_map/slot_attention/pallas_call | solution.py:290
  174.2 0.1 copy.25
  174.3 10.5 %all_to_all.20.ml_ref = f32[8,32,128]{2,1,0:T(8,128)S(1)} all-to-all(f32[8,32,128]{2,1,0:T(8,128)S(1)} %bitcast.121), channel_id=1, replica_groups=mesh['rep'=1,'kv2'=4,'kv'=8] {'kv'}, dimensions={0} | all-to-all | bytes 262144 | tf_op jit(solution)/shard_map/all_to_all | solution.py:328
  184.9 53.1 %all_to_all.21.o_ref = f32[8,2,32,2048]{3,2,1,0:T(8,128)S(1)} all-to-all(f32[8,2,32,2048]{3,2,1,0:T(8,128)} %get-tuple-element.27), channel_id=1, replica_groups=mesh['rep'=1,'kv2'=4,'kv'=8] {'kv'}, dimensions={0} | all-to-all | bytes 8388608 | tf_op jit(solution)/shard_map/all_to_all | solution.py:327
  238.0 2.0 merge_partials.2
  239.9 5.0 %fusion.45 = bf16[64,2048]{1,0:T(8,128)(2,1)S(1)} fusion(bf16[64,2048]{1,0:T(8,128)(2,1)S(1)} %bitcast.104, bf16[2,2048,2048]{2,1,0:T(8,128)(2,1)} %param.17, bf16[64,2048]{1,0:T(8,128)(2,1)S(1)} %bitcast.128), kind=kOutput, calls=%fused_computation.33 | convolution fusion | flops 537264128 | bytes 9175040 | tf_op jit(solution)/shard_map/dot_general | solution.py:337
  244.9 23.6 %fusion.39 = bf16[64,2048]{1,0:T(8,128)(2,1)S(1)} fusion(bf16[2,8192,2048]{2,1,0:T(8,128)(2,1)} %param.19, bf16[64,2048]{1,0:T(8,128)(2,1)S(1)} %fusion.45, bf16[2,2048,8192]{2,1,0:T(8,128)(2,1)} %param.18), kind=kOutput, calls=%fused_computation.31 | convolution fusion | flops 4300079104 | bytes 67895296 | tf_op jit(solution)/shard_map/dot_general | solution.py:339
  268.5 2.1 fusion.99
  270.6 2.1 fusion.96
  272.7 5.0 %fusion.51 = bf16[64,2048]{1,0:T(8,128)(2,1)S(1)} fusion(bf16[64,2048]{1,0:T(8,128)(2,1)S(1)} %fusion.39, bf16[2,2048,2048]{2,1,0:T(8,128)(2,1)} %param.14), kind=kOutput, calls=%fused_computation.35 | convolution fusion | flops 537001984 | bytes 8912896 | tf_op jit(solution)/shard_map/dot_general | solution.py:323
  277.7 0.8 pad_maximum_fusion.3
  278.5 0.1 all-gather.10.cloned.1.call-update
  278.6 0.0 all-gather.12.cloned.1.call-done.refs_5_.refs_6_
  278.6 23.9 %all-gather.10.cloned.1.call-done = bf16[512,3072]{1,0:T(8,128)(2,1)} async-done(((bf16[64,3072]{1,0:T(8,128)(2,1)}), bf16[512,3072]{1,0:T(8,128)(2,1)}) %all-gather.10.cloned.1.call-update) | async-done | bytes 3145744 | tf_op jit(solution)/shard_map/all_gather | solution.py:324
  302.6 1.9 copy-done.1
  304.4 50.4 %slot_attention.3 = (bf16[2,16,8,64,208]{4,3,2,1,0:T(8,128)(2,1)}, bf16[2,16,8,64,208]{4,3,2,1,0:T(8,128)(2,1)}, f32[8,2,32,2048]{3,2,1,0:T(8,128)}, f32[128,256]{1,0:T(8,128)S(1)}) custom-call(bf16[8,2,32,3072]{3,2,1,0:T(8,128)(2,1)S(1)} %bitcast.110, bf16[8,2,32,3072]{3,2,1,0:T(8,128)(2,1)S(1)} %bitcast.111, ...), custom_call_target="tpu_custom_call", output_to_operand_aliasing={{0}: (12, {}), {1}: (13, {})} | custom-call | flops 40000000000 | bytes 41943040 | tf_op jit(solution)/shard_map/slot_attention/pallas_call | solution.py:290
  354.8 0.1 copy.26
  354.9 8.5 %all_to_all.22.ml_ref = f32[8,32,128]{2,1,0:T(8,128)S(1)} all-to-all(f32[8,32,128]{2,1,0:T(8,128)S(1)} %bitcast.122), channel_id=1, replica_groups=mesh['rep'=1,'kv2'=4,'kv'=8] {'kv'}, dimensions={0} | all-to-all | bytes 262144 | tf_op jit(solution)/shard_map/all_to_all | solution.py:328
  363.4 53.0 %all_to_all.23.o_ref = f32[8,2,32,2048]{3,2,1,0:T(8,128)S(1)} all-to-all(f32[8,2,32,2048]{3,2,1,0:T(8,128)} %get-tuple-element.33), channel_id=1, replica_groups=mesh['rep'=1,'kv2'=4,'kv'=8] {'kv'}, dimensions={0} | all-to-all | bytes 8388608 | tf_op jit(solution)/shard_map/all_to_all | solution.py:327
  416.4 2.0 merge_partials.3
  418.4 5.0 %fusion.42 = bf16[64,2048]{1,0:T(8,128)(2,1)S(1)} fusion(bf16[64,2048]{1,0:T(8,128)(2,1)S(1)} %bitcast.103, bf16[2,2048,2048]{2,1,0:T(8,128)(2,1)} %param.17, bf16[64,2048]{1,0:T(8,128)(2,1)S(1)} %fusion.39), kind=kOutput, calls=%fused_computation.32 | convolution fusion | flops 537264128 | bytes 9175040 | tf_op jit(solution)/shard_map/dot_general | solution.py:337
  423.3 24.3 %fusion.36 = bf16[64,2048]{1,0:T(8,128)(2,1)} fusion(bf16[2,8192,2048]{2,1,0:T(8,128)(2,1)} %param.19, bf16[64,2048]{1,0:T(8,128)(2,1)S(1)} %fusion.42, bf16[2,2048,8192]{2,1,0:T(8,128)(2,1)} %param.18), kind=kOutput, calls=%fused_computation.30 | convolution fusion | flops 4300079104 | bytes 67895296 | tf_op jit(solution)/shard_map/dot_general | solution.py:339
  (26 shorter events, 0.1 us)
Async XLA Ops:
  7.2 4.4 copy-start.16
  7.2 85.2 %all-gather.6.cloned.1.call-start = ((), (), s32[]{:S(2)}) async-start(), calls=%async_computation.4 | async-start | bytes 3538944 | tf_op jit(solution)/shard_map/all_gather | solution.py:324
  11.6 5.9 %copy-start.13 = (s32[16]{0:T(128)S(1)}, s32[16]{0:T(128)}, u32[]{:S(2)}) copy-start(s32[16]{0:T(128)} %param.24) | copy-start | bytes 196
  17.4 100.0 %all-gather.8.cloned.1.call-start = ((), (), s32[]{:S(2)}) async-start(), calls=%async_computation.5 | async-start | bytes 17301504 | tf_op jit(solution)/shard_map/all_gather | solution.py:239
  26.0 8.0 %copy-start.12 = (s32[32,3]{0,1:T(4,128)S(1)}, s32[32,3]{0,1:T(4,128)}, u32[]{:S(2)}) copy-start(s32[32,3]{0,1:T(4,128)} %param.22) | copy-start | bytes 1156
  26.0 8.1 %copy-start.14 = (s32[16]{0:T(128)S(1)}, s32[16]{0:T(128)}, u32[]{:S(2)}) copy-start(s32[16]{0:T(128)} %param.25) | copy-start | bytes 196
  26.0 8.1 %copy-start.15 = (s32[32]{0:T(128)S(1)}, s32[32]{0:T(128)}, u32[]{:S(2)}) copy-start(s32[32]{0:T(128)} %param.23) | copy-start | bytes 388
  26.0 252.5 %all-gather.12.cloned.1.call-start = ((), (), s32[]{:S(2)}) async-start(), calls=%async_computation.7 | async-start | bytes 17301504 | tf_op jit(solution)/shard_map/all_gather | solution.py:239
  34.0 268.6 %all-gather.10.cloned.1.call-start = ((), (), s32[]{:S(2)}) async-start(), calls=%async_computation.6 | async-start | bytes 3538944 | tf_op jit(solution)/shard_map/all_gather | solution.py:324
  117.4 1.9 copy-start
  119.3 1.0 copy-start.2
  120.3 0.9 copy-start.4
  121.3 0.9 copy-start.6
  122.2 0.9 copy-start.8
  123.1 0.7 copy-start.10
  272.6 29.9 %copy-start.3 = (bf16[768,208]{1,0:T(8,128)(2,1)S(1)}, bf16[768,208]{1,0:T(8,128)(2,1)}, u32[]{:S(2)}) copy-start(bf16[768,208]{1,0:T(8,128)(2,1)} %get-tuple-element.24.refs_9_) | copy-start | bytes 958468
  272.6 29.9 %copy-start.5 = (bf16[512,208]{1,0:T(8,128)(2,1)S(1)}, bf16[512,208]{1,0:T(8,128)(2,1)}, u32[]{:S(2)}) copy-start(bf16[512,208]{1,0:T(8,128)(2,1)} %get-tuple-element.25.refs_10_) | copy-start | bytes 638980
  272.7 29.9 %copy-start.7 = (bf16[256,208]{1,0:T(8,128)(2,1)S(1)}, bf16[256,208]{1,0:T(8,128)(2,1)}, u32[]{:S(2)}) copy-start(bf16[256,208]{1,0:T(8,128)(2,1)} %get-tuple-element.22.refs_7_) | copy-start | bytes 319492
  272.7 29.9 %copy-start.9 = (bf16[256,208]{1,0:T(8,128)(2,1)S(1)}, bf16[256,208]{1,0:T(8,128)(2,1)}, u32[]{:S(2)}) copy-start(bf16[256,208]{1,0:T(8,128)(2,1)} %get-tuple-element.23.refs_8_) | copy-start | bytes 319492
  272.7 29.9 %copy-start.11 = (f32[8,208]{1,0:T(8,128)S(1)}, f32[8,208]{1,0:T(8,128)}, u32[]{:S(2)}) copy-start(f32[8,208]{1,0:T(8,128)} %get-tuple-element.26.refs_11_) | copy-start | bytes 19972
  302.6 1.9 copy-start.1
Sparse Core Ops, SparseCore 0:
  17.5 29.4 all-gather.5
  49.7 67.7 all-gather.7
  119.5 66.8 all-gather.11
  278.7 23.8 all-gather.9

commit v2 on v1

v2 whole, which is shorter than its diff:
```python
import functools

import jax
import jax.numpy as jnp
from jax import lax
from jax.experimental import pallas as pl
from jax.experimental.pallas import tpu as pltpu
from jax.sharding import PartitionSpec as P

F32 = jnp.float32
BF16 = jnp.bfloat16
I32 = jnp.int32
NEG = -1e30
NN = (((1,), (0,)), ((), ()))
NT = (((1,), (1,)), ((), ()))
TN = (((0,), (0,)), ((), ()))
MESH = pl.DeviceIdType.MESH
LANES = 256
I0, I1, I2, I3, I4, I5 = range(6)


def _dot(a, b, dims):
    return lax.dot_general(a, b, dims, preferred_element_type=F32)


def _split(x):
    hi = x.astype(BF16)
    rest = x - hi.astype(F32)
    mid = rest.astype(BF16)
    low = (rest - mid.astype(F32)).astype(BF16)
    return hi, mid, low


def _pick_lhs(x, sel, dims):
    hi, mid, low = _split(x)
    return _dot(hi, sel, dims) + _dot(mid, sel, dims) + _dot(low, sel, dims)


def _pick_rhs(sel, x, dims):
    hi, mid, low = _split(x)
    return _dot(sel, hi, dims) + _dot(sel, mid, dims) + _dot(sel, low, dims)


def _prep_kernel(n_pages, page, n_cols, n_slots, old_ref, src_ref, dstr_ref, dstc_ref, len_ref, mysrc_ref, mysrcc_ref, pos_ref, qsel_ref, cell_ref, arr_ref, info_ref, wsel_ref, mig_ref, winfo_ref):
    base = pos_ref[0]
    my_col = pos_ref[1]
    n_seq = len_ref.shape[0]
    n_all = src_ref.shape[1]
    n_move = mysrc_ref.shape[1]
    n_arr = arr_ref.shape[0]
    spare = LANES - n_slots
    old = old_ref[...]
    hit = old == src_ref[...]
    entry = jnp.sum(jnp.where(hit, lax.broadcasted_iota(I32, (1, n_all), 1) + 1, 0).astype(F32), axis=1, keepdims=True).astype(I32)
    dst = jnp.sum(jnp.where(hit, dstr_ref[...] + 1, 0).astype(F32), axis=1, keepdims=True).astype(I32) - 1
    is_moved = entry > 0
    entry = entry - 1
    dev = entry // n_move
    nth = entry - dev * n_move
    arrival = (dev // n_cols) * n_move + nth
    free = jnp.sum(jnp.where(nth == lax.broadcasted_iota(I32, (1, n_move), 1), mysrc_ref[...] - base, 0).astype(F32), axis=1, keepdims=True).astype(I32)
    arr_lane = jnp.where(arrival < spare, n_slots + arrival, free)
    here = old - base
    here = jnp.where((here >= 0) & (here < n_slots), here, -1)
    lane = jnp.where(is_moved, jnp.where(dev % n_cols == my_col, arr_lane, -1), here)
    final = jnp.where(is_moved, dst, old) - base
    lane_ids = lax.broadcasted_iota(I32, (1, LANES), 1)
    slot_ids = lax.broadcasted_iota(I32, (1, n_slots), 1)
    lens = len_ref[...]
    last = lens // page
    q_sel = jnp.zeros((n_seq, LANES), F32)
    w_sel = jnp.zeros((n_seq, n_slots), F32)
    first = jnp.zeros((1, LANES), F32)
    for j in range(n_pages):
        eq = (lane[j * n_seq:(j + 1) * n_seq] == lane_ids).astype(F32)
        cell_ref[j * n_seq:(j + 1) * n_seq, :] = eq.astype(BF16)
        q_sel = q_sel + eq
        first = first + jnp.sum(eq, axis=0, keepdims=True) * float(j * page)
        w_sel = w_sel + jnp.where((final[j * n_seq:(j + 1) * n_seq] == slot_ids) & (last == j), 1.0, 0.0)
    qsel_ref[...] = q_sel.astype(BF16)
    wsel_ref[...] = w_sel.astype(BF16)
    used = jnp.sum(q_sel, axis=0, keepdims=True)
    slot_len = jnp.sum(q_sel * lens.astype(F32), axis=0, keepdims=True)
    arr_ids = lax.broadcasted_iota(I32, (n_arr, LANES), 0)
    at_spare = jnp.where(lane_ids == n_slots + arr_ids, 1.0, 0.0)
    arr_ref[...] = at_spare.astype(BF16)
    mine = mysrcc_ref[...] - base
    for k in range(n_arr - spare):
        arr_ref[spare + k:spare + k + 1, :] = jnp.where(lane_ids == mine[k:k + 1], 1.0, 0.0).astype(BF16)
    out_lanes = jnp.sum(jnp.where(mine == lane_ids, 1.0, 0.0), axis=0, keepdims=True)
    info_ref[0:1, :] = used
    info_ref[1:2, :] = jnp.where(used > 0, slot_len - first - 1.0, -100.0)
    info_ref[2:3, :] = jnp.where(lane_ids >= n_slots, 1.0, out_lanes)
    info_ref[3:8, :] = jnp.zeros((5, LANES), F32)
    written = jnp.sum(w_sel, axis=0, keepdims=True)
    w_off = jnp.sum(w_sel * (lens - last * page).astype(F32), axis=0, keepdims=True)
    mig = ((dstc_ref[...] - base) == slot_ids).astype(F32)
    mig_ref[...] = mig.astype(BF16)
    winfo_ref[0:1, :] = jnp.sum(mig, axis=0, keepdims=True)
    winfo_ref[1:2, :] = jnp.where(written > 0, w_off, -100.0)
    winfo_ref[2:8, :] = jnp.zeros((6, n_slots), F32)


def _pack_kernel(heads, onehot_ref, k_ref, v_ref, out_ref):
    page, _, dim, n_slots = k_ref.shape[1:]
    width = page * dim
    for h in range(heads):
        for which, src in enumerate((k_ref, v_ref)):
            rows = src[0, :, h].reshape(width, n_slots)
            out_ref[which, :, h * width:(h + 1) * width] = _dot(onehot_ref[...], rows, NT).astype(BF16)


def _copy(src, dst, sems, k, dev):
    return pltpu.make_async_remote_copy(src_ref=src, dst_ref=dst, send_sem=sems.at[0, k], recv_sem=sems.at[1, k], device_id=dev, device_id_type=MESH)


def _rows_on_y(own, out, sems, halves):
    n = out.shape[I0]
    y = lax.axis_index('kv2')
    up, dn, far = (y + I1) % n, (y + n - I1) % n, (y + I2) % n
    to_up, to_dn = {'kv2': up}, {'kv2': dn}
    first = [
        _copy(halves(own, I0), halves(out.at[y], I0), sems, I0, to_up),
        _copy(halves(own, I1), halves(out.at[y], I1), sems, I1, to_up),
        _copy(halves(own, I1), halves(out.at[y], I1), sems, I2, to_dn),
        _copy(halves(own, I0), halves(out.at[y], I0), sems, I3, to_dn),
    ]
    relay = [
        _copy(halves(out.at[dn], I0), halves(out.at[dn], I0), sems, I4, to_up),
        _copy(halves(out.at[up], I1), halves(out.at[up], I1), sems, I5, to_dn),
    ]
    lands = [(dn, I0), (dn, I1), (up, I1), (up, I0), (far, I0), (far, I1)]

    def got(k):
        at, h = lands[k]
        _copy(halves(out.at[at], h), halves(out.at[at], h), sems, k, to_up).wait_recv()

    def start():
        for k in (I0, I2, I1, I3):
            first[k].start()

    def forward():
        got(I0)
        relay[I0].start()
        got(I2)
        relay[I1].start()

    def finish():
        for k in (I1, I3, I4, I5):
            got(k)
        for c in first + relay:
            c.wait_send()

    return start, forward, finish


def _signal_all(devs):
    barrier = pltpu.get_barrier_semaphore()
    for dev in devs:
        pl.semaphore_signal(barrier, inc=1, device_id=dev, device_id_type=MESH)
    pl.semaphore_wait(barrier, len(devs))


def _q_gather(n_cols, q_ref, q_all, x_sem):
    n_x = n_cols // I2
    at = lax.axis_index('kv')
    x, core = at // I2, at % I2
    up, dn, far = (x + I1) % n_x, (x + n_x - I1) % n_x, (x + I2) % n_x
    to_up, to_dn, to_pal = {'kv': up * I2 + core}, {'kv': dn * I2 + core}, {'kv': x * I2 + I1 - core}
    n_half = q_ref.shape[I0] // I2

    def half(ref, h):
        return ref.at[pl.ds(h * n_half, n_half)]

    def slot(pos, c):
        return q_all.at[pos * I2 + c]

    first = [
        _copy(half(q_ref, I0), half(slot(x, core), I0), x_sem, I0, to_up),
        _copy(half(q_ref, I1), half(slot(x, core), I1), x_sem, I1, to_up),
        _copy(half(q_ref, I1), half(slot(x, core), I1), x_sem, I2, to_dn),
        _copy(half(q_ref, I0), half(slot(x, core), I0), x_sem, I3, to_dn),
    ]
    relay = [
        _copy(half(slot(dn, core), I0), half(slot(dn, core), I0), x_sem, I4, to_up),
        _copy(half(slot(up, core), I1), half(slot(up, core), I1), x_sem, I5, to_dn),
    ]
    lands = [(dn, I0), (dn, I1), (up, I1), (up, I0), (far, I0), (far, I1)]
    pal = [_copy(half(slot(p, core), h), half(slot(p, core), h), x_sem, 6 + k, to_pal) for k, (p, h) in enumerate(lands)]
    own = _copy(q_ref, slot(x, core), x_sem, 12, to_pal)

    def got(k):
        p, h = lands[k]
        _copy(half(slot(p, core), h), half(slot(p, core), h), x_sem, k, to_up).wait_recv()

    for k in (I0, I2, I1, I3):
        first[k].start()
    own.start()
    q_all[at] = q_ref[...]
    yield
    got(I0)
    relay[I0].start()
    pal[I0].start()
    got(I2)
    relay[I1].start()
    pal[I2].start()
    yield
    for k in (I1, I3, I4, I5):
        got(k)
        pal[k].start()
    yield
    _copy(q_ref, slot(x, I1 - core), x_sem, 12, to_pal).wait_recv()
    for k, (p, h) in enumerate(lands):
        _copy(half(slot(p, I1 - core), h), half(slot(p, I1 - core), h), x_sem, 6 + k, to_pal).wait_recv()
    for c in first + relay + pal + [own]:
        c.wait_send()


def _x_peers(n_cols):
    n_x = n_cols // I2
    at = lax.axis_index('kv')
    x, core = at // I2, at % I2
    return [{'kv': ((x + I1) % n_x) * I2 + core}, {'kv': ((x + n_x - I1) % n_x) * I2 + core}, {'kv': x * I2 + I1 - core}]


def _y_peers(n_rows):
    y = lax.axis_index('kv2')
    return [{'kv2': (y + I1) % n_rows}, {'kv2': (y + n_rows - I1) % n_rows}]


def _half0(ref, h):
    return ref.at[h]


def _head_kernel(n_rows, n_cols, meta_ref, pages_ref, q_ref, meta_all, pages_all, q_all, m_sem, y_sem, x_sem):
    y, at = lax.axis_index('kv2'), lax.axis_index('kv')
    offsets = [(a, b) for a in range(n_rows) for b in range(n_cols) if (a, b) != (0, 0)]
    peers = [{'kv2': (y + a) % n_rows, 'kv': (at + b) % n_cols} for a, b in offsets]
    _signal_all(peers)
    me = y * n_cols + at
    metas = [_copy(meta_ref, meta_all.at[me], m_sem, k, peers[k]) for k in range(len(peers))]
    for c in metas:
        c.start()
    start, forward, finish = _rows_on_y(pages_ref, pages_all, y_sem, _half0)
    start()
    steps = _q_gather(n_cols, q_ref, q_all, x_sem)
    next(steps)
    meta_all[me] = meta_ref[...]
    pages_all[y] = pages_ref[...]
    next(steps)
    forward()
    next(steps)
    finish()
    for _ in steps:
        pass
    for k, (a, b) in enumerate(offsets):
        frm = ((y + n_rows - a) % n_rows) * n_cols + (at + n_cols - b) % n_cols
        _copy(meta_ref, meta_all.at[frm], m_sem, k, peers[k]).wait_recv()
    for c in metas:
        c.wait_send()


def _query_kernel(n_cols, q_ref, q_all, x_sem):
    _signal_all(_x_peers(n_cols))
    for _ in _q_gather(n_cols, q_ref, q_all, x_sem):
        pass


def _attn_kernel(steps, group, heads, q_ref, k_ref, v_ref, mk_ref, mv_ref, qsel_ref, cell_ref, arr_ref, info_ref, o_ref, ml_ref, q_s, mk_s, mv_s, s_s, os_s, ml_s, ml_all):
    page, _, dim, n_slots = k_ref.shape[1:]
    n_seq = qsel_ref.shape[0]
    n_core, n_x, _, home = o_ref.shape[:4]
    n_arr = arr_ref.shape[0]
    pid = pl.program_id(0)
    n_rt = steps * group
    width = page * dim
    used = info_ref[0:1, :]
    limit = info_ref[1:2, :]
    freed = info_ref[2:3, 0:n_slots] > 0
    cells = cell_ref[...]
    owned = _dot(jnp.ones((8, LANES), BF16), cells, NT)[0:1] > 0
    scale = dim ** -0.5
    q_sel = qsel_ref[...]

    @pl.when(pid == 0)
    def _():
        ml_all[...] = jnp.zeros_like(ml_all)

    for t in range(steps):
        q_s[t] = _dot(q_ref[:, t].reshape(n_seq, heads * group * dim), q_sel, TN)
    tops, sums = [[] for _ in range(steps)], [[] for _ in range(steps)]
    for h in range(heads):
        for pages, full in ((mk_ref, mk_s), (mv_ref, mv_s)):
            full[...] = _dot(pages[:, 0, :, h * width:(h + 1) * width].reshape(n_arr, width), arr_ref[...], TN).reshape(page, dim, LANES)

        def join(tok, _, h=h):
            for pool, full in ((k_ref, mk_s), (v_ref, mv_s)):
                full[tok, :, 0:n_slots] = jnp.where(freed, full[tok, :, 0:n_slots], pool[0, tok, h].astype(F32))
            return 0

        lax.fori_loop(0, page, join, 0)

        def score(pair, _, h=h):
            toks = [pair * 2, pair * 2 + 1]
            keys = [mk_s[tok] for tok in toks]
            for t in range(steps):
                for r in range(group):
                    q_row = q_s[t, (h * group + r) * dim:(h * group + r + 1) * dim, :]
                    for tok, key in zip(toks, keys):
                        s_s[t * group + r, pl.ds(tok, 1), :] = jnp.sum(key * q_row, axis=0, keepdims=True)
            return 0

        lax.fori_loop(0, page // 2, score, 0)
        visible = lax.broadcasted_iota(I32, (page, LANES), 0).astype(F32) <= limit
        for rt in range(n_rt):
            sc = jnp.where(visible, s_s[rt] * scale, NEG)
            top = jnp.max(sc, axis=0, keepdims=True)
            ex = jnp.where(visible, jnp.exp(sc - top), 0.0)
            s_s[rt] = ex
            ml_s[rt:rt + 1, :] = top
            ml_s[n_rt + rt:n_rt + rt + 1, :] = jnp.sum(ex, axis=0, keepdims=True)
        live = (used > 0) & (limit >= 0)
        m_slot = ml_s[0:n_rt]
        l_slot = ml_s[n_rt:2 * n_rt]
        m_cell = jnp.where(owned, _pick_lhs(m_slot, cells, NT), NEG)
        m_seq = m_cell[:, 0:n_seq]
        for j in range(1, cells.shape[0] // n_seq):
            m_seq = jnp.maximum(m_seq, m_cell[:, j * n_seq:(j + 1) * n_seq])
        m_back = _pick_lhs(m_seq, q_sel, NN)
        w_slot = jnp.where(live, jnp.exp(jnp.minimum(m_slot - m_back, 0.0)), 0.0)
        l_seq = _pick_lhs(l_slot * w_slot, q_sel, NT)
        for t in range(steps):
            tops[t].append(m_seq[t * group:(t + 1) * group])
            sums[t].append(l_seq[t * group:(t + 1) * group])
        for rt in range(n_rt):
            s_s[rt] = s_s[rt] * w_slot[rt:rt + 1]

        def weigh(c, _):
            row = pl.multiple_of(c * 8, 8)
            acc = [jnp.zeros((8, LANES), F32) for _ in range(n_rt)]
            for tok in range(page):
                vals = mv_s[tok, pl.ds(row, 8), :]
                for rt in range(n_rt):
                    acc[rt] = acc[rt] + s_s[rt, tok:tok + 1, :] * vals
            for rt in range(n_rt):
                os_s[pl.ds(rt * dim + row, 8), :] = acc[rt]
            return 0

        lax.fori_loop(0, dim // 8, weigh, 0)
        for t in range(steps):
            part = _pick_rhs(q_sel, os_s[t * group * dim:(t + 1) * group * dim, :], NT).reshape(n_x, n_core, home, group * dim)
            for c in range(n_core):
                o_ref[c, :, t, :, h * group * dim:(h + 1) * group * dim] = part[:, c]

    n_row = heads * group
    for t in range(steps):
        ml_all[t, pl.ds(pl.multiple_of(pid * n_row, n_row), n_row), :] = jnp.concatenate(tops[t], axis=0)
        ml_all[t, pl.ds(pl.multiple_of((pl.num_programs(0) + pid) * n_row, n_row), n_row), :] = jnp.concatenate(sums[t], axis=0)

    @pl.when(pid == pl.num_programs(0) - 1)
    def _():
        for t in range(steps):
            flat = ml_all[t].T.reshape(n_x, n_core, home, ml_all.shape[1])
            for c in range(n_core):
                ml_ref[c, :, t] = flat[:, c]


def _exchange_kernel(n_cols, n_rows, heads, dim, has_pages, *refs):
    o_ref, ml_ref, q_ref, kv_ref = refs[:I4]
    n_in = I5 if has_pages else I4
    n_out = I2 if has_pages else I1
    out_ref = refs[n_in]
    rp_o, rp_ml, cur_o, cur_ml, rel_o, rel_ml, fin_o, fin_ml, spread, expand, p_sem, r_sem, y_sem = refs[n_in + n_out:]
    n_x = n_cols // I2
    home = q_ref.shape[I0] // I2
    width = heads * dim
    at = lax.axis_index('kv')
    x, core = at // I2, at % I2
    up, dn, far = (x + I1) % n_x, (x + n_x - I1) % n_x, (x + I2) % n_x
    to_up, to_dn, to_pal = {'kv': up * I2 + core}, {'kv': dn * I2 + core}, {'kv': x * I2 + I1 - core}
    _signal_all(_x_peers(n_cols) + (_y_peers(n_rows) if has_pages else []))
    order = [far, up, dn, x]
    pals = []
    for i, pos in enumerate(order):
        pals.append(_copy(o_ref.at[I1 - core, pos], rp_o.at[i], p_sem, i, to_pal))
        pals.append(_copy(ml_ref.at[I1 - core, pos], rp_ml.at[i], p_sem, I4 + i, to_pal))
    for c in pals:
        c.start()
    if has_pages:
        pages_ref, pages_all = refs[I4], refs[n_in + I1]
        y_start, y_forward, y_finish = _rows_on_y(pages_ref, pages_all, y_sem, _half0)
        y_start()
        pages_all[lax.axis_index('kv2')] = pages_ref[...]

    n_chunk = I4
    cw = width // n_chunk
    kv_w = kv_ref.shape[I1] // I2
    kw = kv_w // n_chunk
    spread[...] = (lax.broadcasted_iota(I32, spread.shape, I1) // dim == lax.broadcasted_iota(I32, spread.shape, I0)).astype(F32).astype(BF16)
    lane = lax.broadcasted_iota(I32, expand.shape, I1)
    row = lax.broadcasted_iota(I32, expand.shape, I0)
    group = cw // kw
    expand[...] = ((lane // (dim * group) == row // dim) & (lane % dim == row % dim)).astype(F32).astype(BF16)

    def widen(w, c):
        return _pick_lhs(w, spread[:, c * cw:(c + I1) * cw], NN)

    s = jnp.zeros((I3 * home, heads), F32)
    for c in range(n_chunk):
        q_c = q_ref[:, c * cw:(c + I1) * cw].astype(F32)
        k_c = _dot(kv_ref[:, c * kw:(c + I1) * kw], expand[...], NN)
        prod = jnp.concatenate([q_c[I0:home] * k_c[I0:home], q_c[home:] * k_c[I0:home], q_c[home:] * k_c[home:]], axis=I0)
        s = s + _pick_lhs(prod, spread[:, c * cw:(c + I1) * cw], NT)
    s = s * dim ** -0.5
    s00, s10, s11 = s[I0:home], s[home:I2 * home], s[I2 * home:]
    m1 = jnp.maximum(s10, s11)
    e10, e11 = jnp.exp(s10 - m1), jnp.exp(s11 - m1)
    self_m = [s00, m1]
    self_l = [jnp.ones_like(s00), e10 + e11]
    self_w = [[(I0, None)], [(I0, e10), (I1, e11)]]

    def stats(ref):
        return ref[:, I0:heads], ref[:, heads:I2 * heads]

    def fold(a_o, a_ml, b_o, b_ml, out_o, out_ml):
        am, al = stats(a_ml)
        bm, bl = stats(b_ml)
        top = jnp.maximum(am, bm)
        aw, bw = jnp.exp(am - top), jnp.exp(bm - top)
        out_ml[:, I0:heads] = top
        out_ml[:, heads:I2 * heads] = aw * al + bw * bl
        w = jnp.concatenate([aw, bw], axis=I0)
        for c in range(n_chunk):
            wx = widen(w, c)
            sl = slice(c * cw, (c + I1) * cw)
            out_o[:, sl] = a_o[:, sl] * wx[I0:home] + b_o[:, sl] * wx[home:]

    cur_ml[...] = jnp.zeros_like(cur_ml)

    def fold_pal(i):
        _copy(o_ref.at[I1 - core, order[i]], rp_o.at[i], p_sem, i, to_pal).wait_recv()
        _copy(ml_ref.at[I1 - core, order[i]], rp_ml.at[i], p_sem, I4 + i, to_pal).wait_recv()
        for t in range(I2):
            fold(o_ref.at[core, order[i], t], ml_ref.at[core, order[i], t], rp_o.at[i, t], rp_ml.at[i, t], cur_o.at[i, t], cur_ml.at[i, t])

    sends = []

    def send(i, t, dst_o, dst_ml, k, dev):
        a = _copy(cur_o.at[i, t], dst_o, r_sem, I2 * k, dev)
        b = _copy(cur_ml.at[i, t], dst_ml, r_sem, I2 * k + I1, dev)
        a.start()
        b.start()
        sends.extend([a, b])

    def got(dst_o, dst_ml, k):
        _copy(dst_o, dst_o, r_sem, I2 * k, to_up).wait_recv()
        _copy(dst_ml, dst_ml, r_sem, I2 * k + I1, to_up).wait_recv()

    fold_pal(I0)
    send(I0, I0, rel_o.at[I0], rel_ml.at[I0], I0, to_up)
    send(I0, I1, rel_o.at[I1], rel_ml.at[I1], I1, to_dn)
    fold_pal(I1)
    send(I1, I1, fin_o.at[I0, I1], fin_ml.at[I0, I1], I2, to_up)
    fold_pal(I2)
    send(I2, I0, fin_o.at[I1, I0], fin_ml.at[I1, I0], I3, to_dn)
    got(rel_o.at[I0], rel_ml.at[I0], I0)
    fold(cur_o.at[I1, I0], cur_ml.at[I1, I0], rel_o.at[I0], rel_ml.at[I0], cur_o.at[I4, I0], cur_ml.at[I4, I0])
    send(I4, I0, fin_o.at[I0, I0], fin_ml.at[I0, I0], I4, to_up)
    got(rel_o.at[I1], rel_ml.at[I1], I1)
    fold(cur_o.at[I2, I1], cur_ml.at[I2, I1], rel_o.at[I1], rel_ml.at[I1], cur_o.at[I4, I1], cur_ml.at[I4, I1])
    send(I4, I1, fin_o.at[I1, I1], fin_ml.at[I1, I1], I5, to_dn)
    fold_pal(I3)
    if has_pages:
        y_forward()
    for side, t, k in ((I0, I1, I2), (I1, I0, I3), (I0, I0, I4), (I1, I1, I5)):
        got(fin_o.at[side, t], fin_ml.at[side, t], k)
    for t in range(I2):
        parts = [(cur_o.at[I3, t], cur_ml.at[I3, t]), (fin_o.at[I0, t], fin_ml.at[I0, t]), (fin_o.at[I1, t], fin_ml.at[I1, t])]
        ms = [stats(ml)[I0] for _, ml in parts] + [self_m[t]]
        ls = [stats(ml)[I1] for _, ml in parts] + [self_l[t]]
        top = functools.reduce(jnp.maximum, ms)
        ws = [jnp.exp(m - top) for m in ms]
        total = functools.reduce(jnp.add, [w * l for w, l in zip(ws, ls)])
        ws = [w / total for w in ws]
        own = ws.pop()
        ws += [own if e is None else own * e for _, e in self_w[t]]
        w = jnp.concatenate(ws, axis=I0)
        for c in range(n_chunk):
            wx = widen(w, c)
            sl = slice(c * cw, (c + I1) * cw)
            v_c = _dot(kv_ref[:, kv_w + c * kw:kv_w + (c + I1) * kw], expand[...], NN)
            acc = jnp.zeros((home, cw), F32)
            for i, (o, _) in enumerate(parts):
                acc = acc + o[:, sl] * wx[i * home:(i + I1) * home]
            for i, (step, _) in enumerate(self_w[t]):
                acc = acc + v_c[step * home:(step + I1) * home] * wx[(I3 + i) * home:(I4 + i) * home]
            out_ref[t * home:(t + I1) * home, sl] = acc.astype(BF16)
    if has_pages:
        y_finish()
    for c in pals + sends:
        c.wait_send()


def _place_kernel(steps, heads, n_alias, *refs):
    kn_ref, vn_ref, k_ref, v_ref, mk_ref, mv_ref, wsel_ref, mig_ref, info_ref = refs[:9]
    ko_ref, vo_ref, kv_s, full = refs[9 + n_alias:]
    page, _, dim, n_slots = k_ref.shape[1:]
    n_seq = wsel_ref.shape[0]
    width = page * dim
    n_all = mig_ref.shape[0]
    moved = info_ref[0:1, :] > 0
    w_off = info_ref[1:2, :]
    for t in range(steps):
        for which, ref in enumerate((kn_ref, vn_ref)):
            kv_s[which, t] = _dot(ref[:, t].reshape(n_seq, heads * dim), wsel_ref[...], TN)
    for h in range(heads):
        for which, (pool, pages, out) in enumerate(((k_ref, mk_ref, ko_ref), (v_ref, mv_ref, vo_ref))):
            full[...] = _dot(pages[:, 0, :, h * width:(h + 1) * width].reshape(n_all, width), mig_ref[...], TN).reshape(page, dim, n_slots)

            def fill(tok, _, which=which, pool=pool, out=out, h=h):
                val = jnp.where(moved, full[tok], pool[0, tok, h].astype(F32))
                at = w_off - tok.astype(F32)
                for t in range(steps):
                    val = jnp.where(at == -float(t), kv_s[which, t, h * dim:(h + 1) * dim, :], val)
                out[0, tok, h] = val.astype(BF16)
                return 0

            lax.fori_loop(0, page, fill, 0)


def solution(mesh):
    n_rows, n_cols = mesh.shape['kv2'], mesh.shape['kv']
    dev_axes = ('rep', 'kv2', 'kv')
    group_axes = ('kv2', 'kv')
    seq_spec = P(None, dev_axes, None)
    pool_spec = P(dev_axes, None, None, None, None)
    table_spec = P(dev_axes, None)
    vec_spec = P(dev_axes)
    full_spec = P()
    pair = 2
    vmem = pl.BlockSpec(memory_space=pltpu.VMEM)
    dma = pltpu.SemaphoreType.DMA

    def per_device(x_embed, w_query, w_key, w_value, w_out, w_up, w_down, k_pool, v_pool, old_table, seq_len, src_slot, dst_slot):
        n_slots, layers, page, kv_heads, dim = k_pool.shape
        steps, seq_dev, width = x_embed.shape
        heads = w_query.shape[2] // dim
        group = heads // kv_heads
        n_pages = old_table.shape[1]
        n_seq = seq_dev * n_cols
        n_move = src_slot.shape[0]
        n_rt = steps * group
        n_grid = kv_heads // pair
        page_w = page * dim
        n_x = n_cols // 2
        n_dev = n_rows * n_cols
        rows = steps * seq_dev
        me = lax.axis_index('kv2') * n_cols + lax.axis_index('kv')
        slot_base = me * n_slots
        k_t = jnp.transpose(k_pool, (1, 2, 3, 4, 0))
        v_t = jnp.transpose(v_pool, (1, 2, 3, 4, 0))
        q_w, kv_w, m_w = pair * group * dim, pair * dim, pair * page_w

        def fixed(shape):
            return pl.BlockSpec(shape, lambda i: (0,) * len(shape), pipeline_mode=pl.Buffered(1))

        src_hot = ((src_slot - slot_base)[:, None] == jnp.arange(n_slots, dtype=I32)[None, :]).astype(BF16)
        page_shape = (2, n_move, kv_heads * page_w)

        def pool_blk(layer):
            return pl.BlockSpec((1, page, pair, dim, n_slots), lambda i: (layer, 0, i, 0, 0))

        def pack(layer):
            blk = pool_blk(layer)
            return pl.pallas_call(
                functools.partial(_pack_kernel, pair),
                grid=(n_grid,),
                in_specs=[pl.BlockSpec((n_move, n_slots), lambda i: (0, 0)), blk, blk],
                out_specs=pl.BlockSpec((2, n_move, m_w), lambda i: (0, 0, i)),
                out_shape=jax.ShapeDtypeStruct(page_shape, BF16),
                cost_estimate=pl.CostEstimate(flops=4 * 10**9, bytes_accessed=8 * 2**20, transcendentals=0),
                name='pack_pages',
            )(src_hot, k_t, v_t)

        packed = [pack(layer) for layer in range(layers)]
        moved = [lax.all_gather(p, group_axes) for p in packed]

        def project(hidden, layer):
            q = jnp.dot(hidden, w_query[layer], preferred_element_type=F32).astype(BF16)
            kv = jnp.concatenate([jnp.dot(hidden, w[layer], preferred_element_type=F32).astype(BF16) for w in (w_key, w_value)], axis=1)
            return q, kv

        hidden = x_embed.reshape(rows, width)
        q, kv = project(hidden, 0)
        meta = jnp.concatenate([old_table.T.reshape(-1), seq_len, src_slot, dst_slot])
        n_meta = meta.shape[0]
        meta = jnp.pad(meta, (0, 8 * 128 - n_meta)).reshape(8, 128)
        pages_all_shape = jax.ShapeDtypeStruct((n_rows,) + page_shape, BF16)
        q_all_shape = jax.ShapeDtypeStruct((n_cols, rows, heads * dim), BF16)
        meta_all, pages_y, q_all = pl.pallas_call(
            functools.partial(_head_kernel, n_rows, n_cols),
            in_specs=[vmem] * 3,
            out_specs=[vmem] * 3,
            out_shape=[jax.ShapeDtypeStruct((n_dev, 8, 128), I32), pages_all_shape, q_all_shape],
            scratch_shapes=[dma((2, n_dev - 1)), dma((2, 6)), dma((2, 13))],
            compiler_params=pltpu.CompilerParams(collective_id=0, has_side_effects=True, vmem_limit_bytes=24 * 2**20),
            cost_estimate=pl.CostEstimate(flops=10**10, bytes_accessed=2**22, transcendentals=0),
            name='head_gather',
        )(meta, packed[0], q)

        meta_all = meta_all.reshape(n_dev, 8 * 128)[:, :n_meta]
        n_tab = n_pages * seq_dev
        row = lax.dynamic_slice_in_dim(meta_all, lax.axis_index('kv2') * n_cols, n_cols, axis=0)
        old_col = row[:, :n_tab].reshape(n_cols, n_pages, seq_dev).transpose(1, 0, 2).reshape(-1, 1)
        len_col = row[:, n_tab:n_tab + seq_dev].reshape(-1, 1)
        src_all = meta_all[:, n_tab + seq_dev:n_tab + seq_dev + n_move].reshape(1, -1)
        dst_all = meta_all[:, n_tab + seq_dev + n_move:].reshape(1, -1)
        n_all = n_dev * n_move
        n_arr = n_rows * n_move
        pos = jnp.stack([slot_base, lax.axis_index('kv')]).astype(I32)
        q_sel, cells, arr, info, w_sel, mig, w_info = pl.pallas_call(
            functools.partial(_prep_kernel, n_pages, page, n_cols, n_slots),
            in_specs=[vmem] * 7 + [pl.BlockSpec(memory_space=pltpu.SMEM)],
            out_specs=[vmem] * 7,
            out_shape=[
                jax.ShapeDtypeStruct((n_seq, LANES), BF16),
                jax.ShapeDtypeStruct((n_pages * n_seq, LANES), BF16),
                jax.ShapeDtypeStruct((n_arr, LANES), BF16),
                jax.ShapeDtypeStruct((8, LANES), F32),
                jax.ShapeDtypeStruct((n_seq, n_slots), BF16),
                jax.ShapeDtypeStruct((n_all, n_slots), BF16),
                jax.ShapeDtypeStruct((8, n_slots), F32),
            ],
            name='prep_tables',
        )(old_col, src_all, dst_all, dst_all.reshape(-1, 1), len_col, src_slot.reshape(1, -1), src_slot.reshape(-1, 1), pos)

        def attend(layer, q_all, pages):
            blk = pool_blk(layer)
            ml_rows = 2 * LANES // 4
            return pl.pallas_call(
                functools.partial(_attn_kernel, steps, group, pair),
                grid=(n_grid,),
                in_specs=[
                    pl.BlockSpec((n_cols, steps, seq_dev, q_w), lambda i: (0, 0, 0, i)),
                    blk, blk,
                    pl.BlockSpec((n_rows, 1, n_move, m_w), lambda i: (0, 0, 0, i)),
                    pl.BlockSpec((n_rows, 1, n_move, m_w), lambda i: (0, 1, 0, i)),
                    fixed(q_sel.shape), fixed(cells.shape), fixed(arr.shape), fixed(info.shape),
                ],
                out_specs=[
                    pl.BlockSpec((2, n_x, steps, seq_dev, q_w), lambda i: (0, 0, 0, 0, i)),
                    pl.BlockSpec((2, n_x, steps, seq_dev, ml_rows), lambda i: (0, 0, 0, 0, 0)),
                ],
                out_shape=[
                    jax.ShapeDtypeStruct((2, n_x, steps, seq_dev, heads * dim), F32),
                    jax.ShapeDtypeStruct((2, n_x, steps, seq_dev, ml_rows), F32),
                ],
                scratch_shapes=[
                    pltpu.VMEM((steps, q_w, LANES), F32),
                    pltpu.VMEM((page, dim, LANES), F32),
                    pltpu.VMEM((page, dim, LANES), F32),
                    pltpu.VMEM((n_rt, page, LANES), F32),
                    pltpu.VMEM((n_rt * dim, LANES), F32),
                    pltpu.VMEM((2 * n_rt, LANES), F32),
                    pltpu.VMEM((steps, ml_rows, n_seq), F32),
                ],
                compiler_params=pltpu.CompilerParams(vmem_limit_bytes=32 * 2**20),
                cost_estimate=pl.CostEstimate(flops=20 * 10**9, bytes_accessed=16 * 2**20, transcendentals=0),
                name='slot_attention',
            )(q_all.reshape(n_cols, steps, seq_dev, heads * dim), k_t, v_t, pages, pages, q_sel, cells, arr, info)

        def exchange(layer, o, ml, q, kv, pages):
            has = pages is not None
            half = (seq_dev, heads * dim)
            stat = (seq_dev, ml.shape[-1])
            out_shape = [jax.ShapeDtypeStruct((rows, heads * dim), BF16)] + ([pages_all_shape] if has else [])
            return pl.pallas_call(
                functools.partial(_exchange_kernel, n_cols, n_rows, heads, dim, has),
                in_specs=[vmem] * (5 if has else 4),
                out_specs=[vmem] * len(out_shape),
                out_shape=out_shape,
                scratch_shapes=[
                    pltpu.VMEM((4, steps) + half, F32), pltpu.VMEM((4, steps) + stat, F32),
                    pltpu.VMEM((5, steps) + half, F32), pltpu.VMEM((5, steps) + stat, F32),
                    pltpu.VMEM((2,) + half, F32), pltpu.VMEM((2,) + stat, F32),
                    pltpu.VMEM((2, steps) + half, F32), pltpu.VMEM((2, steps) + stat, F32),
                    pltpu.VMEM((heads, heads * dim), BF16), pltpu.VMEM((kv_w, q_w), BF16),
                    dma((2, 8)), dma((2, 12)), dma((2, 6)),
                ],
                compiler_params=pltpu.CompilerParams(collective_id=1 + layer, has_side_effects=True, vmem_limit_bytes=32 * 2**20),
                cost_estimate=pl.CostEstimate(flops=10**10, bytes_accessed=2**22, transcendentals=0),
                name='exchange_partials',
            )(o, ml, q, kv, *([pages] if has else []))

        def place(layer, kv_row, k_prev, v_prev):
            blk = pool_blk(layer)
            v_at = kv_heads * dim // kv_w
            in_specs = [
                pl.BlockSpec((n_cols, steps, seq_dev, kv_w), lambda i: (0, 0, 0, i)),
                pl.BlockSpec((n_cols, steps, seq_dev, kv_w), lambda i: (0, 0, 0, v_at + i)),
                blk, blk,
                pl.BlockSpec((n_dev, 1, n_move, m_w), lambda i: (0, 0, 0, i)),
                pl.BlockSpec((n_dev, 1, n_move, m_w), lambda i: (0, 1, 0, i)),
                fixed(w_sel.shape), fixed(mig.shape), fixed(w_info.shape),
            ]
            kv4 = kv_row.reshape(n_cols, steps, seq_dev, -1)
            args = [kv4, kv4, k_t, v_t, moved[layer], moved[layer], w_sel, mig, w_info]
            aliases = {}
            if k_prev is not None:
                in_specs += [pl.BlockSpec(memory_space=pl.ANY)] * 2
                aliases = {len(args): 0, len(args) + 1: 1}
                args += [k_prev, v_prev]
            return pl.pallas_call(
                functools.partial(_place_kernel, steps, pair, len(aliases)),
                grid=(n_grid,),
                in_specs=in_specs,
                out_specs=[blk, blk],
                out_shape=[jax.ShapeDtypeStruct(k_t.shape, BF16), jax.ShapeDtypeStruct(v_t.shape, BF16)],
                scratch_shapes=[pltpu.VMEM((2, steps, kv_w, n_slots), F32), pltpu.VMEM((page, dim, n_slots), F32)],
                input_output_aliases=aliases,
                compiler_params=pltpu.CompilerParams(vmem_limit_bytes=32 * 2**20),
                cost_estimate=pl.CostEstimate(flops=20 * 10**9, bytes_accessed=32 * 2**20, transcendentals=0),
                name='place_pages',
            )(*args)

        k_out = v_out = None
        kv_rows = []
        for layer in range(layers):
            if layer:
                q, kv = project(hidden, layer)
                [q_all] = pl.pallas_call(
                    functools.partial(_query_kernel, n_cols),
                    in_specs=[vmem],
                    out_specs=[vmem],
                    out_shape=[q_all_shape],
                    scratch_shapes=[dma((2, 13))],
                    compiler_params=pltpu.CompilerParams(collective_id=1 + layers + layer, has_side_effects=True, vmem_limit_bytes=16 * 2**20),
                    cost_estimate=pl.CostEstimate(flops=5 * 10**9, bytes_accessed=2**22, transcendentals=0),
                    name='query_gather',
                )(q)
            kv_rows.append(lax.all_gather(kv, 'kv'))
            o, ml = attend(layer, q_all, pages_y)
            nxt = packed[layer + 1] if layer + 1 < layers else None
            attn, *more = exchange(layer, o, ml, q, kv, nxt)
            pages_y = more[0] if more else None
            hidden = (hidden.astype(F32) + jnp.dot(attn, w_out[layer], preferred_element_type=F32)).astype(BF16)
            up_act = jax.nn.gelu(jnp.dot(hidden, w_up[layer], preferred_element_type=F32)).astype(BF16)
            hidden = (hidden.astype(F32) + jnp.dot(up_act, w_down[layer], preferred_element_type=F32)).astype(BF16)
        for layer in range(layers):
            k_out, v_out = place(layer, kv_rows[layer], k_out, v_out)
        y_out = hidden.reshape(steps, seq_dev, width)
        back = (4, 0, 1, 2, 3)
        return y_out, jnp.transpose(k_out, back), jnp.transpose(v_out, back)

    return jax.shard_map(per_device, mesh=mesh, in_specs=(seq_spec, full_spec, full_spec, full_spec, full_spec, full_spec, full_spec, pool_spec, pool_spec, table_spec, vec_spec, vec_spec, vec_spec), out_specs=(seq_spec, pool_spec, pool_spec), check_vma=False)
```

time: 455 us -> 369 us (0.81); the launches traced: 454 us -> 363 us
  blocking collectives: 176 us -> 0 us
  Pallas kernels: 119 us -> 247 us
  waiting for transfers between devices: 49.2 us -> 0.26 us
  local copies, waits for them, and re-layouts: 12.9 us -> 27.6 us
  matrix products: 76.2 us -> 69.8 us
    pallas_call x5 -> x9, Pallas kernels: 107 us -> 235 us  [the longest x2 71.3 us: exchange(): pl.pallas_call(functools.partial(_exchange_kernel, n_cols, n_rows, heads,...]
    all_to_all x4 -> x0, blocking collectives: 125 us -> none  [the longest x2 106 us: per_device(): part = lax.all_to_all(part, 'kv', 0, 0, tiled=True)]
    unnamed x1 -> x0, blocking collectives: 51 us -> none
    all_gather x4, waiting for transfers between devices: 49 us -> 0.01 us  [the longest x2 0.01 us: per_device(): kv_rows.append(lax.all_gather(kv, 'kv'))]
    unnamed x35 -> x75, local copies, waits for them, and re-layouts: 8.28 us -> 22.4 us
    dot_general x2, matrix products: 9.92 us -> 3.18 us  [per_device(): jnp.dot(attn, w_out[layer], preferred_element_type=F32)]
  transfers between devices with their start and end apart: 4 -> 4, of which waited for: 2 -> 0; matrix products, arithmetic and copies ran while one was open for 10% -> 20% of each run, Pallas kernels for 15% -> 62%
where the time goes in v2:
time: 369 us; the launch traced here: 363 us
  Pallas kernels  247 us (67%)
  matrix products  69.8 us (19%)
  local copies, waits for them, and re-layouts  27.6 us (7%)
  between operations  14.5 us (4%)
    pallas_call x2, Pallas kernels, exchange(): pl.pallas_call(functools.partial(_exchange_kernel, n_cols, n_rows, heads,...  71.3 us
    pallas_call x2, Pallas kernels, attend(): pl.pallas_call(functools.partial(_attn_kernel, steps, group, pair), grid=...  68.2 us
    dot_general x2, matrix products, per_device(): jnp.dot(up_act, w_down[layer], preferred_element_type=F32)  48 us
    pallas_call x2, Pallas kernels, place(): pl.pallas_call(functools.partial(_place_kernel, steps, pair, len(aliases)...  41.6 us
    pallas_call x1, Pallas kernels, per_device(): pl.pallas_call(functools.partial(_head_kernel, n_rows, n_cols), in_specs=...  31 us
    unnamed x75, local copies, waits for them, and re-layouts  22.4 us
    pallas_call x1, Pallas kernels, per_device(): pl.pallas_call(functools.partial(_query_kernel, n_cols), in_specs=[vmem],...  19 us
    pallas_call x2, Pallas kernels, pack(): pl.pallas_call(functools.partial(_pack_kernel, pair), grid=(n_grid,), in_...  12.3 us
  transfers between devices with their start and end apart: 4, of which 0 were waited for; matrix products, arithmetic and copies ran while one was open for 20% of the time, Pallas kernels for 62%

profile of v2, /device:TPU:97, one launch (start us, length us, event | category | flops | bytes accessed | tf_op | source)
XLA Modules:
  0.0 362.9 jit_solution(10889829185310986483)
XLA Ops:
  7.2 0.0 copy-start.22
  7.2 0.1 all-gather.13.cloned.1.call-start
  7.3 2.2 fusion.93
  9.4 2.2 fusion.90
  11.6 0.7 pad_maximum_fusion.refs_3_
  12.3 0.1 all-gather.13.cloned.1.call-update
  12.3 0.1 all-gather.15.cloned.1.call-start
  12.4 0.7 fusion.112.onehot_ref
  13.1 6.1 %pack_pages.2.pages_ref = bf16[2,16,8192]{2,1,0:T(8,128)(2,1)} custom-call(bf16[16,208]{1,0:T(8,128)(2,1)} %fusion.112.onehot_ref, bf16[2,16,8,64,208]{4,3,2,1,0:T(8,128)(2,1)} %bitcast.110, bf16[2,16,8,64,208]{4,3,2,1,0:T(8,128)(2,1)} %bitcast.118), custom_call_target="tpu_custom_call" | custom-call | flops 4000000000 | bytes 8388608 | tf_op jit(solution)/shard_map/pack_pages/pallas_call | solution.py:575
  19.2 0.1 all-gather.15.cloned.1.call-update
  19.2 0.1 all-gather.9.cloned.1.call-start
  19.3 0.1 reshape.56
  19.4 0.1 pad_add_fusion
  19.5 5.0 %fusion.48.q_ref.refs_2_ = bf16[64,2048]{1,0:T(8,128)(2,1)S(1)} fusion(bf16[64,2048]{1,0:T(8,128)(2,1)S(1)} %bitcast.147, bf16[2,2048,2048]{2,1,0:T(8,128)(2,1)} %param.14), kind=kOutput, calls=%fused_computation.34 | convolution fusion | flops 537001984 | bytes 8912896 | tf_op jit(solution)/shard_map/dot_general | solution.py:589
  24.5 31.0 %head_gather.1 = (s32[32,8,128]{2,1,0:T(8,128)S(1)}, bf16[4,2,16,8192]{3,2,1,0:T(8,128)(2,1)S(1)}, bf16[8,64,2048]{2,1,0:T(8,128)(2,1)S(1)}) custom-call(s32[8,128]{1,0:T(8,128)S(1)} %pad_bitcast_fusion.meta_ref, bf16[2,16,8192]{2,1,0:T(8,128)(2,1)S(1)} %copy-done.5, bf16[64,2048]{1,0:T(8,128)(2,1)S(1)} %fusion.48.q_ref.refs_2_), custom_call_target="tpu_custom_call" | custom-call | flops 10000000000 | bytes 4194304 | tf_op jit(solution)/shard_map/head_gather/pallas_call | solution.py:600
  55.5 0.0 copy-start.20
  55.5 1.3 copy-done.20
  56.9 0.1 fusion.121
  57.0 0.7 reshape.63.dstr_ref
  57.6 0.9 reshape_reshape.4.dstc_ref
  58.5 0.1 reshape.60
  58.6 1.2 reshape.77.old_ref
  59.8 0.7 reshape.62.src_ref
  60.4 0.1 dynamic-slice.1
  60.5 0.8 reshape.78.len_ref
  61.3 0.7 copy.29.mysrcc_ref
  62.0 0.6 pad_add_fusion.1.pos_ref
  62.6 3.8 %prep_tables.1 = (bf16[256,256]{1,0:T(8,128)(2,1)}, bf16[768,256]{1,0:T(8,128)(2,1)}, bf16[64,256]{1,0:T(8,128)(2,1)}, f32[8,256]{1,0:T(8,128)}, bf16[256,208]{1...) custom-call(s32[768,1]{1,0:T(8,128)} %reshape.77.old_ref, s32[1,512]{1,0:T(1,128)} %reshape.62.src_ref, ...), custom_call_target="tpu_custom_call" | custom-call | tf_op jit(solution)/shard_map/prep_tables/pallas_call | solution.py:621
  66.4 6.2 %pack_pages.3.refs_4_ = bf16[2,16,8192]{2,1,0:T(8,128)(2,1)} custom-call(bf16[16,208]{1,0:T(8,128)(2,1)} %fusion.112.onehot_ref, bf16[2,16,8,64,208]{4,3,2,1,0:T(8,128)(2,1)} %bitcast.111, bf16[2,16,8,64,208]{4,3,2,1,0:T(8,128)(2,1)} %bitcast.119), custom_call_target="tpu_custom_call" | custom-call | flops 4000000000 | bytes 8388608 | tf_op jit(solution)/shard_map/pack_pages/pallas_call | solution.py:575
  72.7 0.0 copy-start
  72.7 3.4 copy-done
  76.1 1.6 copy-done.21
  77.7 0.0 slice-start.3
  77.7 0.0 slice-start.4
  77.7 34.1 %slot_attention.2 = (f32[2,4,2,32,2048]{4,3,2,1,0:T(8,128)S(1)}, f32[2,4,2,32,128]{4,3,2,1,0:T(8,128)S(1)}) custom-call(bf16[8,2,32,2048]{3,2,1,0:T(8,128)(2,1)S(1)} %bitcast.129, bf16[2,16,8,64,208]{4,3,2,1,0:T(8,128)(2,1)S(1)} %bitcast.112, bf16[2,16,8,64,208]{4,3,2,1,0:T(8,128)(2,1)} %bitcast.120, bf16[4,2,16,8192]{3,2,1,0:T(8,128)(2,1)S(1)} %copy-done.21, ...), custom_call_target="tpu_custom_call" | custom-call | flops 20000000000 | bytes 16777216 | tf_op jit(solution)/shard_map/slot_attention/pallas_call | solution.py:640
  111.9 0.0 slice-start.5
  111.9 27.0 %exchange_partials.2 = (bf16[64,2048]{1,0:T(8,128)(2,1)S(1)}, bf16[4,2,16,8192]{3,2,1,0:T(8,128)(2,1)S(1)}) custom-call(f32[2,4,2,32,2048]{4,3,2,1,0:T(8,128)S(1)} %get-tuple-element.30.refs_0_, f32[2,4,2,32,128]{4,3,2,1,0:T(8,128)S(1)} %get-tuple-element.31.refs_1_, bf16[64,2048]{1,0:T(8,128)(2,1)S(1)} %copy-done.19, bf16[64,1024]{1,0:T(8,128)(2,1)S(1)} %copy-done.7, ...), custom_call_target="tpu_custom_call" | custom-call | flops 10000000000 | bytes 4194304 | tf_op jit(solution)/shard_map/exchange_partials/pallas_call | solution.py:677
  139.0 1.6 fusion.45
  140.6 23.6 %fusion.39 = bf16[64,2048]{1,0:T(8,128)(2,1)S(1)} fusion(bf16[2,8192,2048]{2,1,0:T(8,128)(2,1)} %param.19, bf16[64,2048]{1,0:T(8,128)(2,1)S(1)} %fusion.45, bf16[2,2048,8192]{2,1,0:T(8,128)(2,1)} %param.18), kind=kOutput, calls=%fused_computation.31 | convolution fusion | flops 4300079104 | bytes 67895296 | tf_op jit(solution)/shard_map/dot_general | solution.py:748
  164.2 2.1 fusion.99
  166.2 2.1 fusion.96
  168.3 0.7 pad_maximum_fusion.1.refs_3_
  169.0 0.1 all-gather.9.cloned.1.call-update
  169.0 0.5 all-gather.11.cloned.1.call-start
  169.6 0.1 all-gather.11.cloned.1.call-update
  169.7 0.0 slice-start
  169.7 5.1 %fusion.51.q_ref.refs_2_ = bf16[64,2048]{1,0:T(8,128)(2,1)S(1)} fusion(bf16[64,2048]{1,0:T(8,128)(2,1)S(1)} %fusion.39, bf16[2,2048,2048]{2,1,0:T(8,128)(2,1)} %param.14), kind=kOutput, calls=%fused_computation.35 | convolution fusion | flops 537001984 | bytes 8912896 | tf_op jit(solution)/shard_map/dot_general | solution.py:589
  174.8 0.0 slice-start.1
  174.8 19.0 %query_gather.1 = bf16[8,64,2048]{2,1,0:T(8,128)(2,1)S(1)} custom-call(bf16[64,2048]{1,0:T(8,128)(2,1)S(1)} %fusion.51.q_ref.refs_2_), custom_call_target="tpu_custom_call" | custom-call | flops 5000000000 | bytes 4194304 | tf_op jit(solution)/shard_map/query_gather/pallas_call | solution.py:731
  193.9 0.0 slice-start.6
  194.0 34.1 %slot_attention.3 = (f32[2,4,2,32,2048]{4,3,2,1,0:T(8,128)S(1)}, f32[2,4,2,32,128]{4,3,2,1,0:T(8,128)S(1)}) custom-call(bf16[8,2,32,2048]{3,2,1,0:T(8,128)(2,1)S(1)} %bitcast.130, bf16[2,16,8,64,208]{4,3,2,1,0:T(8,128)(2,1)S(1)} %bitcast.115, bf16[2,16,8,64,208]{4,3,2,1,0:T(8,128)(2,1)} %bitcast.121, ...), custom_call_target="tpu_custom_call" | custom-call | flops 20000000000 | bytes 16777216 | tf_op jit(solution)/shard_map/slot_attention/pallas_call | solution.py:640
  228.1 0.0 slice-start.9
  228.1 44.3 %exchange_partials.3 = bf16[64,2048]{1,0:T(8,128)(2,1)S(1)} custom-call(f32[2,4,2,32,2048]{4,3,2,1,0:T(8,128)S(1)} %get-tuple-element.34.refs_0_, f32[2,4,2,32,128]{4,3,2,1,0:T(8,128)S(1)} %get-tuple-element.35.refs_1_, bf16[64,2048]{1,0:T(8,128)(2,1)S(1)} %fusion.51.q_ref.refs_2_, bf16[64,1024]{1,0:T(8,128)(2,1)S(1)} %copy-done.8), custom_call_target="tpu_custom_call" | custom-call | flops 10000000000 | bytes 4194304 | tf_op jit(solution)/shard_map/exchange_partials/pallas_call | solution.py:677
  272.5 1.6 fusion.42
  274.1 24.4 %fusion.36 = bf16[64,2048]{1,0:T(8,128)(2,1)} fusion(bf16[2,8192,2048]{2,1,0:T(8,128)(2,1)} %param.19, bf16[64,2048]{1,0:T(8,128)(2,1)S(1)} %fusion.42, bf16[2,2048,8192]{2,1,0:T(8,128)(2,1)} %param.18), kind=kOutput, calls=%fused_computation.30 | convolution fusion | flops 4300079104 | bytes 67895296 | tf_op jit(solution)/shard_map/dot_general | solution.py:748
  298.5 0.0 copy-start.1
  298.6 3.4 copy-done.1
  301.9 3.4 copy-done.3
  305.3 1.2 copy-done.9
  306.5 20.9 %place_pages.2 = (bf16[2,16,8,64,208]{4,3,2,1,0:T(8,128)(2,1)}, bf16[2,16,8,64,208]{4,3,2,1,0:T(8,128)(2,1)}) custom-call(bf16[8,2,32,1024]{3,2,1,0:T(8,128)(2,1)S(1)} %bitcast.125, bf16[8,2,32,1024]{3,2,1,0:T(8,128)(2,1)S(1)} %bitcast.126, bf16[2,16,8,64,208]{4,3,2,1,0:T(8,128)(2,1)S(1)} %bitcast.116, bf16[2,16,8,64,208]{4,3,2,1,0:T(8,128)(2,1)S(1)} %bitcast.122, ...), custom_call_target="tpu_custom_call" | custom-call | flops 20000000000 | bytes 33554432 | tf_op jit(solution)/shard_map/place_pages/pallas_call | solution.py:713
  327.4 3.4 copy-done.2
  330.8 3.4 copy-done.4
  334.2 1.2 copy-done.10
  335.4 20.7 %place_pages.3 = (bf16[2,16,8,64,208]{4,3,2,1,0:T(8,128)(2,1)}, bf16[2,16,8,64,208]{4,3,2,1,0:T(8,128)(2,1)}) custom-call(bf16[8,2,32,1024]{3,2,1,0:T(8,128)(2,1)S(1)} %bitcast.127, bf16[8,2,32,1024]{3,2,1,0:T(8,128)(2,1)S(1)} %bitcast.128, bf16[2,16,8,64,208]{4,3,2,1,0:T(8,128)(2,1)S(1)} %bitcast.117, ...), custom_call_target="tpu_custom_call", output_to_operand_aliasing={{0}: (9, {}), {1}: (10, {})} | custom-call | flops 20000000000 | bytes 33554432 | tf_op jit(solution)/shard_map/place_pages/pallas_call | solution.py:713
  (67 shorter events, 0.2 us)
Async XLA Ops:
  7.2 5.2 %copy-start.22 = (s32[16]{0:T(128)S(1)}, s32[16]{0:T(128)}, u32[]{:S(2)}) copy-start(s32[16]{0:T(128)} %param.24) | copy-start | bytes 196
  7.2 291.3 %all-gather.13.cloned.1.call-start = ((), (), s32[]{:S(2)}) async-start(), calls=%async_computation.2 | async-start | bytes 1179648 | tf_op jit(solution)/shard_map/all_gather | solution.py:741
  12.3 286.2 %all-gather.15.cloned.1.call-start = ((), (), s32[]{:S(2)}) async-start(), calls=%async_computation.3 | async-start | bytes 17301504 | tf_op jit(solution)/shard_map/all_gather | solution.py:586
  13.1 6.2 %copy-start.23 = (s32[32,3]{0,1:T(4,128)S(1)}, s32[32,3]{0,1:T(4,128)}, u32[]{:S(2)}) copy-start(s32[32,3]{0,1:T(4,128)} %param.22) | copy-start | bytes 1156
  13.1 6.3 %copy-start.24 = (s32[16]{0:T(128)S(1)}, s32[16]{0:T(128)}, u32[]{:S(2)}) copy-start(s32[16]{0:T(128)} %param.25) | copy-start | bytes 196
  13.1 6.3 %copy-start.25 = (s32[32]{0:T(128)S(1)}, s32[32]{0:T(128)}, u32[]{:S(2)}) copy-start(s32[32]{0:T(128)} %param.23) | copy-start | bytes 388
  13.1 6.4 %copy-start.26 = (bf16[2,32,2048]{2,1,0:T(8,128)(2,1)S(1)}, bf16[2,32,2048]{2,1,0:T(8,128)(2,1)}, u32[]{:S(2)}) copy-start(bf16[2,32,2048]{2,1,0:T(8,128)(2,1)} %param.13) | copy-start | bytes 786436
  19.2 308.2 %all-gather.9.cloned.1.call-start = ((), (), s32[]{:S(2)}) async-start(), calls=%async_computation | async-start | bytes 1179648 | tf_op jit(solution)/shard_map/all_gather | solution.py:741
  19.5 5.0 %copy-start.5 = (bf16[2,16,8192]{2,1,0:T(8,128)(2,1)S(1)}, bf16[2,16,8192]{2,1,0:T(8,128)(2,1)}, u32[]{:S(2)}) copy-start(bf16[2,16,8192]{2,1,0:T(8,128)(2,1)} %pack_pages.2.pages_ref) | copy-start | bytes 1572868
  24.5 31.0 %copy-start.18 = (bf16[64,2048]{1,0:T(8,128)(2,1)}, bf16[64,2048]{1,0:T(8,128)(2,1)S(1)}, u32[]{:S(2)}) copy-start(bf16[64,2048]{1,0:T(8,128)(2,1)S(1)} %fusion.48.q_ref.refs_2_) | copy-start | bytes 786436
  55.5 1.3 copy-start.20
  66.4 6.3 %copy-start.11 = (bf16[768,256]{1,0:T(8,128)(2,1)S(1)}, bf16[768,256]{1,0:T(8,128)(2,1)}, u32[]{:S(2)}) copy-start(bf16[768,256]{1,0:T(8,128)(2,1)} %get-tuple-element.27.cell_ref) | copy-start | bytes 1179652
  66.4 6.3 %copy-start.14 = (bf16[256,256]{1,0:T(8,128)(2,1)S(1)}, bf16[256,256]{1,0:T(8,128)(2,1)}, u32[]{:S(2)}) copy-start(bf16[256,256]{1,0:T(8,128)(2,1)} %get-tuple-element.26.qsel_ref) | copy-start | bytes 393220
  66.4 6.3 %copy-start.15 = (bf16[64,256]{1,0:T(8,128)(2,1)S(1)}, bf16[64,256]{1,0:T(8,128)(2,1)}, u32[]{:S(2)}) copy-start(bf16[64,256]{1,0:T(8,128)(2,1)} %get-tuple-element.28.arr_ref) | copy-start | bytes 98308
  66.4 6.3 %copy-start.17 = (f32[8,256]{1,0:T(8,128)S(1)}, f32[8,256]{1,0:T(8,128)}, u32[]{:S(2)}) copy-start(f32[8,256]{1,0:T(8,128)} %get-tuple-element.29.info_ref) | copy-start | bytes 24580
  72.7 3.4 copy-start
  76.1 1.6 copy-start.21
  77.7 34.1 %copy-start.6 = (bf16[2,16,8192]{2,1,0:T(8,128)(2,1)S(1)}, bf16[2,16,8192]{2,1,0:T(8,128)(2,1)}, u32[]{:S(2)}) copy-start(bf16[2,16,8192]{2,1,0:T(8,128)(2,1)} %pack_pages.3.refs_4_) | copy-start | bytes 1572868
  77.7 34.2 %copy-start.7 = (bf16[64,1024]{1,0:T(8,128)(2,1)S(1)}, bf16[64,1024]{1,0:T(8,128)(2,1)}, u32[]{:S(2)}) copy-start(bf16[64,1024]{1,0:T(8,128)(2,1)} %pad_maximum_fusion.refs_3_) | copy-start | bytes 393220
  77.7 34.2 %copy-start.19 = (bf16[64,2048]{1,0:T(8,128)(2,1)S(1)}, bf16[64,2048]{1,0:T(8,128)(2,1)}, u32[]{:S(2)}) copy-start(bf16[64,2048]{1,0:T(8,128)(2,1)} %copy-done.18) | copy-start | bytes 786436
  77.7 61.2 %slice-start.2 = ((s8[16777216]{0:T(1024)(128)(4,1)}), s8[4194304]{0:T(1024)(128)(4,1)S(1)}, s32[]{:S(2)}) async-start(s8[16777216]{0:T(1024)(128)(4,1)} %bitcast.137), calls=%async_computation.6 | async-start | bytes 8388608
  77.7 61.2 %slice-start.3 = ((s8[16777216]{0:T(1024)(128)(4,1)}), s8[4194304]{0:T(1024)(128)(4,1)S(1)}, s32[]{:S(2)}) async-start(s8[16777216]{0:T(1024)(128)(4,1)} %bitcast.137), calls=%async_computation.7 | async-start | bytes 8388608
  77.7 61.2 %slice-start.4 = ((s8[16777216]{0:T(1024)(128)(4,1)}), s8[4194304]{0:T(1024)(128)(4,1)S(1)}, s32[]{:S(2)}) async-start(s8[16777216]{0:T(1024)(128)(4,1)} %bitcast.137), calls=%async_computation.8 | async-start | bytes 8388608
  111.9 27.1 %slice-start.5 = ((s8[16777216]{0:T(1024)(128)(4,1)}), s8[4194304]{0:T(1024)(128)(4,1)S(1)}, s32[]{:S(2)}) async-start(s8[16777216]{0:T(1024)(128)(4,1)} %bitcast.137), calls=%async_computation.9 | async-start | bytes 8388608
  169.0 158.4 %all-gather.11.cloned.1.call-start = ((), (), s32[]{:S(2)}) async-start(), calls=%async_computation.1 | async-start | bytes 17301504 | tf_op jit(solution)/shard_map/all_gather | solution.py:586
  169.7 24.2 %slice-start = ((s8[8388608]{0:T(1024)(128)(4,1)}), s8[4194304]{0:T(1024)(128)(4,1)S(1)}, s32[]{:S(2)}) async-start(s8[8388608]{0:T(1024)(128)(4,1)} %bitcast.113), calls=%async_computation.4 | async-start | bytes 8388608
  174.8 19.1 %slice-start.1 = ((s8[8388608]{0:T(1024)(128)(4,1)}), s8[4194304]{0:T(1024)(128)(4,1)S(1)}, s32[]{:S(2)}) async-start(s8[8388608]{0:T(1024)(128)(4,1)} %bitcast.113), calls=%async_computation.5 | async-start | bytes 8388608
  193.9 34.2 %copy-start.8 = (bf16[64,1024]{1,0:T(8,128)(2,1)S(1)}, bf16[64,1024]{1,0:T(8,128)(2,1)}, u32[]{:S(2)}) copy-start(bf16[64,1024]{1,0:T(8,128)(2,1)} %pad_maximum_fusion.1.refs_3_) | copy-start | bytes 393220
  193.9 78.5 %slice-start.6 = ((s8[16777216]{0:T(1024)(128)(4,1)}), s8[4194304]{0:T(1024)(128)(4,1)S(1)}, s32[]{:S(2)}) async-start(s8[16777216]{0:T(1024)(128)(4,1)} %bitcast.139), calls=%async_computation.10 | async-start | bytes 8388608
  193.9 78.5 %slice-start.7 = ((s8[16777216]{0:T(1024)(128)(4,1)}), s8[4194304]{0:T(1024)(128)(4,1)S(1)}, s32[]{:S(2)}) async-start(s8[16777216]{0:T(1024)(128)(4,1)} %bitcast.139), calls=%async_computation.11 | async-start | bytes 8388608
  193.9 78.5 %slice-start.8 = ((s8[16777216]{0:T(1024)(128)(4,1)}), s8[4194304]{0:T(1024)(128)(4,1)S(1)}, s32[]{:S(2)}) async-start(s8[16777216]{0:T(1024)(128)(4,1)} %bitcast.139), calls=%async_computation.12 | async-start | bytes 8388608
  228.1 44.4 %slice-start.9 = ((s8[16777216]{0:T(1024)(128)(4,1)}), s8[4194304]{0:T(1024)(128)(4,1)S(1)}, s32[]{:S(2)}) async-start(s8[16777216]{0:T(1024)(128)(4,1)} %bitcast.139), calls=%async_computation.13 | async-start | bytes 8388608
  274.1 24.4 %copy-start.12 = (bf16[512,208]{1,0:T(8,128)(2,1)S(1)}, bf16[512,208]{1,0:T(8,128)(2,1)}, u32[]{:S(2)}) copy-start(bf16[512,208]{1,0:T(8,128)(2,1)} %get-tuple-element.37.refs_7_) | copy-start | bytes 638980
  274.1 24.4 %copy-start.13 = (bf16[256,208]{1,0:T(8,128)(2,1)S(1)}, bf16[256,208]{1,0:T(8,128)(2,1)}, u32[]{:S(2)}) copy-start(bf16[256,208]{1,0:T(8,128)(2,1)} %get-tuple-element.36.refs_6_) | copy-start | bytes 319492
  274.1 24.4 %copy-start.16 = (f32[8,208]{1,0:T(8,128)S(1)}, f32[8,208]{1,0:T(8,128)}, u32[]{:S(2)}) copy-start(f32[8,208]{1,0:T(8,128)} %get-tuple-element.38.refs_8_) | copy-start | bytes 19972
  298.5 3.4 copy-start.1
  301.9 3.4 copy-start.3
  305.3 1.2 copy-start.9
  327.4 3.4 copy-start.2
  330.8 3.4 copy-start.4
  334.2 1.2 copy-start.10
Sparse Core Ops, SparseCore 0:
  12.4 26.2 all-gather.12
  41.4 66.9 all-gather.14
  169.2 22.9 all-gather.8
  194.1 84.7 all-gather.10

commit v3 on v2

--- a/solution.py
+++ b/solution.py
@@ -16,7 +16,12 @@
 TN = (((0,), (0,)), ((), ()))
 MESH = pl.DeviceIdType.MESH
 LANES = 256
+MIB = 2**20
 I0, I1, I2, I3, I4, I5 = range(6)
+
+
+def _cost(gflops, mib):
+    return pl.CostEstimate(flops=gflops * 10**9, bytes_accessed=mib * MIB, transcendentals=0)
 
 
 def _dot(a, b, dims):
@@ -41,20 +46,42 @@
     return _dot(sel, hi, dims) + _dot(sel, mid, dims) + _dot(sel, low, dims)
 
 
-def _prep_kernel(n_pages, page, n_cols, n_slots, old_ref, src_ref, dstr_ref, dstc_ref, len_ref, mysrc_ref, mysrcc_ref, pos_ref, qsel_ref, cell_ref, arr_ref, info_ref, wsel_ref, mig_ref, winfo_ref):
-    base = pos_ref[0]
-    my_col = pos_ref[1]
-    n_seq = len_ref.shape[0]
-    n_all = src_ref.shape[1]
+def _columns(rows):
+    full = jnp.concatenate([rows, jnp.zeros((LANES // 2 - rows.shape[0], rows.shape[1]), F32)], axis=0).T
+    ids = lax.broadcasted_iota(I32, full.shape, 1)
+
+    def column(i):
+        return jnp.sum(jnp.where(ids == i, full, 0.0), axis=1, keepdims=True).astype(I32)
+
+    return column
+
+
+def _tables(dims, meta_all, mysrc_ref, mysrcc_ref, qsel_ref, cell_ref, arr_ref, info_ref, wsel_ref, mig_ref, winfo_ref):
+    n_rows, n_cols, n_slots, n_pages, page, seq_dev = dims
+    y, my_col = lax.axis_index('kv2'), lax.axis_index('kv')
+    base = (y * n_cols + my_col) * n_slots
+    n_seq = n_cols * seq_dev
     n_move = mysrc_ref.shape[1]
     n_arr = arr_ref.shape[0]
     spare = LANES - n_slots
-    old = old_ref[...]
-    hit = old == src_ref[...]
-    entry = jnp.sum(jnp.where(hit, lax.broadcasted_iota(I32, (1, n_all), 1) + 1, 0).astype(F32), axis=1, keepdims=True).astype(I32)
-    dst = jnp.sum(jnp.where(hit, dstr_ref[...] + 1, 0).astype(F32), axis=1, keepdims=True).astype(I32) - 1
-    is_moved = entry > 0
-    entry = entry - 1
+    src = jnp.sum(meta_all[:, 8:16, :], axis=0)
+    dst = jnp.sum(meta_all[:, 16:24, :], axis=0)
+    tab = jnp.concatenate([meta_all[y * n_cols + i, 0:1, :] for i in range(n_cols)], axis=0).astype(F32)
+    column = _columns(tab)
+    tabs = [column(i) for i in range(n_cols)]
+    old = jnp.concatenate([c[j * seq_dev:(j + 1) * seq_dev] for j in range(n_pages) for c in tabs], axis=0)
+    lens = jnp.concatenate([c[n_pages * seq_dev:] for c in tabs], axis=0)
+    per_row = n_cols * n_move
+    ids = lax.broadcasted_iota(I32, (1, per_row), 1)
+    entry = jnp.zeros(old.shape, F32)
+    to = jnp.zeros(old.shape, F32)
+    for r in range(n_rows):
+        hit = old == src[r:r + 1]
+        entry = entry + jnp.sum(jnp.where(hit, ids + (r * per_row + 1), 0).astype(F32), axis=1, keepdims=True)
+        to = to + jnp.sum(jnp.where(hit, dst[r:r + 1] + 1, 0).astype(F32), axis=1, keepdims=True)
+    entry = entry.astype(I32) - 1
+    to = to.astype(I32) - 1
+    is_moved = entry >= 0
     dev = entry // n_move
     nth = entry - dev * n_move
     arrival = (dev // n_cols) * n_move + nth
@@ -63,10 +90,9 @@
     here = old - base
     here = jnp.where((here >= 0) & (here < n_slots), here, -1)
     lane = jnp.where(is_moved, jnp.where(dev % n_cols == my_col, arr_lane, -1), here)
-    final = jnp.where(is_moved, dst, old) - base
+    final = jnp.where(is_moved, to, old) - base
     lane_ids = lax.broadcasted_iota(I32, (1, LANES), 1)
     slot_ids = lax.broadcasted_iota(I32, (1, n_slots), 1)
-    lens = len_ref[...]
     last = lens // page
     q_sel = jnp.zeros((n_seq, LANES), F32)
     w_sel = jnp.zeros((n_seq, n_slots), F32)
@@ -82,23 +108,23 @@
     used = jnp.sum(q_sel, axis=0, keepdims=True)
     slot_len = jnp.sum(q_sel * lens.astype(F32), axis=0, keepdims=True)
     arr_ids = lax.broadcasted_iota(I32, (n_arr, LANES), 0)
-    at_spare = jnp.where(lane_ids == n_slots + arr_ids, 1.0, 0.0)
-    arr_ref[...] = at_spare.astype(BF16)
+    arr_ref[...] = jnp.where(lane_ids == n_slots + arr_ids, 1.0, 0.0).astype(BF16)
     mine = mysrcc_ref[...] - base
-    for k in range(n_arr - spare):
-        arr_ref[spare + k:spare + k + 1, :] = jnp.where(lane_ids == mine[k:k + 1], 1.0, 0.0).astype(BF16)
+    arr_ref[spare:n_arr, :] = jnp.where(lane_ids == mine, 1.0, 0.0).astype(BF16)
     out_lanes = jnp.sum(jnp.where(mine == lane_ids, 1.0, 0.0), axis=0, keepdims=True)
+    info_ref[...] = jnp.zeros_like(info_ref)
     info_ref[0:1, :] = used
     info_ref[1:2, :] = jnp.where(used > 0, slot_len - first - 1.0, -100.0)
     info_ref[2:3, :] = jnp.where(lane_ids >= n_slots, 1.0, out_lanes)
-    info_ref[3:8, :] = jnp.zeros((5, LANES), F32)
     written = jnp.sum(w_sel, axis=0, keepdims=True)
     w_off = jnp.sum(w_sel * (lens - last * page).astype(F32), axis=0, keepdims=True)
-    mig = ((dstc_ref[...] - base) == slot_ids).astype(F32)
+    to_col = _columns(dst.astype(F32))
+    dst_col = jnp.concatenate([to_col(r) for r in range(n_rows)], axis=0)
+    mig = jnp.where(dst_col - base == slot_ids, 1.0, 0.0)
     mig_ref[...] = mig.astype(BF16)
+    winfo_ref[...] = jnp.zeros_like(winfo_ref)
     winfo_ref[0:1, :] = jnp.sum(mig, axis=0, keepdims=True)
     winfo_ref[1:2, :] = jnp.where(written > 0, w_off, -100.0)
-    winfo_ref[2:8, :] = jnp.zeros((6, n_slots), F32)
 
 
 def _pack_kernel(heads, onehot_ref, k_ref, v_ref, out_ref):
@@ -107,7 +133,7 @@
     for h in range(heads):
         for which, src in enumerate((k_ref, v_ref)):
             rows = src[0, :, h].reshape(width, n_slots)
-            out_ref[which, :, h * width:(h + 1) * width] = _dot(onehot_ref[...], rows, NT).astype(BF16)
+            out_ref[0, which, :, h * width:(h + 1) * width] = _dot(onehot_ref[...], rows, NT).astype(BF16)
 
 
 def _copy(src, dst, sems, k, dev):
@@ -232,7 +258,10 @@
     return ref.at[h]
 
 
-def _head_kernel(n_rows, n_cols, meta_ref, pages_ref, q_ref, meta_all, pages_all, q_all, m_sem, y_sem, x_sem):
+def _head_kernel(dims, meta_ref, pages_ref, q_ref, mysrc_ref, mysrcc_ref, pages_all, q_all, *refs):
+    tables, (meta_all, m_sem, y_sem, x_sem) = refs[:7], refs[7:]
+    n_rows, n_cols = dims[:2]
+    pages_ref = pages_ref.at[0]
     y, at = lax.axis_index('kv2'), lax.axis_index('kv')
     offsets = [(a, b) for a in range(n_rows) for b in range(n_cols) if (a, b) != (0, 0)]
     peers = [{'kv2': (y + a) % n_rows, 'kv': (at + b) % n_cols} for a, b in offsets]
@@ -249,13 +278,14 @@
     pages_all[y] = pages_ref[...]
     next(steps)
     forward()
+    for k, (a, b) in enumerate(offsets):
+        frm = ((y + n_rows - a) % n_rows) * n_cols + (at + n_cols - b) % n_cols
+        _copy(meta_ref, meta_all.at[frm], m_sem, k, peers[k]).wait_recv()
+    _tables(dims, meta_all, mysrc_ref, mysrcc_ref, *tables)
     next(steps)
     finish()
     for _ in steps:
         pass
-    for k, (a, b) in enumerate(offsets):
-        frm = ((y + n_rows - a) % n_rows) * n_cols + (at + n_cols - b) % n_cols
-        _copy(meta_ref, meta_all.at[frm], m_sem, k, peers[k]).wait_recv()
     for c in metas:
         c.wait_send()
 
@@ -387,7 +417,7 @@
     for c in pals:
         c.start()
     if has_pages:
-        pages_ref, pages_all = refs[I4], refs[n_in + I1]
+        pages_ref, pages_all = refs[I4].at[I1], refs[n_in + I1]
         y_start, y_forward, y_finish = _rows_on_y(pages_ref, pages_all, y_sem, _half0)
         y_start()
         pages_all[lax.axis_index('kv2')] = pages_ref[...]
@@ -501,31 +531,31 @@
         c.wait_send()
 
 
-def _place_kernel(steps, heads, n_alias, *refs):
-    kn_ref, vn_ref, k_ref, v_ref, mk_ref, mv_ref, wsel_ref, mig_ref, info_ref = refs[:9]
-    ko_ref, vo_ref, kv_s, full = refs[9 + n_alias:]
+def _place_kernel(steps, heads, kn_ref, vn_ref, k_ref, v_ref, mk_ref, mv_ref, wsel_ref, mig_ref, info_ref, ko_ref, vo_ref, kv_s, full):
     page, _, dim, n_slots = k_ref.shape[1:]
     n_seq = wsel_ref.shape[0]
     width = page * dim
     n_all = mig_ref.shape[0]
-    moved = info_ref[0:1, :] > 0
+    moved = info_ref[0:1, :]
     w_off = info_ref[1:2, :]
     for t in range(steps):
         for which, ref in enumerate((kn_ref, vn_ref)):
-            kv_s[which, t] = _dot(ref[:, t].reshape(n_seq, heads * dim), wsel_ref[...], TN)
+            kv_s[which, t] = _dot(ref[:, 0, t].reshape(n_seq, heads * dim), wsel_ref[...], TN).astype(BF16)
     for h in range(heads):
         for which, (pool, pages, out) in enumerate(((k_ref, mk_ref, ko_ref), (v_ref, mv_ref, vo_ref))):
-            full[...] = _dot(pages[:, 0, :, h * width:(h + 1) * width].reshape(n_all, width), mig_ref[...], TN).reshape(page, dim, n_slots)
+            full[...] = _dot(pages[:, 0, 0, :, h * width:(h + 1) * width].reshape(n_all, width), mig_ref[...], TN).astype(BF16).reshape(page, dim, n_slots)
 
             def fill(tok, _, which=which, pool=pool, out=out, h=h):
-                val = jnp.where(moved, full[tok], pool[0, tok, h].astype(F32))
                 at = w_off - tok.astype(F32)
+                new = [jnp.where(at == -float(t), 1.0, 0.0) for t in range(steps)]
+                kept = 1.0 - functools.reduce(jnp.add, new)
+                val = full[tok] * kept.astype(BF16) + pool[0, tok, h] * (kept * (1.0 - moved)).astype(BF16)
                 for t in range(steps):
-                    val = jnp.where(at == -float(t), kv_s[which, t, h * dim:(h + 1) * dim, :], val)
-                out[0, tok, h] = val.astype(BF16)
+                    val = val + kv_s[which, t, h * dim:(h + 1) * dim, :] * new[t].astype(BF16)
+                out[0, tok, h] = val
                 return 0
 
-            lax.fori_loop(0, page, fill, 0)
+            lax.fori_loop(0, page, fill, 0, unroll=2)
 
 
 def solution(mesh):
@@ -557,8 +587,7 @@
         rows = steps * seq_dev
         me = lax.axis_index('kv2') * n_cols + lax.axis_index('kv')
         slot_base = me * n_slots
-        k_t = jnp.transpose(k_pool, (1, 2, 3, 4, 0))
-        v_t = jnp.transpose(v_pool, (1, 2, 3, 4, 0))
+        k_t, v_t = (pltpu.with_memory_space_constraint(jnp.transpose(a, (1, 2, 3, 4, 0)), pltpu.HBM) for a in (k_pool, v_pool))
         q_w, kv_w, m_w = pair * group * dim, pair * dim, pair * page_w
 
         def fixed(shape):
@@ -570,20 +599,17 @@
         def pool_blk(layer):
             return pl.BlockSpec((1, page, pair, dim, n_slots), lambda i: (layer, 0, i, 0, 0))
 
-        def pack(layer):
-            blk = pool_blk(layer)
-            return pl.pallas_call(
-                functools.partial(_pack_kernel, pair),
-                grid=(n_grid,),
-                in_specs=[pl.BlockSpec((n_move, n_slots), lambda i: (0, 0)), blk, blk],
-                out_specs=pl.BlockSpec((2, n_move, m_w), lambda i: (0, 0, i)),
-                out_shape=jax.ShapeDtypeStruct(page_shape, BF16),
-                cost_estimate=pl.CostEstimate(flops=4 * 10**9, bytes_accessed=8 * 2**20, transcendentals=0),
-                name='pack_pages',
-            )(src_hot, k_t, v_t)
-
-        packed = [pack(layer) for layer in range(layers)]
-        moved = [lax.all_gather(p, group_axes) for p in packed]
+        both = pl.BlockSpec((1, page, pair, dim, n_slots), lambda l, i: (l, 0, i, 0, 0))
+        packed = pl.pallas_call(
+            functools.partial(_pack_kernel, pair),
+            grid=(layers, n_grid),
+            in_specs=[pl.BlockSpec((n_move, n_slots), lambda l, i: (0, 0)), both, both],
+            out_specs=pl.BlockSpec((1, 2, n_move, m_w), lambda l, i: (l, 0, 0, i)),
+            out_shape=jax.ShapeDtypeStruct((layers,) + page_shape, BF16),
+            cost_estimate=_cost(8, 16),
+            name='pack_pages',
+        )(src_hot, k_t, v_t)
+        moved = lax.all_gather(packed, group_axes)
 
         def project(hidden, layer):
             q = jnp.dot(hidden, w_query[layer], preferred_element_type=F32).astype(BF16)
@@ -592,37 +618,27 @@
 
         hidden = x_embed.reshape(rows, width)
         q, kv = project(hidden, 0)
-        meta = jnp.concatenate([old_table.T.reshape(-1), seq_len, src_slot, dst_slot])
-        n_meta = meta.shape[0]
-        meta = jnp.pad(meta, (0, 8 * 128 - n_meta)).reshape(8, 128)
+        y, at = lax.axis_index('kv2'), lax.axis_index('kv')
+        n_all = n_dev * n_move
+        n_arr = n_rows * n_move
+
+        def own_place(v):
+            wide = jnp.tile(v, n_cols)[None, :]
+            lane = jnp.arange(n_cols * n_move, dtype=I32)[None, :] // n_move
+            return jnp.where((lane == at) & (jnp.arange(8, dtype=I32)[:, None] == y), wide, 0)
+
+        tab = jnp.concatenate([old_table.T.reshape(-1), seq_len])[None, :]
+        meta = jnp.concatenate([jnp.where(jnp.arange(8, dtype=I32)[:, None] == 0, tab, 0), own_place(src_slot), own_place(dst_slot)], axis=0)
         pages_all_shape = jax.ShapeDtypeStruct((n_rows,) + page_shape, BF16)
         q_all_shape = jax.ShapeDtypeStruct((n_cols, rows, heads * dim), BF16)
-        meta_all, pages_y, q_all = pl.pallas_call(
-            functools.partial(_head_kernel, n_rows, n_cols),
-            in_specs=[vmem] * 3,
-            out_specs=[vmem] * 3,
-            out_shape=[jax.ShapeDtypeStruct((n_dev, 8, 128), I32), pages_all_shape, q_all_shape],
-            scratch_shapes=[dma((2, n_dev - 1)), dma((2, 6)), dma((2, 13))],
-            compiler_params=pltpu.CompilerParams(collective_id=0, has_side_effects=True, vmem_limit_bytes=24 * 2**20),
-            cost_estimate=pl.CostEstimate(flops=10**10, bytes_accessed=2**22, transcendentals=0),
-            name='head_gather',
-        )(meta, packed[0], q)
-
-        meta_all = meta_all.reshape(n_dev, 8 * 128)[:, :n_meta]
-        n_tab = n_pages * seq_dev
-        row = lax.dynamic_slice_in_dim(meta_all, lax.axis_index('kv2') * n_cols, n_cols, axis=0)
-        old_col = row[:, :n_tab].reshape(n_cols, n_pages, seq_dev).transpose(1, 0, 2).reshape(-1, 1)
-        len_col = row[:, n_tab:n_tab + seq_dev].reshape(-1, 1)
-        src_all = meta_all[:, n_tab + seq_dev:n_tab + seq_dev + n_move].reshape(1, -1)
-        dst_all = meta_all[:, n_tab + seq_dev + n_move:].reshape(1, -1)
-        n_all = n_dev * n_move
-        n_arr = n_rows * n_move
-        pos = jnp.stack([slot_base, lax.axis_index('kv')]).astype(I32)
-        q_sel, cells, arr, info, w_sel, mig, w_info = pl.pallas_call(
-            functools.partial(_prep_kernel, n_pages, page, n_cols, n_slots),
-            in_specs=[vmem] * 7 + [pl.BlockSpec(memory_space=pltpu.SMEM)],
-            out_specs=[vmem] * 7,
+        dims = (n_rows, n_cols, n_slots, n_pages, page, seq_dev)
+        pages_y, q_all, q_sel, cells, arr, info, w_sel, mig, w_info = pl.pallas_call(
+            functools.partial(_head_kernel, dims),
+            in_specs=[vmem] * 5,
+            out_specs=[vmem] * 9,
             out_shape=[
+                pages_all_shape,
+                q_all_shape,
                 jax.ShapeDtypeStruct((n_seq, LANES), BF16),
                 jax.ShapeDtypeStruct((n_pages * n_seq, LANES), BF16),
                 jax.ShapeDtypeStruct((n_arr, LANES), BF16),
@@ -631,8 +647,11 @@
                 jax.ShapeDtypeStruct((n_all, n_slots), BF16),
                 jax.ShapeDtypeStruct((8, n_slots), F32),
             ],
-            name='prep_tables',
-        )(old_col, src_all, dst_all, dst_all.reshape(-1, 1), len_col, src_slot.reshape(1, -1), src_slot.reshape(-1, 1), pos)
+            scratch_shapes=[pltpu.VMEM((n_dev,) + meta.shape, I32), dma((2, n_dev - 1)), dma((2, 6)), dma((2, 13))],
+            compiler_params=pltpu.CompilerParams(collective_id=0, has_side_effects=True, vmem_limit_bytes=24 * MIB),
+            cost_estimate=_cost(10, 4),
+            name='head_gather',
+        )(meta, packed, q, src_slot.reshape(1, -1), src_slot.reshape(-1, 1))
 
         def attend(layer, q_all, pages):
             blk = pool_blk(layer)
@@ -664,8 +683,8 @@
                     pltpu.VMEM((2 * n_rt, LANES), F32),
                     pltpu.VMEM((steps, ml_rows, n_seq), F32),
                 ],
-                compiler_params=pltpu.CompilerParams(vmem_limit_bytes=32 * 2**20),
-                cost_estimate=pl.CostEstimate(flops=20 * 10**9, bytes_accessed=16 * 2**20, transcendentals=0),
+                compiler_params=pltpu.CompilerParams(vmem_limit_bytes=32 * MIB),
+                cost_estimate=_cost(20, 16),
                 name='slot_attention',
             )(q_all.reshape(n_cols, steps, seq_dev, heads * dim), k_t, v_t, pages, pages, q_sel, cells, arr, info)
 
@@ -687,44 +706,12 @@
                     pltpu.VMEM((heads, heads * dim), BF16), pltpu.VMEM((kv_w, q_w), BF16),
                     dma((2, 8)), dma((2, 12)), dma((2, 6)),
                 ],
-                compiler_params=pltpu.CompilerParams(collective_id=1 + layer, has_side_effects=True, vmem_limit_bytes=32 * 2**20),
-                cost_estimate=pl.CostEstimate(flops=10**10, bytes_accessed=2**22, transcendentals=0),
+                compiler_params=pltpu.CompilerParams(collective_id=1 + layer, has_side_effects=True, vmem_limit_bytes=32 * MIB),
+                cost_estimate=_cost(10, 4),
                 name='exchange_partials',
             )(o, ml, q, kv, *([pages] if has else []))
 
-        def place(layer, kv_row, k_prev, v_prev):
-            blk = pool_blk(layer)
-            v_at = kv_heads * dim // kv_w
-            in_specs = [
-                pl.BlockSpec((n_cols, steps, seq_dev, kv_w), lambda i: (0, 0, 0, i)),
-                pl.BlockSpec((n_cols, steps, seq_dev, kv_w), lambda i: (0, 0, 0, v_at + i)),
-                blk, blk,
-                pl.BlockSpec((n_dev, 1, n_move, m_w), lambda i: (0, 0, 0, i)),
-                pl.BlockSpec((n_dev, 1, n_move, m_w), lambda i: (0, 1, 0, i)),
-                fixed(w_sel.shape), fixed(mig.shape), fixed(w_info.shape),
-            ]
-            kv4 = kv_row.reshape(n_cols, steps, seq_dev, -1)
-            args = [kv4, kv4, k_t, v_t, moved[layer], moved[layer], w_sel, mig, w_info]
-            aliases = {}
-            if k_prev is not None:
-                in_specs += [pl.BlockSpec(memory_space=pl.ANY)] * 2
-                aliases = {len(args): 0, len(args) + 1: 1}
-                args += [k_prev, v_prev]
-            return pl.pallas_call(
-                functools.partial(_place_kernel, steps, pair, len(aliases)),
-                grid=(n_grid,),
-                in_specs=in_specs,
-                out_specs=[blk, blk],
-                out_shape=[jax.ShapeDtypeStruct(k_t.shape, BF16), jax.ShapeDtypeStruct(v_t.shape, BF16)],
-                scratch_shapes=[pltpu.VMEM((2, steps, kv_w, n_slots), F32), pltpu.VMEM((page, dim, n_slots), F32)],
-                input_output_aliases=aliases,
-                compiler_params=pltpu.CompilerParams(vmem_limit_bytes=32 * 2**20),
-                cost_estimate=pl.CostEstimate(flops=20 * 10**9, bytes_accessed=32 * 2**20, transcendentals=0),
-                name='place_pages',
-            )(*args)
-
-        k_out = v_out = None
-        kv_rows = []
+        kv_all = []
         for layer in range(layers):
             if layer:
                 q, kv = project(hidden, layer)
@@ -734,20 +721,42 @@
                     out_specs=[vmem],
                     out_shape=[q_all_shape],
                     scratch_shapes=[dma((2, 13))],
-                    compiler_params=pltpu.CompilerParams(collective_id=1 + layers + layer, has_side_effects=True, vmem_limit_bytes=16 * 2**20),
-                    cost_estimate=pl.CostEstimate(flops=5 * 10**9, bytes_accessed=2**22, transcendentals=0),
+                    compiler_params=pltpu.CompilerParams(collective_id=1 + layers + layer, has_side_effects=True, vmem_limit_bytes=16 * MIB),
+                    cost_estimate=_cost(5, 4),
                     name='query_gather',
                 )(q)
-            kv_rows.append(lax.all_gather(kv, 'kv'))
+            kv_all.append(kv)
             o, ml = attend(layer, q_all, pages_y)
-            nxt = packed[layer + 1] if layer + 1 < layers else None
+            nxt = packed if layer + 1 < layers else None
             attn, *more = exchange(layer, o, ml, q, kv, nxt)
             pages_y = more[0] if more else None
             hidden = (hidden.astype(F32) + jnp.dot(attn, w_out[layer], preferred_element_type=F32)).astype(BF16)
             up_act = jax.nn.gelu(jnp.dot(hidden, w_up[layer], preferred_element_type=F32)).astype(BF16)
             hidden = (hidden.astype(F32) + jnp.dot(up_act, w_down[layer], preferred_element_type=F32)).astype(BF16)
-        for layer in range(layers):
-            k_out, v_out = place(layer, kv_rows[layer], k_out, v_out)
+        kv_rows = lax.all_gather(jnp.stack(kv_all), 'kv').reshape(n_cols, layers, steps, seq_dev, -1)
+        v_at = kv_heads * dim // kv_w
+
+        def held(arr):
+            return pl.BlockSpec(arr.shape, lambda l, i: (0,) * arr.ndim, pipeline_mode=pl.Buffered(1))
+
+        k_out, v_out = pl.pallas_call(
+            functools.partial(_place_kernel, steps, pair),
+            grid=(layers, n_grid),
+            in_specs=[
+                pl.BlockSpec((n_cols, 1, steps, seq_dev, kv_w), lambda l, i: (0, l, 0, 0, i)),
+                pl.BlockSpec((n_cols, 1, steps, seq_dev, kv_w), lambda l, i: (0, l, 0, 0, v_at + i)),
+                both, both,
+                pl.BlockSpec((n_dev, 1, 1, n_move, m_w), lambda l, i: (0, l, 0, 0, i)),
+                pl.BlockSpec((n_dev, 1, 1, n_move, m_w), lambda l, i: (0, l, 1, 0, i)),
+                held(w_sel), held(mig), held(w_info),
+            ],
+            out_specs=[both, both],
+            out_shape=[jax.ShapeDtypeStruct(k_t.shape, BF16), jax.ShapeDtypeStruct(v_t.shape, BF16)],
+            scratch_shapes=[pltpu.VMEM((2, steps, kv_w, n_slots), BF16), pltpu.VMEM((page, dim, n_slots), BF16)],
+            compiler_params=pltpu.CompilerParams(vmem_limit_bytes=32 * MIB),
+            cost_estimate=_cost(40, 64),
+            name='place_pages',
+        )(kv_rows, kv_rows, k_t, v_t, moved, moved, w_sel, mig, w_info)
         y_out = hidden.reshape(steps, seq_dev, width)
         back = (4, 0, 1, 2, 3)
         return y_out, jnp.transpose(k_out, back), jnp.transpose(v_out, back)

time: 369 us -> 357 us (0.967); the launches traced: 363 us -> 356 us
  waiting for transfers between devices: 0.26 us -> 23.6 us
  local copies, waits for them, and re-layouts: 27.6 us -> 7.58 us
  Pallas kernels: 247 us -> 241 us
    all_gather x4 -> x2, waiting for transfers between devices: 0.01 us -> 22.8 us  [the longest x1 22.8 us: per_device(): moved = lax.all_gather(packed, group_axes)]
    unnamed x75 -> x54, local copies, waits for them, and re-layouts: 22.4 us -> 4.61 us
    pallas_call x6 -> x3, Pallas kernels: 88.7 us -> 80.3 us  [the longest x1 37.5 us: per_device(): pl.pallas_call(functools.partial(_place_kernel, steps, pair), grid=(layer...]
  transfers between devices with their start and end apart: 4 -> 2, of which waited for: 0 -> 1; matrix products, arithmetic and copies ran while one was open for 20% -> 9% of each run, Pallas kernels for 62% -> 28%
where the time goes in v3:
time: 357 us; the launch traced here: 356 us
  Pallas kernels  241 us (68%)
  matrix products  66.4 us (19%)
  waiting for transfers between devices  23.6 us (7%)
  between operations  14.5 us (4%)
  local copies, waits for them, and re-layouts  7.58 us (2%)
    pallas_call x2, Pallas kernels, exchange(): pl.pallas_call(functools.partial(_exchange_kernel, n_cols, n_rows, heads,...  70.7 us
    pallas_call x2, Pallas kernels, attend(): pl.pallas_call(functools.partial(_attn_kernel, steps, group, pair), grid=...  67.4 us
    dot_general x2, matrix products, per_device(): jnp.dot(up_act, w_down[layer], preferred_element_type=F32)  48 us
    pallas_call x1, Pallas kernels, per_device(): pl.pallas_call(functools.partial(_place_kernel, steps, pair), grid=(layer...  37.5 us
    pallas_call x1, Pallas kernels, per_device(): pl.pallas_call(functools.partial(_head_kernel, dims), in_specs=[vmem] * 5...  32.1 us
    all_gather x1, waiting for transfers between devices, per_device(): moved = lax.all_gather(packed, group_axes)  22.8 us
    pallas_call x1, Pallas kernels, per_device(): pl.pallas_call(functools.partial(_query_kernel, n_cols), in_specs=[vmem],...  22.6 us
    pallas_call x1, Pallas kernels, per_device(): pl.pallas_call(functools.partial(_pack_kernel, pair), grid=(layers, n_gri...  10.8 us
  transfers between devices with their start and end apart: 2, of which 1 were waited for; matrix products, arithmetic and copies ran while one was open for 9% of the time, Pallas kernels for 28%

profile of v3, /device:TPU:97, one launch (start us, length us, event | category | flops | bytes accessed | tf_op | source)
XLA Modules:
  0.0 356.1 jit_solution(3685922565296517803)
XLA Ops:
  7.2 0.1 all-gather.5.cloned.1.call-start
  7.3 0.7 tile.6
  7.9 0.1 broadcast_in_dim.51
  8.0 0.7 tile.7
  8.7 0.1 broadcast_in_dim.53
  8.8 0.8 reshape.84
  9.5 0.7 broadcast_subtract_fusion
  10.2 0.7 fusion.112.onehot_ref
  10.9 0.7 copy.17.mysrcc_ref
  11.6 5.2 %fusion.48.q_ref.refs_2_ = bf16[64,2048]{1,0:T(8,128)(2,1)S(1)} fusion(bf16[64,2048]{1,0:T(8,128)(2,1)} %bitcast.124, bf16[2,2048,2048]{2,1,0:T(8,128)(2,1)} %param.14), kind=kOutput, calls=%fused_computation.34 | convolution fusion | flops 537001984 | bytes 8912896 | tf_op jit(solution)/shard_map/dot_general | solution.py:615
  16.8 0.0 copy-done.15
  16.8 0.0 copy-done.17
  16.8 0.0 copy-start.18
  16.8 0.5 fusion.93
  17.3 0.3 copy-done.16
  17.6 0.5 fusion.90
  18.1 0.0 copy-done.18
  18.1 0.1 pad_add_fusion.1
  18.2 0.7 fusion.123
  18.9 0.1 and_select_fusion.1
  18.9 10.8 %pack_pages.1.pages_ref.refs_4_ = bf16[2,2,16,8192]{3,2,1,0:T(8,128)(2,1)} custom-call(bf16[16,208]{1,0:T(8,128)(2,1)} %fusion.112.onehot_ref, bf16[2,16,8,64,208]{4,3,2,1,0:T(8,128)(2,1)} %bitcast.116, bf16[2,16,8,64,208]{4,3,2,1,0:T(8,128)(2,1)} %bitcast.120), custom_call_target="tpu_custom_call" | custom-call | flops 8000000000 | bytes 16777216 | tf_op jit(solution)/shard_map/pack_pages/pallas_call | solution.py:603
  29.7 0.0 copy-done.2
  29.7 1.2 copy-done
  30.9 32.1 %head_gather.1 = (bf16[4,2,16,8192]{3,2,1,0:T(8,128)(2,1)S(1)}, bf16[8,64,2048]{2,1,0:T(8,128)(2,1)S(1)}, bf16[256,256]{1,0:T(8,128)(2,1)S(1)}, bf16[768,256]{1,...) custom-call(s32[24,128]{1,0:T(8,128)S(1)} %pad_add_fusion.meta_ref, ...), custom_call_target="tpu_custom_call" | custom-call | flops 10000000000 | bytes 4194304 | tf_op jit(solution)/shard_map/head_gather/pallas_call | solution.py:635
  63.0 0.0 copy-start.6
  63.0 0.7 copy-done.6
  63.7 0.7 copy-done.8
  64.4 0.0 slice-start
  64.4 0.0 slice-start.1
  64.4 0.0 slice-start.2
  64.4 33.7 %slot_attention.2 = (f32[2,4,2,32,2048]{4,3,2,1,0:T(8,128)S(1)}, f32[2,4,2,32,128]{4,3,2,1,0:T(8,128)S(1)}) custom-call(bf16[8,2,32,2048]{3,2,1,0:T(8,128)(2,1)S(1)} %bitcast.107, bf16[2,16,8,64,208]{4,3,2,1,0:T(8,128)(2,1)} %bitcast.117, bf16[2,16,8,64,208]{4,3,2,1,0:T(8,128)(2,1)} %bitcast.121, ...), custom_call_target="tpu_custom_call" | custom-call | flops 20000000000 | bytes 16777216 | tf_op jit(solution)/shard_map/slot_attention/pallas_call | solution.py:659
  98.2 0.0 copy-done.4
  98.2 0.0 copy-done.10
  98.2 0.0 copy-done.12
  98.2 0.0 slice-start.3
  98.2 26.4 %exchange_partials.2 = (bf16[64,2048]{1,0:T(8,128)(2,1)S(1)}, bf16[4,2,16,8192]{3,2,1,0:T(8,128)(2,1)S(1)}) custom-call(f32[2,4,2,32,2048]{4,3,2,1,0:T(8,128)S(1)} %get-tuple-element.26.refs_0_, f32[2,4,2,32,128]{4,3,2,1,0:T(8,128)S(1)} %get-tuple-element.27.refs_1_, bf16[64,2048]{1,0:T(8,128)(2,1)S(1)} %fusion.48.q_ref.refs_2_, ...), custom_call_target="tpu_custom_call" | custom-call | flops 10000000000 | bytes 4194304 | tf_op jit(solution)/shard_map/exchange_partials/pallas_call | solution.py:696
  124.7 0.0 slice-done
  124.7 0.0 slice-done.1
  124.7 0.0 slice-done.2
  124.7 0.0 slice-done.3
  124.7 1.6 fusion.45
  126.3 23.6 %fusion.39 = bf16[64,2048]{1,0:T(8,128)(2,1)S(1)} fusion(bf16[2,8192,2048]{2,1,0:T(8,128)(2,1)} %param.19, bf16[64,2048]{1,0:T(8,128)(2,1)S(1)} %fusion.45, bf16[2,2048,8192]{2,1,0:T(8,128)(2,1)} %param.18), kind=kOutput, calls=%fused_computation.31 | convolution fusion | flops 4300079104 | bytes 67895296 | tf_op jit(solution)/shard_map/dot_general | solution.py:735
  149.9 0.0 copy-start.14
  149.9 2.1 fusion.99
  152.0 2.1 fusion.96
  154.1 0.7 pad_maximum_fusion
  154.9 0.1 all-gather.5.cloned.1.call-update
  154.9 0.1 all-gather.7.cloned.1.call-start
  155.0 0.7 all-gather.7.cloned.1.call-update
  155.7 5.0 %fusion.51.q_ref.refs_2_ = bf16[64,2048]{1,0:T(8,128)(2,1)S(1)} fusion(bf16[64,2048]{1,0:T(8,128)(2,1)S(1)} %fusion.39, bf16[2,2048,2048]{2,1,0:T(8,128)(2,1)} %param.14), kind=kOutput, calls=%fused_computation.35 | convolution fusion | flops 537001984 | bytes 8912896 | tf_op jit(solution)/shard_map/dot_general | solution.py:615
  160.7 0.0 copy-start.5
  160.7 22.6 %query_gather.1 = bf16[8,64,2048]{2,1,0:T(8,128)(2,1)S(1)} custom-call(bf16[64,2048]{1,0:T(8,128)(2,1)S(1)} %fusion.51.q_ref.refs_2_), custom_call_target="tpu_custom_call" | custom-call | flops 5000000000 | bytes 4194304 | tf_op jit(solution)/shard_map/query_gather/pallas_call | solution.py:718
  183.4 0.0 slice-start.4
  183.4 0.0 slice-start.5
  183.4 0.0 slice-start.6
  183.4 33.7 %slot_attention.3 = (f32[2,4,2,32,2048]{4,3,2,1,0:T(8,128)S(1)}, f32[2,4,2,32,128]{4,3,2,1,0:T(8,128)S(1)}) custom-call(bf16[8,2,32,2048]{3,2,1,0:T(8,128)(2,1)S(1)} %bitcast.108, bf16[2,16,8,64,208]{4,3,2,1,0:T(8,128)(2,1)} %bitcast.118, bf16[2,16,8,64,208]{4,3,2,1,0:T(8,128)(2,1)} %bitcast.122, ...), custom_call_target="tpu_custom_call" | custom-call | flops 20000000000 | bytes 16777216 | tf_op jit(solution)/shard_map/slot_attention/pallas_call | solution.py:659
  217.1 0.0 slice-start.7
  217.1 44.2 %exchange_partials.3 = bf16[64,2048]{1,0:T(8,128)(2,1)S(1)} custom-call(f32[2,4,2,32,2048]{4,3,2,1,0:T(8,128)S(1)} %get-tuple-element.30.refs_0_, f32[2,4,2,32,128]{4,3,2,1,0:T(8,128)S(1)} %get-tuple-element.31.refs_1_, bf16[64,2048]{1,0:T(8,128)(2,1)S(1)} %fusion.51.q_ref.refs_2_, bf16[64,1024]{1,0:T(8,128)(2,1)S(1)} %get-tuple-element.40.refs_3_), custom_call_target="tpu_custom_call" | custom-call | flops 10000000000 | bytes 4194304 | tf_op jit(solution)/shard_map/exchange_partials/pallas_call | solution.py:696
  261.4 1.6 fusion.42
  263.0 24.4 %fusion.36 = bf16[64,2048]{1,0:T(8,128)(2,1)} fusion(bf16[2,8192,2048]{2,1,0:T(8,128)(2,1)} %param.19, bf16[64,2048]{1,0:T(8,128)(2,1)S(1)} %fusion.42, bf16[2,2048,8192]{2,1,0:T(8,128)(2,1)} %param.18), kind=kOutput, calls=%fused_computation.30 | convolution fusion | flops 4300079104 | bytes 67895296 | tf_op jit(solution)/shard_map/dot_general | solution.py:735
  287.4 22.8 %all-gather.7.cloned.1.call-done = bf16[64,2,16,8192]{3,2,1,0:T(8,128)(2,1)} async-done(((bf16[2,2,16,8192]{3,2,1,0:T(8,128)(2,1)}), bf16[64,2,16,8192]{3,2,1,0:T(8,128)(2,1)}) %all-gather.7.cloned.1.call-update) | async-done | bytes 33554448 | tf_op jit(solution)/shard_map/all_gather | solution.py:612
  310.2 0.0 copy-done.9
  310.2 1.6 copy-done.3
  311.8 37.5 %place_pages.1 = (bf16[2,16,8,64,208]{4,3,2,1,0:T(8,128)(2,1)}, bf16[2,16,8,64,208]{4,3,2,1,0:T(8,128)(2,1)}) custom-call(bf16[8,2,2,32,1024]{4,3,2,1,0:T(8,128)(2,1)S(1)} %bitcast.105, bf16[8,2,2,32,1024]{4,3,2,1,0:T(8,128)(2,1)S(1)} %bitcast.106, bf16[2,16,8,64,208]{4,3,2,1,0:T(8,128)(2,1)} %bitcast.119, bf16[2,16,8,64,208]{4,3,2,1,0:T(8,128)(2,1)} %bitcast.123, ...), custom_call_target="tpu_custom_call" | custom-call | flops 40000000000 | bytes 67108864 | tf_op jit(solution)/shard_map/place_pages/pallas_call | solution.py:742
  (33 shorter events, 0.1 us)
Async XLA Ops:
  7.2 280.2 %all-gather.5.cloned.1.call-start = ((), (), s32[]{:S(2)}) async-start(), calls=%async_computation | async-start | bytes 2359296 | tf_op jit(solution)/shard_map/all_gather | solution.py:736
  11.6 5.2 %copy-start.15 = (bf16[2,2048,512]{2,1,0:T(8,128)(2,1)S(1)}, bf16[2,2048,512]{2,1,0:T(8,128)(2,1)}, u32[]{:S(2)}) copy-start(bf16[2,2048,512]{2,1,0:T(8,128)(2,1)} %param.16) | copy-start | bytes 12582916
  11.6 5.2 %copy-start.17 = (bf16[2,32,2048]{2,1,0:T(8,128)(2,1)S(1)}, bf16[2,32,2048]{2,1,0:T(8,128)(2,1)}, u32[]{:S(2)}) copy-start(bf16[2,32,2048]{2,1,0:T(8,128)(2,1)} %param.13) | copy-start | bytes 786436
  11.6 6.0 %copy-start.16 = (bf16[2,2048,512]{2,1,0:T(8,128)(2,1)S(1)}, bf16[2,2048,512]{2,1,0:T(8,128)(2,1)}, u32[]{:S(2)}) copy-start(bf16[2,2048,512]{2,1,0:T(8,128)(2,1)} %param.15) | copy-start | bytes 12582916
  16.8 1.3 copy-start.18
  18.9 10.8 %copy-start.2 = (s32[16]{0:T(128)S(1)}, s32[16]{0:T(128)}, u32[]{:S(2)}) copy-start(s32[16]{0:T(128)} %param.24) | copy-start | bytes 196
  29.7 1.2 copy-start
  63.0 0.7 copy-start.6
  63.7 0.7 copy-start.8
  64.4 33.8 %copy-start.4 = (bf16[768,256]{1,0:T(8,128)(2,1)}, bf16[768,256]{1,0:T(8,128)(2,1)S(1)}, u32[]{:S(2)}) copy-start(bf16[768,256]{1,0:T(8,128)(2,1)S(1)} %get-tuple-element.23.cell_ref) | copy-start | bytes 1179652
  64.4 33.8 %copy-start.10 = (bf16[256,256]{1,0:T(8,128)(2,1)}, bf16[256,256]{1,0:T(8,128)(2,1)S(1)}, u32[]{:S(2)}) copy-start(bf16[256,256]{1,0:T(8,128)(2,1)S(1)} %get-tuple-element.22.qsel_ref) | copy-start | bytes 393220
  64.4 33.8 %copy-start.12 = (bf16[64,256]{1,0:T(8,128)(2,1)}, bf16[64,256]{1,0:T(8,128)(2,1)S(1)}, u32[]{:S(2)}) copy-start(bf16[64,256]{1,0:T(8,128)(2,1)S(1)} %get-tuple-element.24.arr_ref) | copy-start | bytes 98308
  64.4 33.8 %copy-start.1 = (bf16[2,2,16,8192]{3,2,1,0:T(8,128)(2,1)S(1)}, bf16[2,2,16,8192]{3,2,1,0:T(8,128)(2,1)}, u32[]{:S(2)}) copy-start(bf16[2,2,16,8192]{3,2,1,0:T(8,128)(2,1)} %pack_pages.1.pages_ref.refs_4_) | copy-start | bytes 3145732
  64.4 60.3 %slice-start = ((s8[16777216]{0:T(1024)(128)(4,1)}), s8[4194304]{0:T(1024)(128)(4,1)S(1)}, s32[]{:S(2)}) async-start(s8[16777216]{0:T(1024)(128)(4,1)} %bitcast.112), calls=%async_computation.2 | async-start | bytes 8388608
  64.4 60.3 %slice-start.1 = ((s8[16777216]{0:T(1024)(128)(4,1)}), s8[4194304]{0:T(1024)(128)(4,1)S(1)}, s32[]{:S(2)}) async-start(s8[16777216]{0:T(1024)(128)(4,1)} %bitcast.112), calls=%async_computation.3 | async-start | bytes 8388608
  64.4 60.3 %slice-start.2 = ((s8[16777216]{0:T(1024)(128)(4,1)}), s8[4194304]{0:T(1024)(128)(4,1)S(1)}, s32[]{:S(2)}) async-start(s8[16777216]{0:T(1024)(128)(4,1)} %bitcast.112), calls=%async_computation.4 | async-start | bytes 8388608
  98.2 26.5 %slice-start.3 = ((s8[16777216]{0:T(1024)(128)(4,1)}), s8[4194304]{0:T(1024)(128)(4,1)S(1)}, s32[]{:S(2)}) async-start(s8[16777216]{0:T(1024)(128)(4,1)} %bitcast.112), calls=%async_computation.5 | async-start | bytes 8388608
  149.9 4.2 %copy-start.14 = (bf16[1,64,1024]{2,1,0:T(8,128)(2,1)S(1)}, bf16[1,64,1024]{2,1,0:T(8,128)(2,1)}, u32[]{:S(2)}) copy-start(bf16[1,64,1024]{2,1,0:T(8,128)(2,1)} %get-tuple-element.37) | copy-start | bytes 393220
  154.9 155.3 %all-gather.7.cloned.1.call-start = ((), (), s32[]{:S(2)}) async-start(), calls=%async_computation.1 | async-start | bytes 34603008 | tf_op jit(solution)/shard_map/all_gather | solution.py:612
  160.7 22.6 %copy-start.5 = (bf16[768,256]{1,0:T(8,128)(2,1)S(1)}, bf16[768,256]{1,0:T(8,128)(2,1)}, u32[]{:S(2)}) copy-start(bf16[768,256]{1,0:T(8,128)(2,1)} %copy-done.4) | copy-start | bytes 1179652
  160.7 22.6 %copy-start.11 = (bf16[256,256]{1,0:T(8,128)(2,1)S(1)}, bf16[256,256]{1,0:T(8,128)(2,1)}, u32[]{:S(2)}) copy-start(bf16[256,256]{1,0:T(8,128)(2,1)} %copy-done.10) | copy-start | bytes 393220
  160.7 22.6 %copy-start.13 = (bf16[64,256]{1,0:T(8,128)(2,1)S(1)}, bf16[64,256]{1,0:T(8,128)(2,1)}, u32[]{:S(2)}) copy-start(bf16[64,256]{1,0:T(8,128)(2,1)} %copy-done.12) | copy-start | bytes 98308
  183.4 78.0 %slice-start.4 = ((s8[16777216]{0:T(1024)(128)(4,1)}), s8[4194304]{0:T(1024)(128)(4,1)S(1)}, s32[]{:S(2)}) async-start(s8[16777216]{0:T(1024)(128)(4,1)} %bitcast.114), calls=%async_computation.6 | async-start | bytes 8388608
  183.4 78.0 %slice-start.5 = ((s8[16777216]{0:T(1024)(128)(4,1)}), s8[4194304]{0:T(1024)(128)(4,1)S(1)}, s32[]{:S(2)}) async-start(s8[16777216]{0:T(1024)(128)(4,1)} %bitcast.114), calls=%async_computation.7 | async-start | bytes 8388608
  183.4 78.0 %slice-start.6 = ((s8[16777216]{0:T(1024)(128)(4,1)}), s8[4194304]{0:T(1024)(128)(4,1)S(1)}, s32[]{:S(2)}) async-start(s8[16777216]{0:T(1024)(128)(4,1)} %bitcast.114), calls=%async_computation.8 | async-start | bytes 8388608
  217.1 44.3 %slice-start.7 = ((s8[16777216]{0:T(1024)(128)(4,1)}), s8[4194304]{0:T(1024)(128)(4,1)S(1)}, s32[]{:S(2)}) async-start(s8[16777216]{0:T(1024)(128)(4,1)} %bitcast.114), calls=%async_computation.9 | async-start | bytes 8388608
  263.0 47.2 %copy-start.7 = (bf16[512,208]{1,0:T(8,128)(2,1)S(1)}, bf16[512,208]{1,0:T(8,128)(2,1)}, u32[]{:S(2)}) copy-start(bf16[512,208]{1,0:T(8,128)(2,1)} %copy-done.6) | copy-start | bytes 638980
  263.0 47.2 %copy-start.9 = (bf16[256,208]{1,0:T(8,128)(2,1)S(1)}, bf16[256,208]{1,0:T(8,128)(2,1)}, u32[]{:S(2)}) copy-start(bf16[256,208]{1,0:T(8,128)(2,1)} %copy-done.8) | copy-start | bytes 319492
  310.2 1.6 copy-start.3
Sparse Core Ops, SparseCore 0:
  155.0 28.0 all-gather.4
  185.8 124.2 all-gather.6

commit v4 on v3

--- a/solution.py
+++ b/solution.py
@@ -6,6 +6,7 @@
 from jax.experimental import pallas as pl
 from jax.experimental.pallas import tpu as pltpu
 from jax.sharding import PartitionSpec as P
+
 
 F32 = jnp.float32
 BF16 = jnp.bfloat16
@@ -127,13 +128,14 @@
     winfo_ref[1:2, :] = jnp.where(written > 0, w_off, -100.0)
 
 
-def _pack_kernel(heads, onehot_ref, k_ref, v_ref, out_ref):
-    page, _, dim, n_slots = k_ref.shape[1:]
-    width = page * dim
-    for h in range(heads):
-        for which, src in enumerate((k_ref, v_ref)):
+def _pack_kernel(heads, onehot_ref, *refs):
+    half = len(refs) // 2
+    for src, out in zip(refs[:half], refs[half:]):
+        page, _, dim, n_slots = src.shape[1:]
+        width = page * dim
+        for h in range(heads):
             rows = src[0, :, h].reshape(width, n_slots)
-            out_ref[0, which, :, h * width:(h + 1) * width] = _dot(onehot_ref[...], rows, NT).astype(BF16)
+            out[:, h * width:(h + 1) * width] = _dot(onehot_ref[...], rows, NT).astype(BF16)
 
 
 def _copy(src, dst, sems, k, dev):
@@ -255,13 +257,13 @@
 
 
 def _half0(ref, h):
-    return ref.at[h]
-
-
-def _head_kernel(dims, meta_ref, pages_ref, q_ref, mysrc_ref, mysrcc_ref, pages_all, q_all, *refs):
+    return ref[h] if isinstance(ref, tuple) else ref.at[h]
+
+
+def _head_kernel(dims, meta_ref, kp_ref, vp_ref, q_ref, mysrc_ref, mysrcc_ref, pages_all, q_all, *refs):
     tables, (meta_all, m_sem, y_sem, x_sem) = refs[:7], refs[7:]
     n_rows, n_cols = dims[:2]
-    pages_ref = pages_ref.at[0]
+    pages_ref = (kp_ref, vp_ref)
     y, at = lax.axis_index('kv2'), lax.axis_index('kv')
     offsets = [(a, b) for a in range(n_rows) for b in range(n_cols) if (a, b) != (0, 0)]
     peers = [{'kv2': (y + a) % n_rows, 'kv': (at + b) % n_cols} for a, b in offsets]
@@ -275,7 +277,8 @@
     steps = _q_gather(n_cols, q_ref, q_all, x_sem)
     next(steps)
     meta_all[me] = meta_ref[...]
-    pages_all[y] = pages_ref[...]
+    for h, ref in enumerate(pages_ref):
+        pages_all[y, h] = ref[...]
     next(steps)
     forward()
     for k, (a, b) in enumerate(offsets):
@@ -397,7 +400,7 @@
 
 def _exchange_kernel(n_cols, n_rows, heads, dim, has_pages, *refs):
     o_ref, ml_ref, q_ref, kv_ref = refs[:I4]
-    n_in = I5 if has_pages else I4
+    n_in = 6 if has_pages else I4
     n_out = I2 if has_pages else I1
     out_ref = refs[n_in]
     rp_o, rp_ml, cur_o, cur_ml, rel_o, rel_ml, fin_o, fin_ml, spread, expand, p_sem, r_sem, y_sem = refs[n_in + n_out:]
@@ -417,10 +420,11 @@
     for c in pals:
         c.start()
     if has_pages:
-        pages_ref, pages_all = refs[I4].at[I1], refs[n_in + I1]
+        pages_ref, pages_all = refs[I4:n_in], refs[n_in + I1]
         y_start, y_forward, y_finish = _rows_on_y(pages_ref, pages_all, y_sem, _half0)
         y_start()
-        pages_all[lax.axis_index('kv2')] = pages_ref[...]
+        for h, ref in enumerate(pages_ref):
+            pages_all[lax.axis_index('kv2'), h] = ref[...]
 
     n_chunk = I4
     cw = width // n_chunk
@@ -531,7 +535,9 @@
         c.wait_send()
 
 
-def _place_kernel(steps, heads, kn_ref, vn_ref, k_ref, v_ref, mk_ref, mv_ref, wsel_ref, mig_ref, info_ref, ko_ref, vo_ref, kv_s, full):
+def _place_kernel(steps, heads, n_alias, *refs):
+    kn_ref, vn_ref, k_ref, v_ref, mk_ref, mv_ref, wsel_ref, mig_ref, info_ref = refs[:9]
+    ko_ref, vo_ref, kv_s, full = refs[9 + n_alias:]
     page, _, dim, n_slots = k_ref.shape[1:]
     n_seq = wsel_ref.shape[0]
     width = page * dim
@@ -543,7 +549,7 @@
             kv_s[which, t] = _dot(ref[:, 0, t].reshape(n_seq, heads * dim), wsel_ref[...], TN).astype(BF16)
     for h in range(heads):
         for which, (pool, pages, out) in enumerate(((k_ref, mk_ref, ko_ref), (v_ref, mv_ref, vo_ref))):
-            full[...] = _dot(pages[:, 0, 0, :, h * width:(h + 1) * width].reshape(n_all, width), mig_ref[...], TN).astype(BF16).reshape(page, dim, n_slots)
+            full[...] = _dot(pages[:, :, h * width:(h + 1) * width].reshape(n_all, width), mig_ref[...], TN).astype(BF16).reshape(page, dim, n_slots)
 
             def fill(tok, _, which=which, pool=pool, out=out, h=h):
                 at = w_off - tok.astype(F32)
@@ -599,17 +605,20 @@
         def pool_blk(layer):
             return pl.BlockSpec((1, page, pair, dim, n_slots), lambda i: (layer, 0, i, 0, 0))
 
-        both = pl.BlockSpec((1, page, pair, dim, n_slots), lambda l, i: (l, 0, i, 0, 0))
+        page_blk = pl.BlockSpec((n_move, m_w), lambda i: (0, i))
+        flat = jax.ShapeDtypeStruct((n_move, kv_heads * page_w), BF16)
         packed = pl.pallas_call(
             functools.partial(_pack_kernel, pair),
-            grid=(layers, n_grid),
-            in_specs=[pl.BlockSpec((n_move, n_slots), lambda l, i: (0, 0)), both, both],
-            out_specs=pl.BlockSpec((1, 2, n_move, m_w), lambda l, i: (l, 0, 0, i)),
-            out_shape=jax.ShapeDtypeStruct((layers,) + page_shape, BF16),
+            grid=(n_grid,),
+            in_specs=[pl.BlockSpec((n_move, n_slots), lambda i: (0, 0))] + [pool_blk(l) for l in range(layers) for _ in (k_t, v_t)],
+            out_specs=[page_blk] * (2 * layers),
+            out_shape=[flat] * (2 * layers),
             cost_estimate=_cost(8, 16),
             name='pack_pages',
-        )(src_hot, k_t, v_t)
-        moved = lax.all_gather(packed, group_axes)
+        )(src_hot, *[a for _ in range(layers) for a in (k_t, v_t)])
+
+        def whole(i, after):
+            return lax.all_gather(lax.optimization_barrier((packed[i], after))[0], group_axes)
 
         def project(hidden, layer):
             q = jnp.dot(hidden, w_query[layer], preferred_element_type=F32).astype(BF16)
@@ -634,7 +643,7 @@
         dims = (n_rows, n_cols, n_slots, n_pages, page, seq_dev)
         pages_y, q_all, q_sel, cells, arr, info, w_sel, mig, w_info = pl.pallas_call(
             functools.partial(_head_kernel, dims),
-            in_specs=[vmem] * 5,
+            in_specs=[vmem] * 6,
             out_specs=[vmem] * 9,
             out_shape=[
                 pages_all_shape,
@@ -651,7 +660,7 @@
             compiler_params=pltpu.CompilerParams(collective_id=0, has_side_effects=True, vmem_limit_bytes=24 * MIB),
             cost_estimate=_cost(10, 4),
             name='head_gather',
-        )(meta, packed, q, src_slot.reshape(1, -1), src_slot.reshape(-1, 1))
+        )(meta, *packed[:2], q, src_slot.reshape(1, -1), src_slot.reshape(-1, 1))
 
         def attend(layer, q_all, pages):
             blk = pool_blk(layer)
@@ -695,7 +704,7 @@
             out_shape = [jax.ShapeDtypeStruct((rows, heads * dim), BF16)] + ([pages_all_shape] if has else [])
             return pl.pallas_call(
                 functools.partial(_exchange_kernel, n_cols, n_rows, heads, dim, has),
-                in_specs=[vmem] * (5 if has else 4),
+                in_specs=[vmem] * (6 if has else 4),
                 out_specs=[vmem] * len(out_shape),
                 out_shape=out_shape,
                 scratch_shapes=[
@@ -709,9 +718,9 @@
                 compiler_params=pltpu.CompilerParams(collective_id=1 + layer, has_side_effects=True, vmem_limit_bytes=32 * MIB),
                 cost_estimate=_cost(10, 4),
                 name='exchange_partials',
-            )(o, ml, q, kv, *([pages] if has else []))
-
-        kv_all = []
+            )(o, ml, q, kv, *(pages if has else []))
+
+        kv_all, moved = [], []
         for layer in range(layers):
             if layer:
                 q, kv = project(hidden, layer)
@@ -726,37 +735,40 @@
                     name='query_gather',
                 )(q)
             kv_all.append(kv)
+            if layer + 1 == layers:
+                kv_rows = lax.all_gather(jnp.stack(kv_all), 'kv')
+                kv_rows = kv_rows.reshape(n_cols, layers, steps, seq_dev, -1)
             o, ml = attend(layer, q_all, pages_y)
-            nxt = packed if layer + 1 < layers else None
+            nxt = packed[2 * (layer + 1):2 * (layer + 2)] if layer + 1 < layers else None
+            moved.append(whole(2 * layer, q_all))
             attn, *more = exchange(layer, o, ml, q, kv, nxt)
             pages_y = more[0] if more else None
+            moved.append(whole(2 * layer + 1, attn))
             hidden = (hidden.astype(F32) + jnp.dot(attn, w_out[layer], preferred_element_type=F32)).astype(BF16)
             up_act = jax.nn.gelu(jnp.dot(hidden, w_up[layer], preferred_element_type=F32)).astype(BF16)
             hidden = (hidden.astype(F32) + jnp.dot(up_act, w_down[layer], preferred_element_type=F32)).astype(BF16)
-        kv_rows = lax.all_gather(jnp.stack(kv_all), 'kv').reshape(n_cols, layers, steps, seq_dev, -1)
         v_at = kv_heads * dim // kv_w
-
-        def held(arr):
-            return pl.BlockSpec(arr.shape, lambda l, i: (0,) * arr.ndim, pipeline_mode=pl.Buffered(1))
-
-        k_out, v_out = pl.pallas_call(
-            functools.partial(_place_kernel, steps, pair),
-            grid=(layers, n_grid),
-            in_specs=[
-                pl.BlockSpec((n_cols, 1, steps, seq_dev, kv_w), lambda l, i: (0, l, 0, 0, i)),
-                pl.BlockSpec((n_cols, 1, steps, seq_dev, kv_w), lambda l, i: (0, l, 0, 0, v_at + i)),
-                both, both,
-                pl.BlockSpec((n_dev, 1, 1, n_move, m_w), lambda l, i: (0, l, 0, 0, i)),
-                pl.BlockSpec((n_dev, 1, 1, n_move, m_w), lambda l, i: (0, l, 1, 0, i)),
-                held(w_sel), held(mig), held(w_info),
-            ],
-            out_specs=[both, both],
-            out_shape=[jax.ShapeDtypeStruct(k_t.shape, BF16), jax.ShapeDtypeStruct(v_t.shape, BF16)],
-            scratch_shapes=[pltpu.VMEM((2, steps, kv_w, n_slots), BF16), pltpu.VMEM((page, dim, n_slots), BF16)],
-            compiler_params=pltpu.CompilerParams(vmem_limit_bytes=32 * MIB),
-            cost_estimate=_cost(40, 64),
-            name='place_pages',
-        )(kv_rows, kv_rows, k_t, v_t, moved, moved, w_sel, mig, w_info)
+        outs = []
+        for layer in range(layers):
+            blk = pool_blk(layer)
+            specs = [
+                pl.BlockSpec((n_cols, 1, steps, seq_dev, kv_w), lambda i, layer=layer: (0, layer, 0, 0, i)),
+                pl.BlockSpec((n_cols, 1, steps, seq_dev, kv_w), lambda i, layer=layer: (0, layer, 0, 0, v_at + i)),
+                blk, blk,
+            ] + [pl.BlockSpec((n_dev, n_move, m_w), lambda i: (0, 0, i))] * 2 + [fixed(a.shape) for a in (w_sel, mig, w_info)]
+            outs = pl.pallas_call(
+                functools.partial(_place_kernel, steps, pair, len(outs)),
+                grid=(n_grid,),
+                in_specs=specs + [pl.BlockSpec(memory_space=pl.ANY)] * len(outs),
+                out_specs=[blk, blk],
+                out_shape=[jax.ShapeDtypeStruct(a.shape, BF16) for a in (k_t, v_t)],
+                scratch_shapes=[pltpu.VMEM((2, steps, kv_w, n_slots), BF16), pltpu.VMEM((page, dim, n_slots), BF16)],
+                input_output_aliases={len(specs) + i: i for i in range(len(outs))},
+                compiler_params=pltpu.CompilerParams(vmem_limit_bytes=32 * MIB),
+                cost_estimate=_cost(20, 32),
+                name='place_pages',
+            )(kv_rows, kv_rows, k_t, v_t, moved[2 * layer], moved[2 * layer + 1], w_sel, mig, w_info, *outs)
+        k_out, v_out = outs
         y_out = hidden.reshape(steps, seq_dev, width)
         back = (4, 0, 1, 2, 3)
         return y_out, jnp.transpose(k_out, back), jnp.transpose(v_out, back)

time: 357 us -> 437 us (1.22); the launches traced: 356 us -> 429 us
  waiting for transfers between devices: 23.6 us -> 78.4 us
  local copies, waits for them, and re-layouts: 7.58 us -> 27.2 us
  Pallas kernels: 241 us -> 229 us
  matrix products: 66.4 us -> 77.8 us
    all_gather x2 -> x5, waiting for transfers between devices: 22.8 us -> 76.7 us  [the longest x4 76.7 us: whole(): lax.all_gather(lax.optimization_barrier((packed[i], after))[0], group_axes)]
    unnamed x54 -> x38, local copies, waits for them, and re-layouts: 4.61 us -> 24.2 us
    pallas_call x2, Pallas kernels: 70.7 us -> 58.8 us  [exchange(): pl.pallas_call(functools.partial(_exchange_kernel, n_cols, n_rows, heads,...]
    dot_general x2, matrix products: 3.15 us -> 9.97 us  [per_device(): jnp.dot(attn, w_out[layer], preferred_element_type=F32)]
    pallas_call x3 -> x4, Pallas kernels: 80.3 us -> 81.3 us  [the longest x2 40.4 us: per_device(): pl.pallas_call(functools.partial(_place_kernel, steps, pair, len(outs)),...]
  transfers between devices with their start and end apart: 2 -> 5, of which waited for: 1 -> 3; matrix products, arithmetic and copies ran while one was open for 9% -> 8% of each run, Pallas kernels for 28% -> 25%
where the time goes in v4:
time: 437 us; the launch traced here: 429 us
  Pallas kernels  229 us (52%)
  waiting for transfers between devices  78.4 us (18%)
  matrix products  77.8 us (18%)
  local copies, waits for them, and re-layouts  27.2 us (6%)
  between operations  14.3 us (3%)
    all_gather x4, waiting for transfers between devices, whole(): lax.all_gather(lax.optimization_barrier((packed[i], after))[0], group_axes)  76.7 us
    pallas_call x2, Pallas kernels, attend(): pl.pallas_call(functools.partial(_attn_kernel, steps, group, pair), grid=...  67.4 us
    pallas_call x2, Pallas kernels, exchange(): pl.pallas_call(functools.partial(_exchange_kernel, n_cols, n_rows, heads,...  58.8 us
    dot_general x2, matrix products, per_device(): jnp.dot(up_act, w_down[layer], preferred_element_type=F32)  49.3 us
    pallas_call x2, Pallas kernels, per_device(): pl.pallas_call(functools.partial(_place_kernel, steps, pair, len(outs)),...  40.4 us
    pallas_call x1, Pallas kernels, per_device(): pl.pallas_call(functools.partial(_head_kernel, dims), in_specs=[vmem] * 6...  31.8 us
    unnamed x38, local copies, waits for them, and re-layouts  24.2 us
    pallas_call x1, Pallas kernels, per_device(): pl.pallas_call(functools.partial(_query_kernel, n_cols), in_specs=[vmem],...  21.8 us
  transfers between devices with their start and end apart: 5, of which 3 were waited for; matrix products, arithmetic and copies ran while one was open for 8% of the time, Pallas kernels for 25%

profile of v4, /device:TPU:97, one launch (start us, length us, event | category | flops | bytes accessed | tf_op | source)
XLA Modules:
  0.0 429.4 jit_solution(3826468055830328804)
XLA Ops:
  7.2 0.0 copy-start.15
  7.2 0.1 all-gather.11.cloned.1.call-start
  7.3 0.8 reshape.84
  8.1 0.7 tile.7
  8.7 0.1 broadcast_in_dim.53
  8.8 0.7 broadcast_subtract_fusion
  9.5 0.7 tile.6
  10.1 0.1 broadcast_in_dim.51
  10.2 0.7 fusion.112.onehot_ref
  10.9 0.7 copy.19.mysrcc_ref
  11.6 2.2 fusion.93
  13.8 2.2 fusion.90
  16.0 0.0 copy-done.15
  16.0 0.0 copy-start.16
  16.0 5.0 %fusion.48.q_ref.refs_2_ = bf16[64,2048]{1,0:T(8,128)(2,1)S(1)} fusion(bf16[64,2048]{1,0:T(8,128)(2,1)S(1)} %bitcast.133, bf16[2,2048,2048]{2,1,0:T(8,128)(2,1)} %param.14), kind=kOutput, calls=%fused_computation.34 | convolution fusion | flops 537001984 | bytes 8912896 | tf_op jit(solution)/shard_map/dot_general | solution.py:624
  21.0 0.1 pad_add_fusion.1
  21.1 0.1 and_select_fusion.1
  21.1 9.0 %pack_pages.1 = (bf16[16,8192]{1,0:T(8,128)(2,1)}, bf16[16,8192]{1,0:T(8,128)(2,1)}, bf16[16,8192]{1,0:T(8,128)(2,1)}, bf16[16,8192]{1,0:T(8,128)(2,1)}) custom-call(bf16[16,208]{1,0:T(8,128)(2,1)} %fusion.112.onehot_ref, bf16[2,16,8,64,208]{4,3,2,1,0:T(8,128)(2,1)} %bitcast.118, bf16[2,16,8,64,208]{4,3,2,1,0:T(8,128)(2,1)} %bitcast.124, ...), custom_call_target="tpu_custom_call" | custom-call | flops 8000000000 | bytes 16777216 | tf_op jit(solution)/shard_map/pack_pages/pallas_call | solution.py:610
  30.1 0.9 copy-done.2
  31.1 0.9 copy-done.3
  32.0 31.8 %head_gather.1 = (bf16[4,2,16,8192]{3,2,1,0:T(8,128)(2,1)S(1)}, bf16[8,64,2048]{2,1,0:T(8,128)(2,1)S(1)}, bf16[256,256]{1,0:T(8,128)(2,1)S(1)}, bf16[768,256]{1,...) custom-call(s32[24,128]{1,0:T(8,128)S(1)} %pad_add_fusion.meta_ref, ...), custom_call_target="tpu_custom_call" | custom-call | flops 10000000000 | bytes 4194304 | tf_op jit(solution)/shard_map/head_gather/pallas_call | solution.py:644
  63.9 33.9 %slot_attention.2 = (f32[2,4,2,32,2048]{4,3,2,1,0:T(8,128)S(1)}, f32[2,4,2,32,128]{4,3,2,1,0:T(8,128)S(1)}) custom-call(bf16[8,2,32,2048]{3,2,1,0:T(8,128)(2,1)S(1)} %bitcast.117, bf16[2,16,8,64,208]{4,3,2,1,0:T(8,128)(2,1)} %bitcast.120, bf16[2,16,8,64,208]{4,3,2,1,0:T(8,128)(2,1)} %bitcast.126, ...), custom_call_target="tpu_custom_call" | custom-call | flops 20000000000 | bytes 16777216 | tf_op jit(solution)/shard_map/slot_attention/pallas_call | solution.py:668
  97.8 0.0 copy-start.11
  97.8 2.0 copy-done.11
  99.8 0.0 copy-done.1
  99.8 2.2 copy-done.12
  102.0 26.7 %exchange_partials.2 = (bf16[64,2048]{1,0:T(8,128)(2,1)S(1)}, bf16[4,2,16,8192]{3,2,1,0:T(8,128)(2,1)S(1)}) custom-call(f32[2,4,2,32,2048]{4,3,2,1,0:T(8,128)S(1)} %copy-done.12, f32[2,4,2,32,128]{4,3,2,1,0:T(8,128)S(1)} %get-tuple-element.39.refs_1_, bf16[64,2048]{1,0:T(8,128)(2,1)S(1)} %fusion.48.q_ref.refs_2_, ...), custom_call_target="tpu_custom_call" | custom-call | flops 10000000000 | bytes 4194304 | tf_op jit(solution)/shard_map/exchange_partials/pallas_call | solution.py:705
  128.7 0.0 copy-start.13
  128.7 1.3 copy-done.13
  130.0 5.0 %fusion.45 = bf16[64,2048]{1,0:T(8,128)(2,1)S(1)} fusion(bf16[64,2048]{1,0:T(8,128)(2,1)S(1)} %get-tuple-element.42, bf16[2,2048,2048]{2,1,0:T(8,128)(2,1)} %param.17, bf16[64,2048]{1,0:T(8,128)(2,1)S(1)} %bitcast.134), kind=kOutput, calls=%fused_computation.33 | convolution fusion | flops 537264128 | bytes 9175040 | tf_op jit(solution)/shard_map/dot_general | solution.py:747
  135.0 23.6 %fusion.39 = bf16[64,2048]{1,0:T(8,128)(2,1)S(1)} fusion(bf16[2,8192,2048]{2,1,0:T(8,128)(2,1)} %param.19, bf16[64,2048]{1,0:T(8,128)(2,1)S(1)} %fusion.45, bf16[2,2048,8192]{2,1,0:T(8,128)(2,1)} %param.18), kind=kOutput, calls=%fused_computation.31 | convolution fusion | flops 4300079104 | bytes 67895296 | tf_op jit(solution)/shard_map/dot_general | solution.py:749
  158.6 0.0 copy-start.17
  158.6 2.2 fusion.99
  160.8 2.1 fusion.96
  162.9 0.7 pad_maximum_fusion
  163.6 0.1 all-gather.11.cloned.1.call-update
  163.7 0.1 all-gather.17.cloned.1.call-start
  163.7 0.7 all-gather.17.cloned.1.call-update
  164.5 0.1 all-gather.19.cloned.1.call-start
  164.5 0.7 all-gather.19.cloned.1.call-update
  165.3 0.1 all-gather.13.cloned.1.call-start
  165.4 5.0 %fusion.51.q_ref.refs_2_ = bf16[64,2048]{1,0:T(8,128)(2,1)S(1)} fusion(bf16[64,2048]{1,0:T(8,128)(2,1)S(1)} %fusion.39, bf16[2,2048,2048]{2,1,0:T(8,128)(2,1)} %param.14), kind=kOutput, calls=%fused_computation.35 | convolution fusion | flops 537001984 | bytes 8912896 | tf_op jit(solution)/shard_map/dot_general | solution.py:624
  170.3 21.8 %query_gather.1 = bf16[8,64,2048]{2,1,0:T(8,128)(2,1)S(1)} custom-call(bf16[64,2048]{1,0:T(8,128)(2,1)S(1)} %fusion.51.q_ref.refs_2_), custom_call_target="tpu_custom_call" | custom-call | flops 5000000000 | bytes 4194304 | tf_op jit(solution)/shard_map/query_gather/pallas_call | solution.py:727
  192.1 0.1 all-gather.13.cloned.1.call-update
  192.2 0.1 all-gather.15.cloned.1.call-start
  192.2 0.0 copy-start.14
  192.3 1.6 copy-done.14
  193.8 33.5 %slot_attention.3 = (f32[2,4,2,32,2048]{4,3,2,1,0:T(8,128)S(1)}, f32[2,4,2,32,128]{4,3,2,1,0:T(8,128)S(1)}) custom-call(bf16[8,2,32,2048]{3,2,1,0:T(8,128)(2,1)S(1)} %bitcast.116, bf16[2,16,8,64,208]{4,3,2,1,0:T(8,128)(2,1)} %bitcast.121, bf16[2,16,8,64,208]{4,3,2,1,0:T(8,128)(2,1)} %bitcast.127, bf16[4,2,16,8192]{3,2,1,0:T(8,128)(2,1)S(1)} %copy-done.14, ...), custom_call_target="tpu_custom_call" | custom-call | flops 20000000000 | bytes 16777216 | tf_op jit(solution)/shard_map/slot_attention/pallas_call | solution.py:668
  227.4 0.0 copy-start.18
  227.4 32.1 %exchange_partials.3 = bf16[64,2048]{1,0:T(8,128)(2,1)S(1)} custom-call(f32[2,4,2,32,2048]{4,3,2,1,0:T(8,128)S(1)} %get-tuple-element.44.refs_0_, f32[2,4,2,32,128]{4,3,2,1,0:T(8,128)S(1)} %get-tuple-element.45.refs_1_, bf16[64,2048]{1,0:T(8,128)(2,1)S(1)} %fusion.51.q_ref.refs_2_, bf16[64,1024]{1,0:T(8,128)(2,1)S(1)} %get-tuple-element.60.refs_3_), custom_call_target="tpu_custom_call" | custom-call | flops 10000000000 | bytes 4194304 | tf_op jit(solution)/shard_map/exchange_partials/pallas_call | solution.py:705
  259.5 0.1 all-gather.15.cloned.1.call-update
  259.6 0.0 copy-done.18
  259.6 5.0 %fusion.42 = bf16[64,2048]{1,0:T(8,128)(2,1)S(1)} fusion(bf16[64,2048]{1,0:T(8,128)(2,1)S(1)} %exchange_partials.3, bf16[2,2048,2048]{2,1,0:T(8,128)(2,1)} %param.17, bf16[64,2048]{1,0:T(8,128)(2,1)S(1)} %copy-done.18), kind=kOutput, calls=%fused_computation.32 | convolution fusion | flops 537264128 | bytes 9175040 | tf_op jit(solution)/shard_map/dot_general | solution.py:747
  264.6 25.8 %fusion.36 = bf16[64,2048]{1,0:T(8,128)(2,1)} fusion(bf16[2,8192,2048]{2,1,0:T(8,128)(2,1)} %param.19, bf16[64,2048]{1,0:T(8,128)(2,1)S(1)} %fusion.42, bf16[2,2048,8192]{2,1,0:T(8,128)(2,1)} %param.18), kind=kOutput, calls=%fused_computation.30 | convolution fusion | flops 4300079104 | bytes 67895296 | tf_op jit(solution)/shard_map/dot_general | solution.py:749
  290.3 7.2 %all-gather.19.cloned.1.call-done = bf16[512,8192]{1,0:T(8,128)(2,1)} async-done(((bf16[16,8192]{1,0:T(8,128)(2,1)}), bf16[512,8192]{1,0:T(8,128)(2,1)}) %all-gather.19.cloned.1.call-update) | async-done | bytes 8388624 | tf_op jit(solution)/shard_map/all_gather | solution.py:621
  297.6 3.4 copy-done.5
  300.9 3.4 copy-done.7
  304.3 1.6 copy-done.9
  306.0 20.4 %place_pages.2 = (bf16[2,16,8,64,208]{4,3,2,1,0:T(8,128)(2,1)}, bf16[2,16,8,64,208]{4,3,2,1,0:T(8,128)(2,1)}) custom-call(bf16[8,2,2,32,1024]{4,3,2,1,0:T(8,128)(2,1)S(1)} %bitcast.112, bf16[8,2,2,32,1024]{4,3,2,1,0:T(8,128)(2,1)S(1)} %bitcast.113, bf16[2,16,8,64,208]{4,3,2,1,0:T(8,128)(2,1)} %bitcast.122, bf16[2,16,8,64,208]{4,3,2,1,0:T(8,128)(2,1)} %bitcast.128, ...), custom_call_target="tpu_custom_call" | custom-call | flops 20000000000 | bytes 33554432 | tf_op jit(solution)/shard_map/place_pages/pallas_call | solution.py:759
  326.4 20.4 %all-gather.13.cloned.1.call-done = bf16[512,8192]{1,0:T(8,128)(2,1)} async-done(((bf16[16,8192]{1,0:T(8,128)(2,1)}), bf16[512,8192]{1,0:T(8,128)(2,1)}) %all-gather.13.cloned.1.call-update) | async-done | bytes 8388624 | tf_op jit(solution)/shard_map/all_gather | solution.py:621
  346.8 49.2 %all-gather.15.cloned.1.call-done = bf16[512,8192]{1,0:T(8,128)(2,1)} async-done(((bf16[16,8192]{1,0:T(8,128)(2,1)}), bf16[512,8192]{1,0:T(8,128)(2,1)}) %all-gather.15.cloned.1.call-update) | async-done | bytes 8388624 | tf_op jit(solution)/shard_map/all_gather | solution.py:621
  395.9 3.4 copy-done.6
  399.3 3.4 copy-done.8
  402.7 20.0 %place_pages.3 = (bf16[2,16,8,64,208]{4,3,2,1,0:T(8,128)(2,1)}, bf16[2,16,8,64,208]{4,3,2,1,0:T(8,128)(2,1)}) custom-call(bf16[8,2,2,32,1024]{4,3,2,1,0:T(8,128)(2,1)S(1)} %bitcast.114, bf16[8,2,2,32,1024]{4,3,2,1,0:T(8,128)(2,1)S(1)} %bitcast.115, bf16[2,16,8,64,208]{4,3,2,1,0:T(8,128)(2,1)} %bitcast.123, ...), custom_call_target="tpu_custom_call", output_to_operand_aliasing={{0}: (9, {}), {1}: (10, {})} | custom-call | flops 20000000000 | bytes 33554432 | tf_op jit(solution)/shard_map/place_pages/pallas_call | solution.py:759
  (25 shorter events, 0.1 us)
Async XLA Ops:
  7.2 8.8 %copy-start.15 = (bf16[2,32,2048]{2,1,0:T(8,128)(2,1)S(1)}, bf16[2,32,2048]{2,1,0:T(8,128)(2,1)}, u32[]{:S(2)}) copy-start(bf16[2,32,2048]{2,1,0:T(8,128)(2,1)} %param.13) | copy-start | bytes 786436
  7.2 283.1 %all-gather.11.cloned.1.call-start = ((), (), s32[]{:S(2)}) async-start(), calls=%async_computation | async-start | bytes 2359296 | tf_op jit(solution)/shard_map/all_gather | solution.py:739
  16.0 5.0 %copy-start.16 = (s32[32]{0:T(128)S(1)}, s32[32]{0:T(128)}, u32[]{:S(2)}) copy-start(s32[32]{0:T(128)} %param.23) | copy-start | bytes 388
  21.1 9.0 %copy-start.4 = (s32[16]{0:T(128)S(1)}, s32[16]{0:T(128)}, u32[]{:S(2)}) copy-start(s32[16]{0:T(128)} %param.24) | copy-start | bytes 196
  30.1 1.0 copy-start.2
  31.1 0.9 copy-start.3
  63.9 35.9 %copy-start = (bf16[16,8192]{1,0:T(8,128)(2,1)S(1)}, bf16[16,8192]{1,0:T(8,128)(2,1)}, u32[]{:S(2)}) copy-start(bf16[16,8192]{1,0:T(8,128)(2,1)} %get-tuple-element.47.refs_5_) | copy-start | bytes 786436
  63.9 35.9 %copy-start.1 = (bf16[16,8192]{1,0:T(8,128)(2,1)S(1)}, bf16[16,8192]{1,0:T(8,128)(2,1)}, u32[]{:S(2)}) copy-start(bf16[16,8192]{1,0:T(8,128)(2,1)} %get-tuple-element.46.refs_4_) | copy-start | bytes 786436
  97.8 2.0 copy-start.11
  99.8 2.2 copy-start.12
  128.7 1.3 copy-start.13
  158.6 6.8 %copy-start.17 = (bf16[64,2048]{1,0:T(8,128)(2,1)}, bf16[64,2048]{1,0:T(8,128)(2,1)S(1)}, u32[]{:S(2)}) copy-start(bf16[64,2048]{1,0:T(8,128)(2,1)S(1)} %fusion.39) | copy-start | bytes 786436
  163.7 126.7 %all-gather.17.cloned.1.call-start = ((), (), s32[]{:S(2)}) async-start(), calls=%async_computation.3 | async-start | bytes 8650752 | tf_op jit(solution)/shard_map/all_gather | solution.py:621
  164.5 133.1 %all-gather.19.cloned.1.call-start = ((), (), s32[]{:S(2)}) async-start(), calls=%async_computation.4 | async-start | bytes 8650752 | tf_op jit(solution)/shard_map/all_gather | solution.py:621
  165.3 181.5 %all-gather.13.cloned.1.call-start = ((), (), s32[]{:S(2)}) async-start(), calls=%async_computation.1 | async-start | bytes 8650752 | tf_op jit(solution)/shard_map/all_gather | solution.py:621
  192.2 203.8 %all-gather.15.cloned.1.call-start = ((), (), s32[]{:S(2)}) async-start(), calls=%async_computation.2 | async-start | bytes 8650752 | tf_op jit(solution)/shard_map/all_gather | solution.py:621
  192.2 1.6 copy-start.14
  227.4 32.2 %copy-start.18 = (bf16[64,2048]{1,0:T(8,128)(2,1)S(1)}, bf16[64,2048]{1,0:T(8,128)(2,1)}, u32[]{:S(2)}) copy-start(bf16[64,2048]{1,0:T(8,128)(2,1)} %copy-done.17) | copy-start | bytes 786436
  297.5 3.4 copy-start.5
  300.9 3.4 copy-start.7
  304.3 1.6 copy-start.9
  305.9 90.0 %copy-start.10 = (bf16[16,64,1024]{2,1,0:T(8,128)(2,1)S(1)}, bf16[16,64,1024]{2,1,0:T(8,128)(2,1)}, u32[]{:S(2)}) copy-start(bf16[16,64,1024]{2,1,0:T(8,128)(2,1)} %all-gather.11.cloned.1.call-done) | copy-start | bytes 6291460
  395.9 3.4 copy-start.6
  399.3 3.4 copy-start.8
Sparse Core Ops, SparseCore 0:
  163.8 27.7 all-gather.10
  194.2 53.6 all-gather.16
  250.0 47.5 all-gather.18
  299.5 47.2 all-gather.12
  348.7 47.1 all-gather.14

commit v5 on v4

--- a/solution.py
+++ b/solution.py
@@ -293,7 +293,8 @@
         c.wait_send()
 
 
-def _query_kernel(n_cols, q_ref, q_all, x_sem):
+def _query_kernel(n_cols, q_ref, q_all, done_ref, x_sem):
+    done_ref[...] = jnp.zeros_like(done_ref)
     _signal_all(_x_peers(n_cols))
     for _ in _q_gather(n_cols, q_ref, q_all, x_sem):
         pass
@@ -398,15 +399,28 @@
                 ml_ref[c, :, t] = flat[:, c]
 
 
-def _exchange_kernel(n_cols, n_rows, heads, dim, has_pages, *refs):
-    o_ref, ml_ref, q_ref, kv_ref = refs[:I4]
-    n_in = 6 if has_pages else I4
-    n_out = I2 if has_pages else I1
-    out_ref = refs[n_in]
-    rp_o, rp_ml, cur_o, cur_ml, rel_o, rel_ml, fin_o, fin_ml, spread, expand, p_sem, r_sem, y_sem = refs[n_in + n_out:]
+def _exchange_kernel(n_cols, n_rows, heads, dim, layer, has_pages, *refs):
+    o_ref, ml_ref, q_ref, kv_ref, hid_ref, wo_ref, up_ref, down_ref = refs[:8]
+    n_in = 10 if has_pages else 8
+    n_out = I3 if has_pages else I2
+    out_ref, done_ref = refs[n_in:n_in + I2]
+    done_ref[...] = jnp.zeros_like(done_ref)
+    rp_o, rp_ml, cur_o, cur_ml, rel_o, rel_ml, fin_o, fin_ml, spread, expand, p_sem, r_sem, y_sem = refs[n_in + n_out:n_in + n_out + 13]
+    own_o, own_ml, attn_s, mid_s, acc_s, wo_buf, up_buf, down_buf, own_sem, w_sem = refs[n_in + n_out + 13:]
     n_x = n_cols // I2
     home = q_ref.shape[I0] // I2
     width = heads * dim
+    n_buf, _, ff = up_buf.shape
+    n_ff = up_ref.shape[I2] // ff
+
+    def weights(c, slot):
+        cols = pl.ds(pl.multiple_of(c * ff, ff), ff)
+        return (
+            pltpu.make_async_copy(up_ref.at[layer, :, cols], up_buf.at[slot], w_sem.at[I0, slot]),
+            pltpu.make_async_copy(down_ref.at[layer, cols, :], down_buf.at[slot], w_sem.at[I1, slot]),
+        )
+
+    wo_copy = pltpu.make_async_copy(wo_ref.at[layer], wo_buf, own_sem.at[I0])
     at = lax.axis_index('kv')
     x, core = at // I2, at % I2
     up, dn, far = (x + I1) % n_x, (x + n_x - I1) % n_x, (x + I2) % n_x
@@ -419,8 +433,18 @@
         pals.append(_copy(ml_ref.at[I1 - core, pos], rp_ml.at[i], p_sem, I4 + i, to_pal))
     for c in pals:
         c.start()
+    owns = []
+    for i, pos in enumerate(order):
+        owns.append(pltpu.make_async_copy(o_ref.at[core, pos], own_o.at[i], own_sem.at[I1 + i]))
+        owns.append(pltpu.make_async_copy(ml_ref.at[core, pos], own_ml.at[i], own_sem.at[I5 + i]))
+    for c in owns:
+        c.start()
+    wo_copy.start()
+    for b in range(n_buf):
+        for c in weights(b, b):
+            c.start()
     if has_pages:
-        pages_ref, pages_all = refs[I4:n_in], refs[n_in + I1]
+        pages_ref, pages_all = refs[8:n_in], refs[n_in + I2]
         y_start, y_forward, y_finish = _rows_on_y(pages_ref, pages_all, y_sem, _half0)
         y_start()
         for h, ref in enumerate(pages_ref):
@@ -464,18 +488,24 @@
         out_ml[:, I0:heads] = top
         out_ml[:, heads:I2 * heads] = aw * al + bw * bl
         w = jnp.concatenate([aw, bw], axis=I0)
-        for c in range(n_chunk):
-            wx = widen(w, c)
-            sl = slice(c * cw, (c + I1) * cw)
+
+        def chunk(c, _):
+            sl = pl.ds(pl.multiple_of(c * cw, cw), cw)
+            wx = _pick_lhs(w, spread[:, sl], NN)
             out_o[:, sl] = a_o[:, sl] * wx[I0:home] + b_o[:, sl] * wx[home:]
+            return c
+
+        lax.fori_loop(I0, n_chunk, chunk, I0)
 
     cur_ml[...] = jnp.zeros_like(cur_ml)
 
     def fold_pal(i):
         _copy(o_ref.at[I1 - core, order[i]], rp_o.at[i], p_sem, i, to_pal).wait_recv()
         _copy(ml_ref.at[I1 - core, order[i]], rp_ml.at[i], p_sem, I4 + i, to_pal).wait_recv()
+        owns[I2 * i].wait()
+        owns[I2 * i + I1].wait()
         for t in range(I2):
-            fold(o_ref.at[core, order[i], t], ml_ref.at[core, order[i], t], rp_o.at[i, t], rp_ml.at[i, t], cur_o.at[i, t], cur_ml.at[i, t])
+            fold(own_o.at[i, t], own_ml.at[i, t], rp_o.at[i, t], rp_ml.at[i, t], cur_o.at[i, t], cur_ml.at[i, t])
 
     sends = []
 
@@ -528,16 +558,43 @@
                 acc = acc + o[:, sl] * wx[i * home:(i + I1) * home]
             for i, (step, _) in enumerate(self_w[t]):
                 acc = acc + v_c[step * home:(step + I1) * home] * wx[(I3 + i) * home:(I4 + i) * home]
-            out_ref[t * home:(t + I1) * home, sl] = acc.astype(BF16)
+            attn_s[t * home:(t + I1) * home, sl] = acc.astype(BF16)
     if has_pages:
         y_finish()
+    wo_copy.wait()
+
+    def mix(c, _):
+        sl = pl.ds(pl.multiple_of(c * cw, cw), cw)
+        mid_s[:, sl] = (hid_ref[:, sl].astype(F32) + _dot(attn_s[...], wo_buf[:, sl], NN)).astype(BF16)
+        acc_s[:, sl] = jnp.zeros((I2 * home, cw), F32)
+        return c
+
+    lax.fori_loop(I0, n_chunk, mix, I0)
+
+    def mlp(c, _):
+        slot = c % n_buf
+        up, down = weights(c, slot)
+        up.wait()
+        act = jax.nn.gelu(_dot(mid_s[...], up_buf[slot], NN)).astype(BF16)
+        down.wait()
+        acc_s[...] += _dot(act, down_buf[slot], NN)
+
+        @pl.when(c + n_buf < n_ff)
+        def _():
+            for w in weights(c + n_buf, slot):
+                w.start()
+
+        return c
+
+    lax.fori_loop(I0, n_ff, mlp, I0)
+    out_ref[...] = (mid_s[...].astype(F32) + acc_s[...]).astype(BF16)
     for c in pals + sends:
         c.wait_send()
 
 
 def _place_kernel(steps, heads, n_alias, *refs):
     kn_ref, vn_ref, k_ref, v_ref, mk_ref, mv_ref, wsel_ref, mig_ref, info_ref = refs[:9]
-    ko_ref, vo_ref, kv_s, full = refs[9 + n_alias:]
+    ko_ref, vo_ref, kv_s, full = refs[11 + n_alias:]
     page, _, dim, n_slots = k_ref.shape[1:]
     n_seq = wsel_ref.shape[0]
     width = page * dim
@@ -547,21 +604,27 @@
     for t in range(steps):
         for which, ref in enumerate((kn_ref, vn_ref)):
             kv_s[which, t] = _dot(ref[:, 0, t].reshape(n_seq, heads * dim), wsel_ref[...], TN).astype(BF16)
-    for h in range(heads):
+
+    def head(h, _):
+        lanes = pl.ds(pl.multiple_of(h * width, width), width)
         for which, (pool, pages, out) in enumerate(((k_ref, mk_ref, ko_ref), (v_ref, mv_ref, vo_ref))):
-            full[...] = _dot(pages[:, :, h * width:(h + 1) * width].reshape(n_all, width), mig_ref[...], TN).astype(BF16).reshape(page, dim, n_slots)
-
-            def fill(tok, _, which=which, pool=pool, out=out, h=h):
+            full[...] = _dot(pages[:, :, lanes].reshape(n_all, width), mig_ref[...], TN).astype(BF16).reshape(page, dim, n_slots)
+
+            def fill(tok, _, which=which, pool=pool, out=out):
                 at = w_off - tok.astype(F32)
                 new = [jnp.where(at == -float(t), 1.0, 0.0) for t in range(steps)]
                 kept = 1.0 - functools.reduce(jnp.add, new)
                 val = full[tok] * kept.astype(BF16) + pool[0, tok, h] * (kept * (1.0 - moved)).astype(BF16)
+                rows = pl.ds(pl.multiple_of(h * dim, dim), dim)
                 for t in range(steps):
-                    val = val + kv_s[which, t, h * dim:(h + 1) * dim, :] * new[t].astype(BF16)
+                    val = val + kv_s[which, t, rows, :] * new[t].astype(BF16)
                 out[0, tok, h] = val
                 return 0
 
             lax.fori_loop(0, page, fill, 0, unroll=2)
+        return 0
+
+    lax.fori_loop(0, heads, head, 0)
 
 
 def solution(mesh):
@@ -574,7 +637,8 @@
     vec_spec = P(dev_axes)
     full_spec = P()
     pair = 2
-    vmem = pl.BlockSpec(memory_space=pltpu.VMEM)
+    vmem, hbm = pl.BlockSpec(memory_space=pltpu.VMEM), pl.BlockSpec(memory_space=pl.ANY)
+    n_buf, ff = 8, 512
     dma = pltpu.SemaphoreType.DMA
 
     def per_device(x_embed, w_query, w_key, w_value, w_out, w_up, w_down, k_pool, v_pool, old_table, seq_len, src_slot, dst_slot):
@@ -618,7 +682,8 @@
         )(src_hot, *[a for _ in range(layers) for a in (k_t, v_t)])
 
         def whole(i, after):
-            return lax.all_gather(lax.optimization_barrier((packed[i], after))[0], group_axes)
+            page, token = lax.optimization_barrier((packed[i], after))
+            return lax.all_gather(page, group_axes), token
 
         def project(hidden, layer):
             q = jnp.dot(hidden, w_query[layer], preferred_element_type=F32).astype(BF16)
@@ -639,6 +704,7 @@
         tab = jnp.concatenate([old_table.T.reshape(-1), seq_len])[None, :]
         meta = jnp.concatenate([jnp.where(jnp.arange(8, dtype=I32)[:, None] == 0, tab, 0), own_place(src_slot), own_place(dst_slot)], axis=0)
         pages_all_shape = jax.ShapeDtypeStruct((n_rows,) + page_shape, BF16)
+        done_shape = jax.ShapeDtypeStruct((8, 128), F32)
         q_all_shape = jax.ShapeDtypeStruct((n_cols, rows, heads * dim), BF16)
         dims = (n_rows, n_cols, n_slots, n_pages, page, seq_dev)
         pages_y, q_all, q_sel, cells, arr, info, w_sel, mig, w_info = pl.pallas_call(
@@ -692,19 +758,19 @@
                     pltpu.VMEM((2 * n_rt, LANES), F32),
                     pltpu.VMEM((steps, ml_rows, n_seq), F32),
                 ],
-                compiler_params=pltpu.CompilerParams(vmem_limit_bytes=32 * MIB),
+                compiler_params=pltpu.CompilerParams(vmem_limit_bytes=60 * MIB),
                 cost_estimate=_cost(20, 16),
                 name='slot_attention',
             )(q_all.reshape(n_cols, steps, seq_dev, heads * dim), k_t, v_t, pages, pages, q_sel, cells, arr, info)
 
-        def exchange(layer, o, ml, q, kv, pages):
+        def exchange(layer, o, ml, q, kv, hidden, pages):
             has = pages is not None
             half = (seq_dev, heads * dim)
             stat = (seq_dev, ml.shape[-1])
-            out_shape = [jax.ShapeDtypeStruct((rows, heads * dim), BF16)] + ([pages_all_shape] if has else [])
+            out_shape = [jax.ShapeDtypeStruct((rows, width), BF16), done_shape] + ([pages_all_shape] if has else [])
             return pl.pallas_call(
-                functools.partial(_exchange_kernel, n_cols, n_rows, heads, dim, has),
-                in_specs=[vmem] * (6 if has else 4),
+                functools.partial(_exchange_kernel, n_cols, n_rows, heads, dim, layer, has),
+                in_specs=[hbm, hbm, vmem, vmem, vmem, hbm, hbm, hbm] + [vmem] * (2 if has else 0),
                 out_specs=[vmem] * len(out_shape),
                 out_shape=out_shape,
                 scratch_shapes=[
@@ -714,21 +780,25 @@
                     pltpu.VMEM((2, steps) + half, F32), pltpu.VMEM((2, steps) + stat, F32),
                     pltpu.VMEM((heads, heads * dim), BF16), pltpu.VMEM((kv_w, q_w), BF16),
                     dma((2, 8)), dma((2, 12)), dma((2, 6)),
+                    pltpu.VMEM((4, steps) + half, F32), pltpu.VMEM((4, steps) + stat, F32),
+                    pltpu.VMEM((rows, heads * dim), BF16), pltpu.VMEM((rows, width), BF16), pltpu.VMEM((rows, width), F32),
+                    pltpu.VMEM(w_out.shape[1:], BF16), pltpu.VMEM((n_buf, width, ff), BF16), pltpu.VMEM((n_buf, ff, width), BF16),
+                    dma((9,)), dma((2, n_buf)),
                 ],
-                compiler_params=pltpu.CompilerParams(collective_id=1 + layer, has_side_effects=True, vmem_limit_bytes=32 * MIB),
+                compiler_params=pltpu.CompilerParams(collective_id=1 + layer, has_side_effects=True, vmem_limit_bytes=56 * MIB),
                 cost_estimate=_cost(10, 4),
                 name='exchange_partials',
-            )(o, ml, q, kv, *(pages if has else []))
-
-        kv_all, moved = [], []
+            )(o, ml, q, kv, hidden, w_out, w_up, w_down, *(pages if has else []))
+
+        kv_all, moved, done = [], [], info
         for layer in range(layers):
             if layer:
                 q, kv = project(hidden, layer)
-                [q_all] = pl.pallas_call(
+                q_all, done = pl.pallas_call(
                     functools.partial(_query_kernel, n_cols),
                     in_specs=[vmem],
-                    out_specs=[vmem],
-                    out_shape=[q_all_shape],
+                    out_specs=[vmem] * 2,
+                    out_shape=[q_all_shape, done_shape],
                     scratch_shapes=[dma((2, 13))],
                     compiler_params=pltpu.CompilerParams(collective_id=1 + layers + layer, has_side_effects=True, vmem_limit_bytes=16 * MIB),
                     cost_estimate=_cost(5, 4),
@@ -740,17 +810,15 @@
                 kv_rows = kv_rows.reshape(n_cols, layers, steps, seq_dev, -1)
             o, ml = attend(layer, q_all, pages_y)
             nxt = packed[2 * (layer + 1):2 * (layer + 2)] if layer + 1 < layers else None
-            moved.append(whole(2 * layer, q_all))
-            attn, *more = exchange(layer, o, ml, q, kv, nxt)
+            moved.append(whole(2 * layer, done))
+            hidden, done, *more = exchange(layer, o, ml, q, kv, hidden, nxt)
             pages_y = more[0] if more else None
-            moved.append(whole(2 * layer + 1, attn))
-            hidden = (hidden.astype(F32) + jnp.dot(attn, w_out[layer], preferred_element_type=F32)).astype(BF16)
-            up_act = jax.nn.gelu(jnp.dot(hidden, w_up[layer], preferred_element_type=F32)).astype(BF16)
-            hidden = (hidden.astype(F32) + jnp.dot(up_act, w_down[layer], preferred_element_type=F32)).astype(BF16)
+            moved.append(whole(2 * layer + 1, done))
         v_at = kv_heads * dim // kv_w
         outs = []
         for layer in range(layers):
             blk = pool_blk(layer)
+            pages, tokens = zip(*moved[2 * layer:2 * layer + 2])
             specs = [
                 pl.BlockSpec((n_cols, 1, steps, seq_dev, kv_w), lambda i, layer=layer: (0, layer, 0, 0, i)),
                 pl.BlockSpec((n_cols, 1, steps, seq_dev, kv_w), lambda i, layer=layer: (0, layer, 0, 0, v_at + i)),
@@ -759,15 +827,15 @@
             outs = pl.pallas_call(
                 functools.partial(_place_kernel, steps, pair, len(outs)),
                 grid=(n_grid,),
-                in_specs=specs + [pl.BlockSpec(memory_space=pl.ANY)] * len(outs),
+                in_specs=specs + [pl.BlockSpec(memory_space=pl.ANY)] * (2 + len(outs)),
                 out_specs=[blk, blk],
                 out_shape=[jax.ShapeDtypeStruct(a.shape, BF16) for a in (k_t, v_t)],
                 scratch_shapes=[pltpu.VMEM((2, steps, kv_w, n_slots), BF16), pltpu.VMEM((page, dim, n_slots), BF16)],
-                input_output_aliases={len(specs) + i: i for i in range(len(outs))},
-                compiler_params=pltpu.CompilerParams(vmem_limit_bytes=32 * MIB),
+                input_output_aliases={len(specs) + 2 + i: i for i in range(len(outs))},
+                compiler_params=pltpu.CompilerParams(vmem_limit_bytes=60 * MIB),
                 cost_estimate=_cost(20, 32),
                 name='place_pages',
-            )(kv_rows, kv_rows, k_t, v_t, moved[2 * layer], moved[2 * layer + 1], w_sel, mig, w_info, *outs)
+            )(kv_rows, kv_rows, k_t, v_t, *pages, w_sel, mig, w_info, *tokens, *outs)
         k_out, v_out = outs
         y_out = hidden.reshape(steps, seq_dev, width)
         back = (4, 0, 1, 2, 3)

time: 437 us -> 420 us (0.961); the launches traced: 429 us -> 419 us
  matrix products: 77.8 us -> 17.9 us
  Pallas kernels: 229 us -> 282 us
  local copies, waits for them, and re-layouts: 27.2 us -> 14.7 us
  waiting for transfers between devices: 78.4 us -> 87.3 us
    dot_general x4 -> x0, matrix products: 59.3 us -> none  [the longest x2 49.3 us: per_device(): jnp.dot(up_act, w_down[layer], preferred_element_type=F32)]
    pallas_call x2, Pallas kernels: 58.8 us -> 106 us  [exchange(): pl.pallas_call(functools.partial(_exchange_kernel, n_cols, n_rows, heads,...]
    unnamed x38 -> x43, local copies, waits for them, and re-layouts: 24.2 us -> 11.7 us
    all_gather x4, waiting for transfers between devices: 76.7 us -> 85.7 us  [whole(): return (lax.all_gather(page, group_axes), token)]
  transfers between devices with their start and end apart: 5 -> 5, of which waited for: 3 -> 3; matrix products, arithmetic and copies ran while one was open for 8% -> 1% of each run, Pallas kernels for 25% -> 32%
where the time goes in v5:
time: 420 us; the launch traced here: 419 us
  Pallas kernels  282 us (67%)
  waiting for transfers between devices  87.3 us (21%)
  matrix products  17.9 us (4%)
  local copies, waits for them, and re-layouts  14.7 us (4%)
  between operations  14.1 us (3%)
    pallas_call x2, Pallas kernels, exchange(): pl.pallas_call(functools.partial(_exchange_kernel, n_cols, n_rows, heads,...  106 us
    all_gather x4, waiting for transfers between devices, whole(): return (lax.all_gather(page, group_axes), token)  85.7 us
    pallas_call x2, Pallas kernels, attend(): pl.pallas_call(functools.partial(_attn_kernel, steps, group, pair), grid=...  68.8 us
    pallas_call x2, Pallas kernels, per_device(): pl.pallas_call(functools.partial(_place_kernel, steps, pair, len(outs)),...  43 us
    pallas_call x1, Pallas kernels, per_device(): pl.pallas_call(functools.partial(_head_kernel, dims), in_specs=[vmem] * 6...  31.8 us
    pallas_call x1, Pallas kernels, per_device(): pl.pallas_call(functools.partial(_query_kernel, n_cols), in_specs=[vmem],...  23.1 us
    unnamed x43, local copies, waits for them, and re-layouts  11.7 us
    dot_general x2, matrix products, project(): q = jnp.dot(hidden, w_query[layer], preferred_element_type=F32).astype(BF16)  9.91 us
  transfers between devices with their start and end apart: 5, of which 3 were waited for; matrix products, arithmetic and copies ran while one was open for 1% of the time, Pallas kernels for 32%

profile of v5, /device:TPU:97, one launch (start us, length us, event | category | flops | bytes accessed | tf_op | source)
XLA Modules:
  0.0 419.5 jit_solution(13268022142969016971)
XLA Ops:
  7.2 0.0 copy-start.16
  7.2 0.1 all-gather.11.cloned.1.call-start
  7.3 0.8 reshape.83
  8.1 0.7 tile.7
  8.7 0.1 broadcast_in_dim.53
  8.8 0.7 broadcast_subtract_fusion
  9.5 0.7 tile.6
  10.1 0.1 broadcast_in_dim.51
  10.2 0.7 fusion.36.onehot_ref
  10.9 0.7 copy.19.mysrcc_ref
  11.6 2.2 fusion.27
  13.8 2.2 fusion.24
  16.0 0.0 copy-start.20
  16.0 5.0 %fusion.6.q_ref.refs_2_ = bf16[64,2048]{1,0:T(8,128)(2,1)S(1)} fusion(bf16[64,2048]{1,0:T(8,128)(2,1)S(1)} %bitcast.75, bf16[2,2048,2048]{2,1,0:T(8,128)(2,1)} %param.14), kind=kOutput, calls=%fused_computation.6 | convolution fusion | flops 537001984 | bytes 8912896 | tf_op jit(solution)/shard_map/dot_general | solution.py:689
  21.0 0.1 pad_add_fusion.1
  21.0 0.7 fusion.39
  21.7 0.1 and_select_fusion.1
  21.8 9.0 %pack_pages.1 = (bf16[16,8192]{1,0:T(8,128)(2,1)}, bf16[16,8192]{1,0:T(8,128)(2,1)}, bf16[16,8192]{1,0:T(8,128)(2,1)}, bf16[16,8192]{1,0:T(8,128)(2,1)}) custom-call(bf16[16,208]{1,0:T(8,128)(2,1)} %fusion.36.onehot_ref, bf16[2,16,8,64,208]{4,3,2,1,0:T(8,128)(2,1)} %bitcast.60, bf16[2,16,8,64,208]{4,3,2,1,0:T(8,128)(2,1)} %bitcast.66, ...), custom_call_target="tpu_custom_call" | custom-call | flops 8000000000 | bytes 16777216 | tf_op jit(solution)/shard_map/pack_pages/pallas_call | solution.py:674
  30.8 0.0 copy-done.4
  30.8 0.0 copy-start.2
  30.8 0.9 copy-done.2
  31.8 0.9 copy-done.3
  32.7 31.8 %head_gather.1 = (bf16[4,2,16,8192]{3,2,1,0:T(8,128)(2,1)S(1)}, bf16[8,64,2048]{2,1,0:T(8,128)(2,1)S(1)}, bf16[256,256]{1,0:T(8,128)(2,1)S(1)}, bf16[768,256]{1,...) custom-call(s32[24,128]{1,0:T(8,128)S(1)} %pad_add_fusion.meta_ref, ...), custom_call_target="tpu_custom_call" | custom-call | flops 10000000000 | bytes 4194304 | tf_op jit(solution)/shard_map/head_gather/pallas_call | solution.py:710
  64.6 0.0 copy-start.6
  64.6 1.3 copy-done.6
  65.9 1.3 copy-done.7
  67.2 0.7 copy-done.8
  67.9 0.6 copy-done.9
  68.6 0.7 copy-done.10
  69.3 0.6 copy-done.11
  70.0 0.6 copy-done.12
  70.6 0.6 copy-done.13
  71.1 0.6 copy-done.15
  71.7 34.4 %slot_attention.2 = (f32[2,4,2,32,2048]{4,3,2,1,0:T(8,128)}, f32[2,4,2,32,128]{4,3,2,1,0:T(8,128)}) custom-call(bf16[8,2,32,2048]{3,2,1,0:T(8,128)(2,1)} %bitcast.59, bf16[2,16,8,64,208]{4,3,2,1,0:T(8,128)(2,1)} %bitcast.62, bf16[2,16,8,64,208]{4,3,2,1,0:T(8,128)(2,1)} %bitcast.68, bf16[4,2,16,8192]{3,2,1,0:T(8,128)(2,1)} %copy-done.7, ...), custom_call_target="tpu_custom_call" | custom-call | flops 20000000000 | bytes 16777216 | tf_op jit(solution)/shard_map/slot_attention/pallas_call | solution.py:734
  106.1 51.5 %exchange_partials.2 = (bf16[64,2048]{1,0:T(8,128)(2,1)}, f32[8,128]{1,0:T(8,128)}, bf16[4,2,16,8192]{3,2,1,0:T(8,128)(2,1)}) custom-call(f32[2,4,2,32,2048]{4,3,2,1,0:T(8,128)} %get-tuple-element.47.refs_0_, f32[2,4,2,32,128]{4,3,2,1,0:T(8,128)} %get-tuple-element.48.refs_1_, bf16[64,2048]{1,0:T(8,128)(2,1)} %copy-done, ...), custom_call_target="tpu_custom_call" | custom-call | flops 10000000000 | bytes 4194304 | tf_op jit(solution)/shard_map/exchange_partials/pallas_call | solution.py:771
  157.6 1.5 fusion.33
  159.1 2.2 fusion.30
  161.3 0.7 fusion.38
  162.0 0.7 pad_maximum_fusion
  162.7 0.1 all-gather.11.cloned.1.call-update
  162.8 0.1 all-gather.17.cloned.1.call-start
  162.8 0.7 all-gather.17.cloned.1.call-update
  163.6 0.1 all-gather.19.cloned.1.call-start
  163.7 0.7 all-gather.19.cloned.1.call-update
  164.4 0.1 all-gather.13.cloned.1.call-start
  164.5 5.0 %fusion.9.q_ref.refs_2_ = bf16[64,2048]{1,0:T(8,128)(2,1)S(1)} fusion(bf16[64,2048]{1,0:T(8,128)(2,1)S(1)} %copy-done.17, bf16[2,2048,2048]{2,1,0:T(8,128)(2,1)} %param.14), kind=kOutput, calls=%fused_computation.7 | convolution fusion | flops 537001984 | bytes 8912896 | tf_op jit(solution)/shard_map/dot_general | solution.py:689
  169.4 23.1 %query_gather.1 = (bf16[8,64,2048]{2,1,0:T(8,128)(2,1)S(1)}, f32[8,128]{1,0:T(8,128)S(1)}) custom-call(bf16[64,2048]{1,0:T(8,128)(2,1)S(1)} %fusion.9.q_ref.refs_2_), custom_call_target="tpu_custom_call" | custom-call | flops 5000000000 | bytes 4194304 | tf_op jit(solution)/shard_map/query_gather/pallas_call | solution.py:797
  192.5 0.0 copy-start.5
  192.5 1.3 copy-done.5
  193.8 0.6 copy-done.14
  194.4 0.1 all-gather.13.cloned.1.call-update
  194.5 0.1 all-gather.15.cloned.1.call-start
  194.6 34.4 %slot_attention.3 = (f32[2,4,2,32,2048]{4,3,2,1,0:T(8,128)}, f32[2,4,2,32,128]{4,3,2,1,0:T(8,128)}) custom-call(bf16[8,2,32,2048]{3,2,1,0:T(8,128)(2,1)} %bitcast.58, bf16[2,16,8,64,208]{4,3,2,1,0:T(8,128)(2,1)} %bitcast.63, bf16[2,16,8,64,208]{4,3,2,1,0:T(8,128)(2,1)} %bitcast.69, bf16[4,2,16,8192]{3,2,1,0:T(8,128)(2,1)} %get-tuple-element.53.mk_ref.mv_ref, ...), custom_call_target="tpu_custom_call" | custom-call | flops 20000000000 | bytes 16777216 | tf_op jit(solution)/shard_map/slot_attention/pallas_call | solution.py:734
  229.0 54.5 %exchange_partials.3 = (bf16[64,2048]{1,0:T(8,128)(2,1)}, f32[8,128]{1,0:T(8,128)}) custom-call(f32[2,4,2,32,2048]{4,3,2,1,0:T(8,128)} %get-tuple-element.54.refs_0_, f32[2,4,2,32,128]{4,3,2,1,0:T(8,128)} %get-tuple-element.55.refs_1_, bf16[64,2048]{1,0:T(8,128)(2,1)} %copy-done.1, bf16[64,1024]{1,0:T(8,128)(2,1)} %get-tuple-element.78.refs_3_, ...), custom_call_target="tpu_custom_call" | custom-call | flops 10000000000 | bytes 4194304 | tf_op jit(solution)/shard_map/exchange_partials/pallas_call | solution.py:771
  283.4 0.1 all-gather.15.cloned.1.call-update
  283.5 0.0 all-gather.11.cloned.1.call-done
  283.5 0.0 all-gather.17.cloned.1.call-done
  283.6 9.0 %all-gather.19.cloned.1.call-done = bf16[512,8192]{1,0:T(8,128)(2,1)} async-done(((bf16[16,8192]{1,0:T(8,128)(2,1)}), bf16[512,8192]{1,0:T(8,128)(2,1)}) %all-gather.19.cloned.1.call-update) | async-done | bytes 8388624 | tf_op jit(solution)/shard_map/all_gather | solution.py:686
  292.5 21.5 %place_pages.2 = (bf16[2,16,8,64,208]{4,3,2,1,0:T(8,128)(2,1)}, bf16[2,16,8,64,208]{4,3,2,1,0:T(8,128)(2,1)}) custom-call(bf16[8,2,2,32,1024]{4,3,2,1,0:T(8,128)(2,1)} %bitcast.82, bf16[8,2,2,32,1024]{4,3,2,1,0:T(8,128)(2,1)} %bitcast.83, bf16[2,16,8,64,208]{4,3,2,1,0:T(8,128)(2,1)} %bitcast.64, bf16[2,16,8,64,208]{4,3,2,1,0:T(8,128)(2,1)} %bitcast.70, ...), custom_call_target="tpu_custom_call" | custom-call | flops 20000000000 | bytes 33554432 | tf_op jit(solution)/shard_map/place_pages/pallas_call | solution.py:827
  314.0 27.5 %all-gather.13.cloned.1.call-done = bf16[512,8192]{1,0:T(8,128)(2,1)} async-done(((bf16[16,8192]{1,0:T(8,128)(2,1)}), bf16[512,8192]{1,0:T(8,128)(2,1)}) %all-gather.13.cloned.1.call-update) | async-done | bytes 8388624 | tf_op jit(solution)/shard_map/all_gather | solution.py:686
  341.5 49.2 %all-gather.15.cloned.1.call-done = bf16[512,8192]{1,0:T(8,128)(2,1)} async-done(((bf16[16,8192]{1,0:T(8,128)(2,1)}), bf16[512,8192]{1,0:T(8,128)(2,1)}) %all-gather.15.cloned.1.call-update) | async-done | bytes 8388624 | tf_op jit(solution)/shard_map/all_gather | solution.py:686
  390.7 21.5 %place_pages.3 = (bf16[2,16,8,64,208]{4,3,2,1,0:T(8,128)(2,1)}, bf16[2,16,8,64,208]{4,3,2,1,0:T(8,128)(2,1)}) custom-call(bf16[8,2,2,32,1024]{4,3,2,1,0:T(8,128)(2,1)} %bitcast.84, bf16[8,2,2,32,1024]{4,3,2,1,0:T(8,128)(2,1)} %bitcast.85, bf16[2,16,8,64,208]{4,3,2,1,0:T(8,128)(2,1)} %bitcast.65, ...), custom_call_target="tpu_custom_call", output_to_operand_aliasing={{0}: (11, {}), {1}: (12, {})} | custom-call | flops 20000000000 | bytes 33554432 | tf_op jit(solution)/shard_map/place_pages/pallas_call | solution.py:827
  412.2 0.0 copy-done.18
  412.2 0.7 copy.23
  (26 shorter events, 0.1 us)
Async XLA Ops:
  7.2 8.8 %copy-start.16 = (bf16[2,32,2048]{2,1,0:T(8,128)(2,1)S(1)}, bf16[2,32,2048]{2,1,0:T(8,128)(2,1)}, u32[]{:S(2)}) copy-start(bf16[2,32,2048]{2,1,0:T(8,128)(2,1)} %param.13) | copy-start | bytes 786436
  7.2 276.3 %all-gather.11.cloned.1.call-start = ((), (), s32[]{:S(2)}) async-start(), calls=%async_computation | async-start | bytes 2359296 | tf_op jit(solution)/shard_map/all_gather | solution.py:809
  16.0 5.0 %copy-start.20 = (s32[32]{0:T(128)S(1)}, s32[32]{0:T(128)}, u32[]{:S(2)}) copy-start(s32[32]{0:T(128)} %param.23) | copy-start | bytes 388
  21.0 9.8 %copy-start = (bf16[64,2048]{1,0:T(8,128)(2,1)}, bf16[64,2048]{1,0:T(8,128)(2,1)S(1)}, u32[]{:S(2)}) copy-start(bf16[64,2048]{1,0:T(8,128)(2,1)S(1)} %fusion.6.q_ref.refs_2_) | copy-start | bytes 786436
  21.8 9.0 %copy-start.4 = (s32[16]{0:T(128)S(1)}, s32[16]{0:T(128)}, u32[]{:S(2)}) copy-start(s32[16]{0:T(128)} %param.24) | copy-start | bytes 196
  30.8 1.0 copy-start.2
  31.7 0.9 copy-start.3
  64.6 1.3 copy-start.6
  65.9 1.3 copy-start.7
  67.2 0.7 copy-start.8
  67.9 0.6 copy-start.9
  68.6 0.8 copy-start.10
  69.3 0.6 copy-start.11
  69.9 0.6 copy-start.12
  70.5 0.6 copy-start.13
  71.1 0.6 copy-start.15
  106.1 51.5 %copy-start.19 = (bf16[2,2048,512]{2,1,0:T(8,128)(2,1)S(1)}, bf16[2,2048,512]{2,1,0:T(8,128)(2,1)}, u32[]{:S(2)}) copy-start(bf16[2,2048,512]{2,1,0:T(8,128)(2,1)} %param.16) | copy-start | bytes 12582916
  157.6 6.8 %copy-start.17 = (bf16[64,2048]{1,0:T(8,128)(2,1)S(1)}, bf16[64,2048]{1,0:T(8,128)(2,1)}, u32[]{:S(2)}) copy-start(bf16[64,2048]{1,0:T(8,128)(2,1)} %get-tuple-element.51.refs_4_) | copy-start | bytes 786436
  162.8 120.8 %all-gather.17.cloned.1.call-start = ((), (), s32[]{:S(2)}) async-start(), calls=%async_computation.3 | async-start | bytes 8650752 | tf_op jit(solution)/shard_map/all_gather | solution.py:686
  163.6 128.9 %all-gather.19.cloned.1.call-start = ((), (), s32[]{:S(2)}) async-start(), calls=%async_computation.4 | async-start | bytes 8650752 | tf_op jit(solution)/shard_map/all_gather | solution.py:686
  164.4 177.1 %all-gather.13.cloned.1.call-start = ((), (), s32[]{:S(2)}) async-start(), calls=%async_computation.1 | async-start | bytes 8650752 | tf_op jit(solution)/shard_map/all_gather | solution.py:686
  169.4 23.1 %copy-start.1 = (bf16[64,2048]{1,0:T(8,128)(2,1)}, bf16[64,2048]{1,0:T(8,128)(2,1)S(1)}, u32[]{:S(2)}) copy-start(bf16[64,2048]{1,0:T(8,128)(2,1)S(1)} %fusion.9.q_ref.refs_2_) | copy-start | bytes 786436
  192.5 1.3 copy-start.5
  193.8 0.6 copy-start.14
  194.5 196.2 %all-gather.15.cloned.1.call-start = ((), (), s32[]{:S(2)}) async-start(), calls=%async_computation.2 | async-start | bytes 8650752 | tf_op jit(solution)/shard_map/all_gather | solution.py:686
  390.7 21.5 %copy-start.18 = (bf16[64,2048]{1,0:T(8,128)(2,1)S(1)}, bf16[64,2048]{1,0:T(8,128)(2,1)}, u32[]{:S(2)}) copy-start(bf16[64,2048]{1,0:T(8,128)(2,1)} %get-tuple-element.56) | copy-start | bytes 786436
Sparse Core Ops, SparseCore 0:
  162.9 29.1 all-gather.10
  194.7 46.7 all-gather.16
  243.6 48.8 all-gather.18
  294.5 47.0 all-gather.12
  343.5 47.1 all-gather.14

commit v6 on v4

--- a/solution.py
+++ b/solution.py
@@ -129,10 +129,11 @@
 
 
 def _pack_kernel(heads, onehot_ref, *refs):
-    half = len(refs) // 2
-    for src, out in zip(refs[:half], refs[half:]):
+    n_in = len(refs) * 2 // 3
+    for i, src in enumerate(refs[:n_in]):
         page, _, dim, n_slots = src.shape[1:]
         width = page * dim
+        out = refs[n_in + i // 2].at[i % 2]
         for h in range(heads):
             rows = src[0, :, h].reshape(width, n_slots)
             out[:, h * width:(h + 1) * width] = _dot(onehot_ref[...], rows, NT).astype(BF16)
@@ -257,13 +258,12 @@
 
 
 def _half0(ref, h):
-    return ref[h] if isinstance(ref, tuple) else ref.at[h]
-
-
-def _head_kernel(dims, meta_ref, kp_ref, vp_ref, q_ref, mysrc_ref, mysrcc_ref, pages_all, q_all, *refs):
+    return ref.at[h]
+
+
+def _head_kernel(dims, meta_ref, pages_ref, q_ref, mysrc_ref, mysrcc_ref, pages_all, q_all, *refs):
     tables, (meta_all, m_sem, y_sem, x_sem) = refs[:7], refs[7:]
     n_rows, n_cols = dims[:2]
-    pages_ref = (kp_ref, vp_ref)
     y, at = lax.axis_index('kv2'), lax.axis_index('kv')
     offsets = [(a, b) for a in range(n_rows) for b in range(n_cols) if (a, b) != (0, 0)]
     peers = [{'kv2': (y + a) % n_rows, 'kv': (at + b) % n_cols} for a, b in offsets]
@@ -277,8 +277,7 @@
     steps = _q_gather(n_cols, q_ref, q_all, x_sem)
     next(steps)
     meta_all[me] = meta_ref[...]
-    for h, ref in enumerate(pages_ref):
-        pages_all[y, h] = ref[...]
+    pages_all[y] = pages_ref[...]
     next(steps)
     forward()
     for k, (a, b) in enumerate(offsets):
@@ -400,9 +399,10 @@
 
 def _exchange_kernel(n_cols, n_rows, heads, dim, has_pages, *refs):
     o_ref, ml_ref, q_ref, kv_ref = refs[:I4]
-    n_in = 6 if has_pages else I4
-    n_out = I2 if has_pages else I1
-    out_ref = refs[n_in]
+    n_in = I5 if has_pages else I4
+    n_out = I3 if has_pages else I2
+    out_ref, done_ref = refs[n_in:n_in + I2]
+    done_ref[...] = jnp.zeros_like(done_ref)
     rp_o, rp_ml, cur_o, cur_ml, rel_o, rel_ml, fin_o, fin_ml, spread, expand, p_sem, r_sem, y_sem = refs[n_in + n_out:]
     n_x = n_cols // I2
     home = q_ref.shape[I0] // I2
@@ -420,11 +420,10 @@
     for c in pals:
         c.start()
     if has_pages:
-        pages_ref, pages_all = refs[I4:n_in], refs[n_in + I1]
+        pages_ref, pages_all = refs[I4], refs[n_in + I2]
         y_start, y_forward, y_finish = _rows_on_y(pages_ref, pages_all, y_sem, _half0)
         y_start()
-        for h, ref in enumerate(pages_ref):
-            pages_all[lax.axis_index('kv2'), h] = ref[...]
+        pages_all[lax.axis_index('kv2')] = pages_ref[...]
 
     n_chunk = I4
     cw = width // n_chunk
@@ -464,10 +463,14 @@
         out_ml[:, I0:heads] = top
         out_ml[:, heads:I2 * heads] = aw * al + bw * bl
         w = jnp.concatenate([aw, bw], axis=I0)
-        for c in range(n_chunk):
-            wx = widen(w, c)
-            sl = slice(c * cw, (c + I1) * cw)
+
+        def chunk(c, _):
+            sl = pl.ds(pl.multiple_of(c * cw, cw), cw)
+            wx = _pick_lhs(w, spread[:, sl], NN)
             out_o[:, sl] = a_o[:, sl] * wx[I0:home] + b_o[:, sl] * wx[home:]
+            return c
+
+        lax.fori_loop(I0, n_chunk, chunk, I0)
 
     cur_ml[...] = jnp.zeros_like(cur_ml)
 
@@ -537,7 +540,7 @@
 
 def _place_kernel(steps, heads, n_alias, *refs):
     kn_ref, vn_ref, k_ref, v_ref, mk_ref, mv_ref, wsel_ref, mig_ref, info_ref = refs[:9]
-    ko_ref, vo_ref, kv_s, full = refs[9 + n_alias:]
+    ko_ref, vo_ref, kv_s, full = refs[10 + n_alias:]
     page, _, dim, n_slots = k_ref.shape[1:]
     n_seq = wsel_ref.shape[0]
     width = page * dim
@@ -547,21 +550,27 @@
     for t in range(steps):
         for which, ref in enumerate((kn_ref, vn_ref)):
             kv_s[which, t] = _dot(ref[:, 0, t].reshape(n_seq, heads * dim), wsel_ref[...], TN).astype(BF16)
-    for h in range(heads):
+
+    def head(h, _):
+        lanes = pl.ds(pl.multiple_of(h * width, width), width)
         for which, (pool, pages, out) in enumerate(((k_ref, mk_ref, ko_ref), (v_ref, mv_ref, vo_ref))):
-            full[...] = _dot(pages[:, :, h * width:(h + 1) * width].reshape(n_all, width), mig_ref[...], TN).astype(BF16).reshape(page, dim, n_slots)
-
-            def fill(tok, _, which=which, pool=pool, out=out, h=h):
+            full[...] = _dot(pages[:, 0, :, lanes].reshape(n_all, width), mig_ref[...], TN).astype(BF16).reshape(page, dim, n_slots)
+
+            def fill(tok, _, which=which, pool=pool, out=out):
                 at = w_off - tok.astype(F32)
                 new = [jnp.where(at == -float(t), 1.0, 0.0) for t in range(steps)]
                 kept = 1.0 - functools.reduce(jnp.add, new)
                 val = full[tok] * kept.astype(BF16) + pool[0, tok, h] * (kept * (1.0 - moved)).astype(BF16)
+                rows = pl.ds(pl.multiple_of(h * dim, dim), dim)
                 for t in range(steps):
-                    val = val + kv_s[which, t, h * dim:(h + 1) * dim, :] * new[t].astype(BF16)
+                    val = val + kv_s[which, t, rows, :] * new[t].astype(BF16)
                 out[0, tok, h] = val
                 return 0
 
-            lax.fori_loop(0, page, fill, 0, unroll=2)
+            lax.fori_loop(0, page, fill, 0)
+        return 0
+
+    lax.fori_loop(0, heads, head, 0)
 
 
 def solution(mesh):
@@ -605,20 +614,21 @@
         def pool_blk(layer):
             return pl.BlockSpec((1, page, pair, dim, n_slots), lambda i: (layer, 0, i, 0, 0))
 
-        page_blk = pl.BlockSpec((n_move, m_w), lambda i: (0, i))
-        flat = jax.ShapeDtypeStruct((n_move, kv_heads * page_w), BF16)
+        page_blk = pl.BlockSpec((2, n_move, m_w), lambda i: (0, 0, i))
+        flat = jax.ShapeDtypeStruct(page_shape, BF16)
         packed = pl.pallas_call(
             functools.partial(_pack_kernel, pair),
             grid=(n_grid,),
             in_specs=[pl.BlockSpec((n_move, n_slots), lambda i: (0, 0))] + [pool_blk(l) for l in range(layers) for _ in (k_t, v_t)],
-            out_specs=[page_blk] * (2 * layers),
-            out_shape=[flat] * (2 * layers),
+            out_specs=[page_blk] * layers,
+            out_shape=[flat] * layers,
             cost_estimate=_cost(8, 16),
             name='pack_pages',
         )(src_hot, *[a for _ in range(layers) for a in (k_t, v_t)])
 
         def whole(i, after):
-            return lax.all_gather(lax.optimization_barrier((packed[i], after))[0], group_axes)
+            page, token = (packed[i], src_hot) if after is None else lax.optimization_barrier((packed[i], after))
+            return lax.all_gather(page, group_axes), token
 
         def project(hidden, layer):
             q = jnp.dot(hidden, w_query[layer], preferred_element_type=F32).astype(BF16)
@@ -639,11 +649,12 @@
         tab = jnp.concatenate([old_table.T.reshape(-1), seq_len])[None, :]
         meta = jnp.concatenate([jnp.where(jnp.arange(8, dtype=I32)[:, None] == 0, tab, 0), own_place(src_slot), own_place(dst_slot)], axis=0)
         pages_all_shape = jax.ShapeDtypeStruct((n_rows,) + page_shape, BF16)
+        done_shape = jax.ShapeDtypeStruct((8, 128), F32)
         q_all_shape = jax.ShapeDtypeStruct((n_cols, rows, heads * dim), BF16)
         dims = (n_rows, n_cols, n_slots, n_pages, page, seq_dev)
         pages_y, q_all, q_sel, cells, arr, info, w_sel, mig, w_info = pl.pallas_call(
             functools.partial(_head_kernel, dims),
-            in_specs=[vmem] * 6,
+            in_specs=[vmem] * 5,
             out_specs=[vmem] * 9,
             out_shape=[
                 pages_all_shape,
@@ -660,7 +671,7 @@
             compiler_params=pltpu.CompilerParams(collective_id=0, has_side_effects=True, vmem_limit_bytes=24 * MIB),
             cost_estimate=_cost(10, 4),
             name='head_gather',
-        )(meta, *packed[:2], q, src_slot.reshape(1, -1), src_slot.reshape(-1, 1))
+        )(meta, packed[0], q, src_slot.reshape(1, -1), src_slot.reshape(-1, 1))
 
         def attend(layer, q_all, pages):
             blk = pool_blk(layer)
@@ -701,10 +712,10 @@
             has = pages is not None
             half = (seq_dev, heads * dim)
             stat = (seq_dev, ml.shape[-1])
-            out_shape = [jax.ShapeDtypeStruct((rows, heads * dim), BF16)] + ([pages_all_shape] if has else [])
+            out_shape = [jax.ShapeDtypeStruct((rows, heads * dim), BF16), done_shape] + ([pages_all_shape] if has else [])
             return pl.pallas_call(
                 functools.partial(_exchange_kernel, n_cols, n_rows, heads, dim, has),
-                in_specs=[vmem] * (6 if has else 4),
+                in_specs=[vmem] * (5 if has else 4),
                 out_specs=[vmem] * len(out_shape),
                 out_shape=out_shape,
                 scratch_shapes=[
@@ -718,9 +729,9 @@
                 compiler_params=pltpu.CompilerParams(collective_id=1 + layer, has_side_effects=True, vmem_limit_bytes=32 * MIB),
                 cost_estimate=_cost(10, 4),
                 name='exchange_partials',
-            )(o, ml, q, kv, *(pages if has else []))
-
-        kv_all, moved = [], []
+            )(o, ml, q, kv, *([pages] if has else []))
+
+        kv_all, moved, done = [], [], None
         for layer in range(layers):
             if layer:
                 q, kv = project(hidden, layer)
@@ -739,11 +750,10 @@
                 kv_rows = lax.all_gather(jnp.stack(kv_all), 'kv')
                 kv_rows = kv_rows.reshape(n_cols, layers, steps, seq_dev, -1)
             o, ml = attend(layer, q_all, pages_y)
-            nxt = packed[2 * (layer + 1):2 * (layer + 2)] if layer + 1 < layers else None
-            moved.append(whole(2 * layer, q_all))
-            attn, *more = exchange(layer, o, ml, q, kv, nxt)
+            nxt = packed[layer + 1] if layer + 1 < layers else None
+            moved.append(whole(layer, done))
+            attn, done, *more = exchange(layer, o, ml, q, kv, nxt)
             pages_y = more[0] if more else None
-            moved.append(whole(2 * layer + 1, attn))
             hidden = (hidden.astype(F32) + jnp.dot(attn, w_out[layer], preferred_element_type=F32)).astype(BF16)
             up_act = jax.nn.gelu(jnp.dot(hidden, w_up[layer], preferred_element_type=F32)).astype(BF16)
             hidden = (hidden.astype(F32) + jnp.dot(up_act, w_down[layer], preferred_element_type=F32)).astype(BF16)
@@ -751,23 +761,24 @@
         outs = []
         for layer in range(layers):
             blk = pool_blk(layer)
+            pages, token = moved[layer]
             specs = [
                 pl.BlockSpec((n_cols, 1, steps, seq_dev, kv_w), lambda i, layer=layer: (0, layer, 0, 0, i)),
                 pl.BlockSpec((n_cols, 1, steps, seq_dev, kv_w), lambda i, layer=layer: (0, layer, 0, 0, v_at + i)),
                 blk, blk,
-            ] + [pl.BlockSpec((n_dev, n_move, m_w), lambda i: (0, 0, i))] * 2 + [fixed(a.shape) for a in (w_sel, mig, w_info)]
+            ] + [pl.BlockSpec((n_dev, 1, n_move, m_w), lambda i, which=which: (0, which, 0, i)) for which in range(2)] + [fixed(a.shape) for a in (w_sel, mig, w_info)]
             outs = pl.pallas_call(
                 functools.partial(_place_kernel, steps, pair, len(outs)),
                 grid=(n_grid,),
-                in_specs=specs + [pl.BlockSpec(memory_space=pl.ANY)] * len(outs),
+                in_specs=specs + [pl.BlockSpec(memory_space=pl.ANY)] * (1 + len(outs)),
                 out_specs=[blk, blk],
                 out_shape=[jax.ShapeDtypeStruct(a.shape, BF16) for a in (k_t, v_t)],
                 scratch_shapes=[pltpu.VMEM((2, steps, kv_w, n_slots), BF16), pltpu.VMEM((page, dim, n_slots), BF16)],
-                input_output_aliases={len(specs) + i: i for i in range(len(outs))},
-                compiler_params=pltpu.CompilerParams(vmem_limit_bytes=32 * MIB),
+                input_output_aliases={len(specs) + 1 + i: i for i in range(len(outs))},
+                compiler_params=pltpu.CompilerParams(vmem_limit_bytes=60 * MIB),
                 cost_estimate=_cost(20, 32),
                 name='place_pages',
-            )(kv_rows, kv_rows, k_t, v_t, moved[2 * layer], moved[2 * layer + 1], w_sel, mig, w_info, *outs)
+            )(kv_rows, kv_rows, k_t, v_t, pages, pages, w_sel, mig, w_info, token, *outs)
         k_out, v_out = outs
         y_out = hidden.reshape(steps, seq_dev, width)
         back = (4, 0, 1, 2, 3)

time: 437 us -> 379 us (0.87); the launches traced: 429 us -> 378 us
  waiting for transfers between devices: 78.4 us -> 28.6 us
  Pallas kernels: 229 us -> 249 us
  local copies, waits for them, and re-layouts: 27.2 us -> 12.7 us
  matrix products: 77.8 us -> 70.7 us
    all_gather x4 -> x2, waiting for transfers between devices: 76.7 us -> 27.1 us  [whole(): return (lax.all_gather(page, group_axes), token)]
    pallas_call x2, Pallas kernels: 58.8 us -> 74.1 us  [exchange(): pl.pallas_call(functools.partial(_exchange_kernel, n_cols, n_rows, heads,...]
    unnamed x38 -> x46, local copies, waits for them, and re-layouts: 24.2 us -> 9.77 us
    pallas_call x2, Pallas kernels: 40.4 us -> 45.3 us  [per_device(): pl.pallas_call(functools.partial(_place_kernel, steps, pair, len(outs)),...]
  transfers between devices with their start and end apart: 5 -> 3, of which waited for: 3 -> 1; matrix products, arithmetic and copies ran while one was open for 8% -> 8% of each run, Pallas kernels for 25% -> 33%
where the time goes in v6:
time: 379 us; the launch traced here: 378 us
  Pallas kernels  249 us (66%)
  matrix products  70.7 us (19%)
  waiting for transfers between devices  28.6 us (8%)
  between operations  14.1 us (4%)
  local copies, waits for them, and re-layouts  12.7 us (3%)
    pallas_call x2, Pallas kernels, exchange(): pl.pallas_call(functools.partial(_exchange_kernel, n_cols, n_rows, heads,...  74.1 us
    pallas_call x2, Pallas kernels, attend(): pl.pallas_call(functools.partial(_attn_kernel, steps, group, pair), grid=...  66.8 us
    dot_general x2, matrix products, per_device(): jnp.dot(up_act, w_down[layer], preferred_element_type=F32)  48.9 us
    pallas_call x2, Pallas kernels, per_device(): pl.pallas_call(functools.partial(_place_kernel, steps, pair, len(outs)),...  45.3 us
    pallas_call x1, Pallas kernels, per_device(): pl.pallas_call(functools.partial(_head_kernel, dims), in_specs=[vmem] * 5...  31.8 us
    all_gather x2, waiting for transfers between devices, whole(): return (lax.all_gather(page, group_axes), token)  27.1 us
    pallas_call x1, Pallas kernels, per_device(): pl.pallas_call(functools.partial(_query_kernel, n_cols), in_specs=[vmem],...  21.7 us
    dot_general x2, matrix products, project(): q = jnp.dot(hidden, w_query[layer], preferred_element_type=F32).astype(BF16)  10.1 us
  transfers between devices with their start and end apart: 3, of which 1 were waited for; matrix products, arithmetic and copies ran while one was open for 8% of the time, Pallas kernels for 33%

profile of v6, /device:TPU:97, one launch (start us, length us, event | category | flops | bytes accessed | tf_op | source)
XLA Modules:
  0.0 378.3 jit_solution(957342916540881203)
XLA Ops:
  7.2 0.1 all-gather.7.cloned.1.call-start
  7.3 0.7 tile.6
  7.9 0.1 broadcast_in_dim.51
  8.0 0.7 tile.7
  8.7 0.1 broadcast_in_dim.53
  8.8 0.8 reshape.84
  9.5 0.7 broadcast_subtract_fusion
  10.2 0.7 fusion.112.onehot_ref.refs_9_
  10.9 0.7 copy.19.mysrcc_ref
  11.6 5.2 %fusion.48.q_ref.refs_2_ = bf16[64,2048]{1,0:T(8,128)(2,1)S(1)} fusion(bf16[64,2048]{1,0:T(8,128)(2,1)} %bitcast.131, bf16[2,2048,2048]{2,1,0:T(8,128)(2,1)} %param.14), kind=kOutput, calls=%fused_computation.34 | convolution fusion | flops 537001984 | bytes 8912896 | tf_op jit(solution)/shard_map/dot_general | solution.py:634
  16.8 0.0 copy-done.14
  16.8 0.0 copy-done.16
  16.8 0.0 copy-start.18
  16.8 0.5 fusion.93
  17.3 0.3 copy-done.15
  17.6 0.5 fusion.90
  18.1 0.0 copy-done.18
  18.1 0.1 pad_add_fusion.1
  18.2 0.7 fusion.123
  18.8 0.1 and_select_fusion.1
  18.9 9.2 %pack_pages.1 = (bf16[2,16,8192]{2,1,0:T(8,128)(2,1)}, bf16[2,16,8192]{2,1,0:T(8,128)(2,1)}) custom-call(bf16[16,208]{1,0:T(8,128)(2,1)} %fusion.112.onehot_ref.refs_9_, bf16[2,16,8,64,208]{4,3,2,1,0:T(8,128)(2,1)} %bitcast.108, bf16[2,16,8,64,208]{4,3,2,1,0:T(8,128)(2,1)} %bitcast.114, bf16[2,16,8,64,208]{4,3,2,1,0:T(8,128)(2,1)} %bitcast.109, ...), custom_call_target="tpu_custom_call" | custom-call | flops 8000000000 | bytes 16777216 | tf_op jit(solution)/shard_map/pack_pages/pallas_call | solution.py:619
  28.1 0.0 copy-done.2
  28.1 1.0 copy-done.1
  29.2 31.8 %head_gather.1 = (bf16[4,2,16,8192]{3,2,1,0:T(8,128)(2,1)S(1)}, bf16[8,64,2048]{2,1,0:T(8,128)(2,1)S(1)}, bf16[256,256]{1,0:T(8,128)(2,1)S(1)}, bf16[768,256]{1,...) custom-call(s32[24,128]{1,0:T(8,128)S(1)} %pad_add_fusion.meta_ref, ...), custom_call_target="tpu_custom_call" | custom-call | flops 10000000000 | bytes 4194304 | tf_op jit(solution)/shard_map/head_gather/pallas_call | solution.py:655
  61.0 0.0 copy-start.3
  61.0 0.7 copy-done.3
  61.7 0.6 copy-done.4
  62.4 0.6 copy-done.7
  63.0 33.3 %slot_attention.2 = (f32[2,4,2,32,2048]{4,3,2,1,0:T(8,128)S(1)}, f32[2,4,2,32,128]{4,3,2,1,0:T(8,128)S(1)}) custom-call(bf16[8,2,32,2048]{3,2,1,0:T(8,128)(2,1)S(1)} %bitcast.106, bf16[2,16,8,64,208]{4,3,2,1,0:T(8,128)(2,1)} %bitcast.110, bf16[2,16,8,64,208]{4,3,2,1,0:T(8,128)(2,1)} %bitcast.116, ...), custom_call_target="tpu_custom_call" | custom-call | flops 20000000000 | bytes 16777216 | tf_op jit(solution)/shard_map/slot_attention/pallas_call | solution.py:679
  96.3 0.0 copy-done.11
  96.3 0.0 copy-start.5
  96.3 2.0 copy-done.5
  98.3 0.7 copy-done.9
  99.0 0.0 copy-done
  99.1 2.2 copy-done.6
  101.2 0.9 copy-done.10
  102.2 28.1 %exchange_partials.2 = (bf16[64,2048]{1,0:T(8,128)(2,1)S(1)}, f32[8,128]{1,0:T(8,128)S(1)}, bf16[4,2,16,8192]{3,2,1,0:T(8,128)(2,1)S(1)}) custom-call(f32[2,4,2,32,2048]{4,3,2,1,0:T(8,128)S(1)} %copy-done.6, f32[2,4,2,32,128]{4,3,2,1,0:T(8,128)S(1)} %copy-done.10, bf16[64,2048]{1,0:T(8,128)(2,1)S(1)} %fusion.48.q_ref.refs_2_, ...), custom_call_target="tpu_custom_call" | custom-call | flops 10000000000 | bytes 4194304 | tf_op jit(solution)/shard_map/exchange_partials/pallas_call | solution.py:716
  130.3 0.0 copy-start.8
  130.3 0.6 copy-done.8
  130.9 0.0 copy-done.17
  130.9 5.0 %fusion.45 = bf16[64,2048]{1,0:T(8,128)(2,1)S(1)} fusion(bf16[64,2048]{1,0:T(8,128)(2,1)S(1)} %get-tuple-element.38, bf16[2,2048,2048]{2,1,0:T(8,128)(2,1)} %param.17, bf16[64,2048]{1,0:T(8,128)(2,1)S(1)} %bitcast.134), kind=kOutput, calls=%fused_computation.33 | convolution fusion | flops 537264128 | bytes 9175040 | tf_op jit(solution)/shard_map/dot_general | solution.py:757
  135.9 23.8 %fusion.39 = bf16[64,2048]{1,0:T(8,128)(2,1)S(1)} fusion(bf16[2,8192,2048]{2,1,0:T(8,128)(2,1)} %param.19, bf16[64,2048]{1,0:T(8,128)(2,1)S(1)} %fusion.45, bf16[2,2048,8192]{2,1,0:T(8,128)(2,1)} %param.18), kind=kOutput, calls=%fused_computation.31 | convolution fusion | flops 4300079104 | bytes 67895296 | tf_op jit(solution)/shard_map/dot_general | solution.py:759
  159.7 0.0 copy-start.13
  159.7 2.1 fusion.99
  161.8 2.1 fusion.96
  163.9 0.7 pad_maximum_fusion
  164.7 0.1 all-gather.7.cloned.1.call-update
  164.7 0.1 all-gather.11.cloned.1.call-start
  164.8 0.7 all-gather.11.cloned.1.call-update
  165.5 0.1 all-gather.9.cloned.1.call-start
  165.6 0.7 all-gather.9.cloned.1.call-update
  166.3 5.0 %fusion.51.q_ref.refs_2_ = bf16[64,2048]{1,0:T(8,128)(2,1)S(1)} fusion(bf16[64,2048]{1,0:T(8,128)(2,1)S(1)} %fusion.39, bf16[2,2048,2048]{2,1,0:T(8,128)(2,1)} %param.14), kind=kOutput, calls=%fused_computation.35 | convolution fusion | flops 537001984 | bytes 8912896 | tf_op jit(solution)/shard_map/dot_general | solution.py:634
  171.3 21.7 %query_gather.1 = bf16[8,64,2048]{2,1,0:T(8,128)(2,1)S(1)} custom-call(bf16[64,2048]{1,0:T(8,128)(2,1)S(1)} %fusion.51.q_ref.refs_2_), custom_call_target="tpu_custom_call" | custom-call | flops 5000000000 | bytes 4194304 | tf_op jit(solution)/shard_map/query_gather/pallas_call | solution.py:738
  193.1 0.0 slice-start
  193.1 0.0 slice-start.1
  193.1 0.0 slice-start.2
  193.1 33.5 %slot_attention.3 = (f32[2,4,2,32,2048]{4,3,2,1,0:T(8,128)S(1)}, f32[2,4,2,32,128]{4,3,2,1,0:T(8,128)S(1)}) custom-call(bf16[8,2,32,2048]{3,2,1,0:T(8,128)(2,1)S(1)} %bitcast.107, bf16[2,16,8,64,208]{4,3,2,1,0:T(8,128)(2,1)} %bitcast.111, bf16[2,16,8,64,208]{4,3,2,1,0:T(8,128)(2,1)} %bitcast.117, ...), custom_call_target="tpu_custom_call" | custom-call | flops 20000000000 | bytes 16777216 | tf_op jit(solution)/shard_map/slot_attention/pallas_call | solution.py:679
  226.6 0.0 slice-start.3
  226.6 46.0 %exchange_partials.3 = (bf16[64,2048]{1,0:T(8,128)(2,1)S(1)}, f32[8,128]{1,0:T(8,128)}) custom-call(f32[2,4,2,32,2048]{4,3,2,1,0:T(8,128)S(1)} %get-tuple-element.40.refs_0_, f32[2,4,2,32,128]{4,3,2,1,0:T(8,128)S(1)} %get-tuple-element.41.refs_1_, bf16[64,2048]{1,0:T(8,128)(2,1)S(1)} %fusion.51.q_ref.refs_2_, bf16[64,1024]{1,0:T(8,128)(2,1)S(1)} %get-tuple-element.56.refs_3_), custom_call_target="tpu_custom_call" | custom-call | flops 10000000000 | bytes 4194304 | tf_op jit(solution)/shard_map/exchange_partials/pallas_call | solution.py:716
  272.6 1.6 fusion.42
  274.2 25.1 %fusion.36 = bf16[64,2048]{1,0:T(8,128)(2,1)} fusion(bf16[2,8192,2048]{2,1,0:T(8,128)(2,1)} %param.19, bf16[64,2048]{1,0:T(8,128)(2,1)S(1)} %fusion.42, bf16[2,2048,8192]{2,1,0:T(8,128)(2,1)} %param.18), kind=kOutput, calls=%fused_computation.30 | convolution fusion | flops 4300079104 | bytes 67895296 | tf_op jit(solution)/shard_map/dot_general | solution.py:759
  299.3 22.7 %place_pages.2 = (bf16[2,16,8,64,208]{4,3,2,1,0:T(8,128)(2,1)}, bf16[2,16,8,64,208]{4,3,2,1,0:T(8,128)(2,1)}) custom-call(bf16[8,2,2,32,1024]{4,3,2,1,0:T(8,128)(2,1)} %bitcast.127, bf16[8,2,2,32,1024]{4,3,2,1,0:T(8,128)(2,1)} %bitcast.128, bf16[2,16,8,64,208]{4,3,2,1,0:T(8,128)(2,1)} %bitcast.112, bf16[2,16,8,64,208]{4,3,2,1,0:T(8,128)(2,1)} %bitcast.118, ...), custom_call_target="tpu_custom_call" | custom-call | flops 20000000000 | bytes 33554432 | tf_op jit(solution)/shard_map/place_pages/pallas_call | solution.py:770
  322.0 27.1 %all-gather.9.cloned.1.call-done = bf16[64,16,8192]{2,1,0:T(8,128)(2,1)} async-done(((bf16[2,16,8192]{2,1,0:T(8,128)(2,1)}), bf16[64,16,8192]{2,1,0:T(8,128)(2,1)}) %all-gather.9.cloned.1.call-update) | async-done | bytes 16777232 | tf_op jit(solution)/shard_map/all_gather | solution.py:631
  349.1 22.6 %place_pages.3 = (bf16[2,16,8,64,208]{4,3,2,1,0:T(8,128)(2,1)}, bf16[2,16,8,64,208]{4,3,2,1,0:T(8,128)(2,1)}) custom-call(bf16[8,2,2,32,1024]{4,3,2,1,0:T(8,128)(2,1)} %bitcast.129, bf16[8,2,2,32,1024]{4,3,2,1,0:T(8,128)(2,1)} %bitcast.130, bf16[2,16,8,64,208]{4,3,2,1,0:T(8,128)(2,1)} %bitcast.113, ...), custom_call_target="tpu_custom_call", output_to_operand_aliasing={{0}: (10, {}), {1}: (11, {})} | custom-call | flops 20000000000 | bytes 33554432 | tf_op jit(solution)/shard_map/place_pages/pallas_call | solution.py:770
  (28 shorter events, 0.1 us)
Async XLA Ops:
  7.2 292.1 %all-gather.7.cloned.1.call-start = ((), (), s32[]{:S(2)}) async-start(), calls=%async_computation | async-start | bytes 2359296 | tf_op jit(solution)/shard_map/all_gather | solution.py:750
  11.6 5.2 %copy-start.14 = (bf16[2,2048,512]{2,1,0:T(8,128)(2,1)S(1)}, bf16[2,2048,512]{2,1,0:T(8,128)(2,1)}, u32[]{:S(2)}) copy-start(bf16[2,2048,512]{2,1,0:T(8,128)(2,1)} %param.16) | copy-start | bytes 12582916
  11.6 5.2 %copy-start.16 = (bf16[2,32,2048]{2,1,0:T(8,128)(2,1)S(1)}, bf16[2,32,2048]{2,1,0:T(8,128)(2,1)}, u32[]{:S(2)}) copy-start(bf16[2,32,2048]{2,1,0:T(8,128)(2,1)} %param.13) | copy-start | bytes 786436
  11.6 6.0 %copy-start.15 = (bf16[2,2048,512]{2,1,0:T(8,128)(2,1)S(1)}, bf16[2,2048,512]{2,1,0:T(8,128)(2,1)}, u32[]{:S(2)}) copy-start(bf16[2,2048,512]{2,1,0:T(8,128)(2,1)} %param.15) | copy-start | bytes 12582916
  16.8 1.3 copy-start.18
  18.9 9.2 %copy-start.2 = (s32[16]{0:T(128)S(1)}, s32[16]{0:T(128)}, u32[]{:S(2)}) copy-start(s32[16]{0:T(128)} %param.24) | copy-start | bytes 196
  28.1 1.0 copy-start.1
  61.0 0.7 copy-start.3
  61.7 0.6 copy-start.4
  62.4 0.6 copy-start.7
  62.4 33.9 %copy-start.11 = (bf16[64,256]{1,0:T(8,128)(2,1)}, bf16[64,256]{1,0:T(8,128)(2,1)S(1)}, u32[]{:S(2)}) copy-start(bf16[64,256]{1,0:T(8,128)(2,1)S(1)} %get-tuple-element.33.arr_ref) | copy-start | bytes 98308
  63.0 36.1 %copy-start = (bf16[2,16,8192]{2,1,0:T(8,128)(2,1)S(1)}, bf16[2,16,8192]{2,1,0:T(8,128)(2,1)}, u32[]{:S(2)}) copy-start(bf16[2,16,8192]{2,1,0:T(8,128)(2,1)} %get-tuple-element.44.refs_4_) | copy-start | bytes 1572868
  96.3 2.0 copy-start.5
  98.3 0.7 copy-start.9
  99.1 2.2 copy-start.6
  101.2 0.9 copy-start.10
  102.2 28.7 %copy-start.17 = (bf16[2,32,2048]{2,1,0:T(8,128)(2,1)S(1)}, bf16[2,32,2048]{2,1,0:T(8,128)(2,1)}, u32[]{:S(2)}) copy-start(bf16[2,32,2048]{2,1,0:T(8,128)(2,1)} %param.13) | copy-start | bytes 786436
  130.3 0.6 copy-start.8
  159.7 4.2 %copy-start.13 = (bf16[1,64,1024]{2,1,0:T(8,128)(2,1)S(1)}, bf16[1,64,1024]{2,1,0:T(8,128)(2,1)}, u32[]{:S(2)}) copy-start(bf16[1,64,1024]{2,1,0:T(8,128)(2,1)} %get-tuple-element.53) | copy-start | bytes 393220
  164.7 134.6 %all-gather.11.cloned.1.call-start = ((), (), s32[]{:S(2)}) async-start(), calls=%async_computation.2 | async-start | bytes 17301504 | tf_op jit(solution)/shard_map/all_gather | solution.py:631
  165.5 183.6 %all-gather.9.cloned.1.call-start = ((), (), s32[]{:S(2)}) async-start(), calls=%async_computation.1 | async-start | bytes 17301504 | tf_op jit(solution)/shard_map/all_gather | solution.py:631
  171.3 21.7 %copy-start.12 = (bf16[64,256]{1,0:T(8,128)(2,1)S(1)}, bf16[64,256]{1,0:T(8,128)(2,1)}, u32[]{:S(2)}) copy-start(bf16[64,256]{1,0:T(8,128)(2,1)} %copy-done.11) | copy-start | bytes 98308
  193.1 79.5 %slice-start = ((s8[16777216]{0:T(1024)(128)(4,1)}), s8[4194304]{0:T(1024)(128)(4,1)S(1)}, s32[]{:S(2)}) async-start(s8[16777216]{0:T(1024)(128)(4,1)} %bitcast.121), calls=%async_computation.3 | async-start | bytes 8388608
  193.1 79.5 %slice-start.1 = ((s8[16777216]{0:T(1024)(128)(4,1)}), s8[4194304]{0:T(1024)(128)(4,1)S(1)}, s32[]{:S(2)}) async-start(s8[16777216]{0:T(1024)(128)(4,1)} %bitcast.121), calls=%async_computation.4 | async-start | bytes 8388608
  193.1 79.5 %slice-start.2 = ((s8[16777216]{0:T(1024)(128)(4,1)}), s8[4194304]{0:T(1024)(128)(4,1)S(1)}, s32[]{:S(2)}) async-start(s8[16777216]{0:T(1024)(128)(4,1)} %bitcast.121), calls=%async_computation.5 | async-start | bytes 8388608
  226.6 46.0 %slice-start.3 = ((s8[16777216]{0:T(1024)(128)(4,1)}), s8[4194304]{0:T(1024)(128)(4,1)S(1)}, s32[]{:S(2)}) async-start(s8[16777216]{0:T(1024)(128)(4,1)} %bitcast.121), calls=%async_computation.6 | async-start | bytes 8388608
Sparse Core Ops, SparseCore 0:
  164.8 27.5 all-gather.6
  195.1 84.8 all-gather.10
  282.2 66.9 all-gather.8

commit v7 on v6

--- a/solution.py
+++ b/solution.py
@@ -330,7 +330,7 @@
                 full[tok, :, 0:n_slots] = jnp.where(freed, full[tok, :, 0:n_slots], pool[0, tok, h].astype(F32))
             return 0
 
-        lax.fori_loop(0, page, join, 0)
+        lax.fori_loop(0, page, join, 0, unroll=4)
 
         def score(pair, _, h=h):
             toks = [pair * 2, pair * 2 + 1]
@@ -434,9 +434,6 @@
     row = lax.broadcasted_iota(I32, expand.shape, I0)
     group = cw // kw
     expand[...] = ((lane // (dim * group) == row // dim) & (lane % dim == row % dim)).astype(F32).astype(BF16)
-
-    def widen(w, c):
-        return _pick_lhs(w, spread[:, c * cw:(c + I1) * cw], NN)
 
     s = jnp.zeros((I3 * home, heads), F32)
     for c in range(n_chunk):
@@ -522,16 +519,20 @@
         own = ws.pop()
         ws += [own if e is None else own * e for _, e in self_w[t]]
         w = jnp.concatenate(ws, axis=I0)
-        for c in range(n_chunk):
-            wx = widen(w, c)
-            sl = slice(c * cw, (c + I1) * cw)
-            v_c = _dot(kv_ref[:, kv_w + c * kw:kv_w + (c + I1) * kw], expand[...], NN)
+
+        def close(c, _, t=t, parts=parts, w=w):
+            sl = pl.ds(pl.multiple_of(c * cw, cw), cw)
+            wx = _pick_lhs(w, spread[:, sl], NN)
+            v_c = _dot(kv_ref[:, pl.ds(pl.multiple_of(kv_w + c * kw, kw), kw)], expand[...], NN)
             acc = jnp.zeros((home, cw), F32)
             for i, (o, _) in enumerate(parts):
                 acc = acc + o[:, sl] * wx[i * home:(i + I1) * home]
             for i, (step, _) in enumerate(self_w[t]):
                 acc = acc + v_c[step * home:(step + I1) * home] * wx[(I3 + i) * home:(I4 + i) * home]
             out_ref[t * home:(t + I1) * home, sl] = acc.astype(BF16)
+            return c
+
+        lax.fori_loop(I0, n_chunk, close, I0)
     if has_pages:
         y_finish()
     for c in pals + sends:
@@ -567,7 +568,7 @@
                 out[0, tok, h] = val
                 return 0
 
-            lax.fori_loop(0, page, fill, 0)
+            lax.fori_loop(0, page, fill, 0, unroll=4)
         return 0
 
     lax.fori_loop(0, heads, head, 0)

time: 379 us -> 378 us (level)
  no operation moved by 1% of the time
where the time goes in v7:
time: 378 us; the launch traced here: 377 us
  Pallas kernels  248 us (66%)
  matrix products  70.8 us (19%)
  waiting for transfers between devices  29.2 us (8%)
  between operations  14.1 us (4%)
  local copies, waits for them, and re-layouts  12.7 us (3%)
    pallas_call x2, Pallas kernels, exchange(): pl.pallas_call(functools.partial(_exchange_kernel, n_cols, n_rows, heads,...  76.2 us
    pallas_call x2, Pallas kernels, attend(): pl.pallas_call(functools.partial(_attn_kernel, steps, group, pair), grid=...  66 us
    dot_general x2, matrix products, per_device(): jnp.dot(up_act, w_down[layer], preferred_element_type=F32)  49 us
    pallas_call x2, Pallas kernels, per_device(): pl.pallas_call(functools.partial(_place_kernel, steps, pair, len(outs)),...  42.6 us
    pallas_call x1, Pallas kernels, per_device(): pl.pallas_call(functools.partial(_head_kernel, dims), in_specs=[vmem] * 5...  31.8 us
    all_gather x2, waiting for transfers between devices, whole(): return (lax.all_gather(page, group_axes), token)  27.7 us
    pallas_call x1, Pallas kernels, per_device(): pl.pallas_call(functools.partial(_query_kernel, n_cols), in_specs=[vmem],...  21.7 us
    dot_general x2, matrix products, project(): q = jnp.dot(hidden, w_query[layer], preferred_element_type=F32).astype(BF16)  10.1 us
  transfers between devices with their start and end apart: 3, of which 1 were waited for; matrix products, arithmetic and copies ran while one was open for 8% of the time, Pallas kernels for 33%

profile of v7, /device:TPU:97, one launch (start us, length us, event | category | flops | bytes accessed | tf_op | source)
XLA Modules:
  0.0 377.5 jit_solution(508984762811702658)
XLA Ops:
  7.2 0.1 all-gather.7.cloned.1.call-start
  7.3 0.7 tile.6
  7.9 0.1 broadcast_in_dim.51
  8.0 0.7 tile.7
  8.7 0.1 broadcast_in_dim.53
  8.8 0.8 reshape.84
  9.5 0.7 broadcast_subtract_fusion
  10.2 0.7 fusion.112.onehot_ref.refs_9_
  10.9 0.7 copy.19.mysrcc_ref
  11.6 5.2 %fusion.48.q_ref.refs_2_ = bf16[64,2048]{1,0:T(8,128)(2,1)S(1)} fusion(bf16[64,2048]{1,0:T(8,128)(2,1)} %bitcast.131, bf16[2,2048,2048]{2,1,0:T(8,128)(2,1)} %param.14), kind=kOutput, calls=%fused_computation.34 | convolution fusion | flops 537001984 | bytes 8912896 | tf_op jit(solution)/shard_map/dot_general | solution.py:635
  16.8 0.0 copy-done.14
  16.8 0.0 copy-done.16
  16.8 0.0 copy-start.18
  16.8 0.5 fusion.93
  17.3 0.3 copy-done.15
  17.6 0.5 fusion.90
  18.1 0.0 copy-done.18
  18.1 0.1 pad_add_fusion.1
  18.2 0.7 fusion.123
  18.8 0.1 and_select_fusion.1
  18.9 9.2 %pack_pages.1 = (bf16[2,16,8192]{2,1,0:T(8,128)(2,1)}, bf16[2,16,8192]{2,1,0:T(8,128)(2,1)}) custom-call(bf16[16,208]{1,0:T(8,128)(2,1)} %fusion.112.onehot_ref.refs_9_, bf16[2,16,8,64,208]{4,3,2,1,0:T(8,128)(2,1)} %bitcast.108, bf16[2,16,8,64,208]{4,3,2,1,0:T(8,128)(2,1)} %bitcast.114, bf16[2,16,8,64,208]{4,3,2,1,0:T(8,128)(2,1)} %bitcast.109, ...), custom_call_target="tpu_custom_call" | custom-call | flops 8000000000 | bytes 16777216 | tf_op jit(solution)/shard_map/pack_pages/pallas_call | solution.py:620
  28.1 0.0 copy-done.2
  28.1 1.0 copy-done.1
  29.2 31.8 %head_gather.1 = (bf16[4,2,16,8192]{3,2,1,0:T(8,128)(2,1)S(1)}, bf16[8,64,2048]{2,1,0:T(8,128)(2,1)S(1)}, bf16[256,256]{1,0:T(8,128)(2,1)S(1)}, bf16[768,256]{1,...) custom-call(s32[24,128]{1,0:T(8,128)S(1)} %pad_add_fusion.meta_ref, ...), custom_call_target="tpu_custom_call" | custom-call | flops 10000000000 | bytes 4194304 | tf_op jit(solution)/shard_map/head_gather/pallas_call | solution.py:656
  61.0 0.0 copy-start.3
  61.0 0.7 copy-done.3
  61.7 0.6 copy-done.4
  62.4 0.6 copy-done.7
  63.0 32.9 %slot_attention.2 = (f32[2,4,2,32,2048]{4,3,2,1,0:T(8,128)S(1)}, f32[2,4,2,32,128]{4,3,2,1,0:T(8,128)S(1)}) custom-call(bf16[8,2,32,2048]{3,2,1,0:T(8,128)(2,1)S(1)} %bitcast.106, bf16[2,16,8,64,208]{4,3,2,1,0:T(8,128)(2,1)} %bitcast.110, bf16[2,16,8,64,208]{4,3,2,1,0:T(8,128)(2,1)} %bitcast.116, ...), custom_call_target="tpu_custom_call" | custom-call | flops 20000000000 | bytes 16777216 | tf_op jit(solution)/shard_map/slot_attention/pallas_call | solution.py:680
  95.9 0.0 copy-done.11
  95.9 0.0 copy-start.5
  95.9 2.0 copy-done.5
  98.0 0.7 copy-done.9
  98.7 0.0 copy-done
  98.7 2.2 copy-done.6
  100.8 0.9 copy-done.10
  101.8 29.2 %exchange_partials.2 = (bf16[64,2048]{1,0:T(8,128)(2,1)S(1)}, f32[8,128]{1,0:T(8,128)S(1)}, bf16[4,2,16,8192]{3,2,1,0:T(8,128)(2,1)S(1)}) custom-call(f32[2,4,2,32,2048]{4,3,2,1,0:T(8,128)S(1)} %copy-done.6, f32[2,4,2,32,128]{4,3,2,1,0:T(8,128)S(1)} %copy-done.10, bf16[64,2048]{1,0:T(8,128)(2,1)S(1)} %fusion.48.q_ref.refs_2_, ...), custom_call_target="tpu_custom_call" | custom-call | flops 10000000000 | bytes 4194304 | tf_op jit(solution)/shard_map/exchange_partials/pallas_call | solution.py:717
  131.0 0.0 copy-start.8
  131.0 0.6 copy-done.8
  131.6 0.0 copy-done.17
  131.6 5.0 %fusion.45 = bf16[64,2048]{1,0:T(8,128)(2,1)S(1)} fusion(bf16[64,2048]{1,0:T(8,128)(2,1)S(1)} %get-tuple-element.38, bf16[2,2048,2048]{2,1,0:T(8,128)(2,1)} %param.17, bf16[64,2048]{1,0:T(8,128)(2,1)S(1)} %bitcast.134), kind=kOutput, calls=%fused_computation.33 | convolution fusion | flops 537264128 | bytes 9175040 | tf_op jit(solution)/shard_map/dot_general | solution.py:758
  136.6 23.8 %fusion.39 = bf16[64,2048]{1,0:T(8,128)(2,1)S(1)} fusion(bf16[2,8192,2048]{2,1,0:T(8,128)(2,1)} %param.19, bf16[64,2048]{1,0:T(8,128)(2,1)S(1)} %fusion.45, bf16[2,2048,8192]{2,1,0:T(8,128)(2,1)} %param.18), kind=kOutput, calls=%fused_computation.31 | convolution fusion | flops 4300079104 | bytes 67895296 | tf_op jit(solution)/shard_map/dot_general | solution.py:760
  160.4 2.1 fusion.99
  162.5 2.1 fusion.96
  164.6 0.0 copy-done.13
  164.6 0.7 pad_maximum_fusion
  165.3 0.1 all-gather.7.cloned.1.call-update
  165.4 0.1 all-gather.11.cloned.1.call-start
  165.5 0.7 all-gather.11.cloned.1.call-update
  166.2 0.1 all-gather.9.cloned.1.call-start
  166.3 0.7 all-gather.9.cloned.1.call-update
  167.0 5.0 %fusion.51.q_ref.refs_2_ = bf16[64,2048]{1,0:T(8,128)(2,1)S(1)} fusion(bf16[64,2048]{1,0:T(8,128)(2,1)S(1)} %fusion.39, bf16[2,2048,2048]{2,1,0:T(8,128)(2,1)} %param.14), kind=kOutput, calls=%fused_computation.35 | convolution fusion | flops 537001984 | bytes 8912896 | tf_op jit(solution)/shard_map/dot_general | solution.py:635
  172.0 21.7 %query_gather.1 = bf16[8,64,2048]{2,1,0:T(8,128)(2,1)S(1)} custom-call(bf16[64,2048]{1,0:T(8,128)(2,1)S(1)} %fusion.51.q_ref.refs_2_), custom_call_target="tpu_custom_call" | custom-call | flops 5000000000 | bytes 4194304 | tf_op jit(solution)/shard_map/query_gather/pallas_call | solution.py:739
  193.7 0.0 slice-start
  193.7 0.0 slice-start.1
  193.7 0.0 slice-start.2
  193.7 33.1 %slot_attention.3 = (f32[2,4,2,32,2048]{4,3,2,1,0:T(8,128)S(1)}, f32[2,4,2,32,128]{4,3,2,1,0:T(8,128)S(1)}) custom-call(bf16[8,2,32,2048]{3,2,1,0:T(8,128)(2,1)S(1)} %bitcast.107, bf16[2,16,8,64,208]{4,3,2,1,0:T(8,128)(2,1)} %bitcast.111, bf16[2,16,8,64,208]{4,3,2,1,0:T(8,128)(2,1)} %bitcast.117, ...), custom_call_target="tpu_custom_call" | custom-call | flops 20000000000 | bytes 16777216 | tf_op jit(solution)/shard_map/slot_attention/pallas_call | solution.py:680
  226.8 0.0 slice-start.3
  226.8 47.0 %exchange_partials.3 = (bf16[64,2048]{1,0:T(8,128)(2,1)S(1)}, f32[8,128]{1,0:T(8,128)}) custom-call(f32[2,4,2,32,2048]{4,3,2,1,0:T(8,128)S(1)} %get-tuple-element.40.refs_0_, f32[2,4,2,32,128]{4,3,2,1,0:T(8,128)S(1)} %get-tuple-element.41.refs_1_, bf16[64,2048]{1,0:T(8,128)(2,1)S(1)} %fusion.51.q_ref.refs_2_, bf16[64,1024]{1,0:T(8,128)(2,1)S(1)} %get-tuple-element.56.refs_3_), custom_call_target="tpu_custom_call" | custom-call | flops 10000000000 | bytes 4194304 | tf_op jit(solution)/shard_map/exchange_partials/pallas_call | solution.py:717
  273.9 1.6 fusion.42
  275.5 25.1 %fusion.36 = bf16[64,2048]{1,0:T(8,128)(2,1)} fusion(bf16[2,8192,2048]{2,1,0:T(8,128)(2,1)} %param.19, bf16[64,2048]{1,0:T(8,128)(2,1)S(1)} %fusion.42, bf16[2,2048,8192]{2,1,0:T(8,128)(2,1)} %param.18), kind=kOutput, calls=%fused_computation.30 | convolution fusion | flops 4300079104 | bytes 67895296 | tf_op jit(solution)/shard_map/dot_general | solution.py:760
  300.7 21.5 %place_pages.2 = (bf16[2,16,8,64,208]{4,3,2,1,0:T(8,128)(2,1)}, bf16[2,16,8,64,208]{4,3,2,1,0:T(8,128)(2,1)}) custom-call(bf16[8,2,2,32,1024]{4,3,2,1,0:T(8,128)(2,1)} %bitcast.127, bf16[8,2,2,32,1024]{4,3,2,1,0:T(8,128)(2,1)} %bitcast.128, bf16[2,16,8,64,208]{4,3,2,1,0:T(8,128)(2,1)} %bitcast.112, bf16[2,16,8,64,208]{4,3,2,1,0:T(8,128)(2,1)} %bitcast.118, ...), custom_call_target="tpu_custom_call" | custom-call | flops 20000000000 | bytes 33554432 | tf_op jit(solution)/shard_map/place_pages/pallas_call | solution.py:771
  322.2 27.7 %all-gather.9.cloned.1.call-done = bf16[64,16,8192]{2,1,0:T(8,128)(2,1)} async-done(((bf16[2,16,8192]{2,1,0:T(8,128)(2,1)}), bf16[64,16,8192]{2,1,0:T(8,128)(2,1)}) %all-gather.9.cloned.1.call-update) | async-done | bytes 16777232 | tf_op jit(solution)/shard_map/all_gather | solution.py:632
  349.8 21.1 %place_pages.3 = (bf16[2,16,8,64,208]{4,3,2,1,0:T(8,128)(2,1)}, bf16[2,16,8,64,208]{4,3,2,1,0:T(8,128)(2,1)}) custom-call(bf16[8,2,2,32,1024]{4,3,2,1,0:T(8,128)(2,1)} %bitcast.129, bf16[8,2,2,32,1024]{4,3,2,1,0:T(8,128)(2,1)} %bitcast.130, bf16[2,16,8,64,208]{4,3,2,1,0:T(8,128)(2,1)} %bitcast.113, ...), custom_call_target="tpu_custom_call", output_to_operand_aliasing={{0}: (10, {}), {1}: (11, {})} | custom-call | flops 20000000000 | bytes 33554432 | tf_op jit(solution)/shard_map/place_pages/pallas_call | solution.py:771
  (28 shorter events, 0.1 us)
Async XLA Ops:
  7.2 293.5 %all-gather.7.cloned.1.call-start = ((), (), s32[]{:S(2)}) async-start(), calls=%async_computation | async-start | bytes 2359296 | tf_op jit(solution)/shard_map/all_gather | solution.py:751
  11.6 5.2 %copy-start.14 = (bf16[2,2048,512]{2,1,0:T(8,128)(2,1)S(1)}, bf16[2,2048,512]{2,1,0:T(8,128)(2,1)}, u32[]{:S(2)}) copy-start(bf16[2,2048,512]{2,1,0:T(8,128)(2,1)} %param.16) | copy-start | bytes 12582916
  11.6 5.2 %copy-start.16 = (bf16[2,32,2048]{2,1,0:T(8,128)(2,1)S(1)}, bf16[2,32,2048]{2,1,0:T(8,128)(2,1)}, u32[]{:S(2)}) copy-start(bf16[2,32,2048]{2,1,0:T(8,128)(2,1)} %param.13) | copy-start | bytes 786436
  11.6 6.0 %copy-start.15 = (bf16[2,2048,512]{2,1,0:T(8,128)(2,1)S(1)}, bf16[2,2048,512]{2,1,0:T(8,128)(2,1)}, u32[]{:S(2)}) copy-start(bf16[2,2048,512]{2,1,0:T(8,128)(2,1)} %param.15) | copy-start | bytes 12582916
  16.8 1.3 copy-start.18
  18.9 9.2 %copy-start.2 = (s32[16]{0:T(128)S(1)}, s32[16]{0:T(128)}, u32[]{:S(2)}) copy-start(s32[16]{0:T(128)} %param.24) | copy-start | bytes 196
  28.1 1.0 copy-start.1
  61.0 0.7 copy-start.3
  61.7 0.6 copy-start.4
  62.4 0.6 copy-start.7
  62.4 33.5 %copy-start.11 = (bf16[64,256]{1,0:T(8,128)(2,1)}, bf16[64,256]{1,0:T(8,128)(2,1)S(1)}, u32[]{:S(2)}) copy-start(bf16[64,256]{1,0:T(8,128)(2,1)S(1)} %get-tuple-element.33.arr_ref) | copy-start | bytes 98308
  63.0 35.7 %copy-start = (bf16[2,16,8192]{2,1,0:T(8,128)(2,1)S(1)}, bf16[2,16,8192]{2,1,0:T(8,128)(2,1)}, u32[]{:S(2)}) copy-start(bf16[2,16,8192]{2,1,0:T(8,128)(2,1)} %get-tuple-element.44.refs_4_) | copy-start | bytes 1572868
  95.9 2.0 copy-start.5
  98.0 0.7 copy-start.9
  98.7 2.2 copy-start.6
  100.8 0.9 copy-start.10
  101.8 29.8 %copy-start.17 = (bf16[2,32,2048]{2,1,0:T(8,128)(2,1)S(1)}, bf16[2,32,2048]{2,1,0:T(8,128)(2,1)}, u32[]{:S(2)}) copy-start(bf16[2,32,2048]{2,1,0:T(8,128)(2,1)} %param.13) | copy-start | bytes 786436
  131.0 0.6 copy-start.8
  160.4 4.2 %copy-start.13 = (bf16[1,64,1024]{2,1,0:T(8,128)(2,1)S(1)}, bf16[1,64,1024]{2,1,0:T(8,128)(2,1)}, u32[]{:S(2)}) copy-start(bf16[1,64,1024]{2,1,0:T(8,128)(2,1)} %get-tuple-element.53) | copy-start | bytes 393220
  165.4 135.3 %all-gather.11.cloned.1.call-start = ((), (), s32[]{:S(2)}) async-start(), calls=%async_computation.2 | async-start | bytes 17301504 | tf_op jit(solution)/shard_map/all_gather | solution.py:632
  166.2 183.6 %all-gather.9.cloned.1.call-start = ((), (), s32[]{:S(2)}) async-start(), calls=%async_computation.1 | async-start | bytes 17301504 | tf_op jit(solution)/shard_map/all_gather | solution.py:632
  172.0 21.7 %copy-start.12 = (bf16[64,256]{1,0:T(8,128)(2,1)S(1)}, bf16[64,256]{1,0:T(8,128)(2,1)}, u32[]{:S(2)}) copy-start(bf16[64,256]{1,0:T(8,128)(2,1)} %copy-done.11) | copy-start | bytes 98308
  193.7 80.2 %slice-start = ((s8[16777216]{0:T(1024)(128)(4,1)}), s8[4194304]{0:T(1024)(128)(4,1)S(1)}, s32[]{:S(2)}) async-start(s8[16777216]{0:T(1024)(128)(4,1)} %bitcast.121), calls=%async_computation.3 | async-start | bytes 8388608
  193.7 80.2 %slice-start.1 = ((s8[16777216]{0:T(1024)(128)(4,1)}), s8[4194304]{0:T(1024)(128)(4,1)S(1)}, s32[]{:S(2)}) async-start(s8[16777216]{0:T(1024)(128)(4,1)} %bitcast.121), calls=%async_computation.4 | async-start | bytes 8388608
  193.7 80.2 %slice-start.2 = ((s8[16777216]{0:T(1024)(128)(4,1)}), s8[4194304]{0:T(1024)(128)(4,1)S(1)}, s32[]{:S(2)}) async-start(s8[16777216]{0:T(1024)(128)(4,1)} %bitcast.121), calls=%async_computation.5 | async-start | bytes 8388608
  226.8 47.1 %slice-start.3 = ((s8[16777216]{0:T(1024)(128)(4,1)}), s8[4194304]{0:T(1024)(128)(4,1)S(1)}, s32[]{:S(2)}) async-start(s8[16777216]{0:T(1024)(128)(4,1)} %bitcast.121), calls=%async_computation.6 | async-start | bytes 8388608
Sparse Core Ops, SparseCore 0:
  165.5 27.5 all-gather.6
  195.8 85.0 all-gather.10
  282.9 66.8 all-gather.8
